TPU v7x, 128 devices: a whole 4x4x4 slice. The times are simulated.
128 devices in a mesh: gx: 2 (over core), gy: 4 (over x), gz: 16 (over z, y).
Axes of the slice: x: 4, y: 4, z: 4, core: 2. Of those that a mesh axis runs over, the one named last changes fastest.
Arguments:
- permanent_field: float32 [12, 24, 96, 3], P('gx', 'gy', 'gz'), may hold values from -6 to 6
- polar: float32 [12, 24, 96], P('gx', 'gy', 'gz'), may hold values from 0.4 to 1.4
- jitter: float32 [12, 24, 96, 3], P('gx', 'gy', 'gz'), may hold values from -0.2 to 0.2
- neighbors: int32 [12, 24, 96, 56], P('gx', 'gy', 'gz'), may hold values from -1 to 987, as said below
Outputs:
- dipoles: float32 [12, 24, 96, 3], P('gx', 'gy', 'gz')
- residual: float32 [12, 24, 96, 3], P('gx', 'gy', 'gz')
- step_lengths: float32 [8], replicated
Inputs may be any that keep to these rules, and one draw needn't show every extreme that they name: `neighbors`: each entry is -1 or the flat index of a neighbour in the device's block extended by two sites on every side, with an offset d of squared length 1 to 5 (each component -2 to 2), each offset at most once in a row; the -1 entries come after all others; if site j stands in site i's row with offset d then i stands in j's row with offset -d, the box being periodic.
All inputs are finite; a program needn't handle non-finite values.
Results may differ from a plain program's by a relative error of at most 0.0003.
Values sent between devices are 32-bit elements.
No kernel may reach another device: no remote copies, remote signals or barrier semaphores. Data moves between devices by JAX's collectives and lax.ppermute only.
A program may use at most 64 MiB of HBM per device.

v0:
```python
import jax
import jax.numpy as jnp
from jax import lax
from jax.sharding import Mesh
from jax.sharding import PartitionSpec as P

ITERS = 8
GX_GY_GZ = ("gx", "gy", "gz_0", "gz_1")
GZ = ("gz_0", "gz_1")


thole_damping = 0.39
site_spacing = 3.5


def padded_2(cells, sides, width, closed):
    for axis, dim in sides:
        count = lax.axis_size(axis)
        ends = count if closed else count - 1
        head = lax.slice_in_dim(cells, 0, width, axis=dim)
        tail = lax.slice_in_dim(cells, cells.shape[dim] - width, cells.shape[dim], axis=dim)
        cells = jnp.concatenate(
            [
                lax.ppermute(tail, axis, [(i, (i + 1) % count) for i in range(ends)]),
                cells,
                lax.ppermute(head, axis, [((i + 1) % count, i) for i in range(ends)]),
            ],
            axis=dim,
        )
    return cells


def by_axis(shard, axes):
    for axis in axes:
        shard = lax.psum(shard, axis)
    return shard


def geometry(offsets, jit_self, jit_other, pol_self, pol_other, present):
    separation = (offsets + jit_other - jit_self) * site_spacing
    separation = jnp.where(present[..., None], separation, site_spacing)
    dist_sq = jnp.sum(separation * separation, axis=-1)
    distance = jnp.sqrt(dist_sq)
    dist_cube = dist_sq * distance
    damping = thole_damping * dist_cube / jnp.sqrt(pol_self * pol_other)
    falloff = jnp.exp(-damping)
    lam_three = 1.0 - falloff
    lam_five = 1.0 - (1.0 + damping) * falloff
    isotropic = jnp.where(present, lam_three / dist_cube, 0.0)
    radial = jnp.where(present, 3.0 * lam_five / (dist_cube * dist_sq), 0.0)
    return (separation, isotropic, radial)


def couple(separation, isotropic, radial, values):
    projection = jnp.sum(separation * values, axis=-1, keepdims=True)
    return jnp.sum(
        radial[..., None] * projection * separation - isotropic[..., None] * values, axis=-2
    )


def per_device(permanent_field, polar, jitter, neighbors):
    cell_edge = polar.shape[0]
    padded_edge = cell_edge + 4
    padded_count = padded_edge * padded_edge * padded_edge
    site_count = cell_edge * cell_edge * cell_edge
    slots = neighbors.shape[-1]
    bundle = jnp.concatenate([jitter, polar[..., None]], axis=-1)
    padded = padded_2(bundle, (("gx", 0), ("gy", 1), (GZ, 2)), 2, True)
    flattened = padded.reshape(padded_count, 4)
    neighbor_rows = neighbors.reshape(site_count, slots)
    present = neighbor_rows >= 0
    clipped = jnp.where(present, neighbor_rows, 0)
    plane_a = clipped // (padded_edge * padded_edge)
    plane_b = clipped // padded_edge % padded_edge
    plane_c = clipped % padded_edge
    site_index = lax.broadcasted_iota(jnp.int32, (site_count, 1), 0)
    home_x = site_index // (cell_edge * cell_edge)
    home_y = site_index // cell_edge % cell_edge
    home_z = site_index % cell_edge
    offsets = jnp.stack(
        [plane_a - 2 - home_x, plane_b - 2 - home_y, plane_c - 2 - home_z], axis=-1
    ).astype(jnp.float32)
    remote = flattened[clipped]
    weights = polar.reshape(site_count, 1)
    separation, isotropic, radial = geometry(
        offsets, jitter.reshape(site_count, 1, 3), remote[..., :3], weights, remote[..., 3], present
    )

    def operate(vector):
        ghosts = padded_2(
            vector.reshape(cell_edge, cell_edge, cell_edge, 3),
            (("gx", 0), ("gy", 1), (GZ, 2)),
            2,
            True,
        )
        values = ghosts.reshape(padded_count, 3)[clipped]
        return vector / weights - couple(separation, isotropic, radial, values)

    source = permanent_field.reshape(site_count, 3)
    dipoles = weights * source
    residual = source - operate(dipoles)
    lengths = []

    def joined(left_vec, right_vec, other_vec):
        return (
            by_axis(jnp.sum(left_vec * right_vec), GX_GY_GZ),
            by_axis(jnp.sum(right_vec * other_vec), GX_GY_GZ),
        )

    scaled = weights * residual
    image = operate(scaled)
    gamma_now, delta_now = joined(residual, scaled, image)
    step_len = gamma_now / delta_now
    direction = scaled
    image_dir = image
    for number in range(ITERS):
        lengths.append(step_len)
        dipoles = dipoles + step_len * direction
        residual = residual - step_len * image_dir
        if number + 1 < ITERS:
            scaled = weights * residual
            image = operate(scaled)
            gamma_next, delta_now = joined(residual, scaled, image)
            beta_now = gamma_next / gamma_now
            step_len = gamma_next / (delta_now - beta_now * gamma_next / step_len)
            direction = scaled + beta_now * direction
            image_dir = image + beta_now * image_dir
            gamma_now = gamma_next
    shape_out = (cell_edge, cell_edge, cell_edge, 3)
    return (
        dipoles.reshape(shape_out),
        residual.reshape(shape_out),
        jnp.stack(lengths).astype(jnp.float32),
    )


def solution(mesh):
    finer = Mesh(
        mesh.devices.reshape(mesh.shape["gx"], mesh.shape["gy"], 4, 4), ("gx", "gy", "gz_0", "gz_1")
    )
    return jax.shard_map(
        per_device,
        mesh=finer,
        in_specs=(
            P("gx", "gy", GZ, None),
            P("gx", "gy", GZ),
            P("gx", "gy", GZ, None),
            P("gx", "gy", GZ, None),
        ),
        out_specs=(P("gx", "gy", GZ, None), P("gx", "gy", GZ, None), P()),
        check_vma=False,
    )
```

profile of v0, /device:TPU:0, one launch (start us, length us, event | category | flops | bytes accessed | tf_op | source)
XLA Modules:
  0.0 807.1 jit_solution(16292884457432283287)
XLA Ops:
  24.8 5.3 collective-permute-start.5
  30.7 23.2 %gather_fusion.1 = f32[12096,3]{1,0:T(8,128)} fusion(f32[1000,3]{1,0:T(8,128)S(1)} %copy.226, s32[12288]{0:T(1024)S(1)} %pad_clamp_fusion), kind=kCustom, calls=%fused_computation.1 | custom fusion | bytes 338688 | tf_op jit(solution)/shard_map/gather | solution.py:96
  59.6 23.2 %gather_fusion = f32[12096,4]{1,0:T(8,128)} fusion(f32[1000,4]{1,0:T(8,128)S(1)} %copy.218, s32[12288]{0:T(1024)S(1)} %pad_clamp_fusion), kind=kCustom, calls=%fused_computation | custom fusion | bytes 435456 | tf_op jit(solution)/shard_map/gather | solution.py:83
  82.9 7.0 slice.343
  112.7 5.4 collective-permute-done.16
  118.7 23.2 %gather_fusion.2 = f32[12096,3]{1,0:T(8,128)} fusion(f32[1000,3]{1,0:T(8,128)S(1)} %copy.233, s32[12288]{0:T(1024)S(1)} %pad_clamp_fusion), kind=kCustom, calls=%fused_computation.2 | custom fusion | bytes 338688 | tf_op jit(solution)/shard_map/gather | solution.py:96
  150.7 11.3 %all-reduce.23 = (f32[]{:T(128)}, f32[]{:T(128)}) all-reduce(f32[]{:T(128)} %get-tuple-element.95, f32[]{:T(128)} %get-tuple-element.96), channel_id=1, replica_groups=mesh['gx'=2,'gy'=4,'gz_0'=4,'gz_1'=4] {'gy'}, use_global_device_ids=true, to_apply=%region_5.6 | all-reduce | flops 2 | bytes 16 | tf_op jit(solution)/shard_map/psum | solution.py:35
  162.0 8.3 %all-reduce.15 = (f32[]{:T(128)}, f32[]{:T(128)}) all-reduce(f32[]{:T(128)} %get-tuple-element.79, f32[]{:T(128)} %get-tuple-element.80), channel_id=1, replica_groups=mesh['gx'=2,'gy'=4,'gz_0'=4,'gz_1'=4] {'gz_0'}, use_global_device_ids=true, to_apply=%region_6.7 | all-reduce | flops 2 | bytes 16 | tf_op jit(solution)/shard_map/psum | solution.py:35
  170.4 14.0 %all-reduce.7 = (f32[]{:T(128)}, f32[]{:T(128)}) all-reduce(f32[]{:T(128)} %get-tuple-element.63, f32[]{:T(128)} %get-tuple-element.64), channel_id=1, replica_groups=mesh['gx'=2,'gy'=4,'gz_0'=4,'gz_1'=4] {'gz_1'}, use_global_device_ids=true, to_apply=%region_7.8 | all-reduce | flops 2 | bytes 16 | tf_op jit(solution)/shard_map/psum | solution.py:35
  192.9 5.3 collective-permute-start.23
  198.3 5.4 collective-permute-done.22
  204.3 23.2 %gather_fusion.3 = f32[12096,3]{1,0:T(8,128)} fusion(f32[1000,3]{1,0:T(8,128)S(1)} %copy.239, s32[12288]{0:T(1024)S(1)} %pad_clamp_fusion), kind=kCustom, calls=%fused_computation.3 | custom fusion | bytes 338688 | tf_op jit(solution)/shard_map/gather | solution.py:96
  236.4 11.3 %all-reduce.22 = (f32[]{:T(128)}, f32[]{:T(128)}) all-reduce(f32[]{:T(128)} %get-tuple-element.93, f32[]{:T(128)} %get-tuple-element.94), channel_id=1, replica_groups=mesh['gx'=2,'gy'=4,'gz_0'=4,'gz_1'=4] {'gy'}, use_global_device_ids=true, to_apply=%region_17.18 | all-reduce | flops 2 | bytes 16 | tf_op jit(solution)/shard_map/psum | solution.py:35
  247.7 8.4 %all-reduce.14 = (f32[]{:T(128)}, f32[]{:T(128)}) all-reduce(f32[]{:T(128)} %get-tuple-element.77, f32[]{:T(128)} %get-tuple-element.78), channel_id=1, replica_groups=mesh['gx'=2,'gy'=4,'gz_0'=4,'gz_1'=4] {'gz_0'}, use_global_device_ids=true, to_apply=%region_18.19 | all-reduce | flops 2 | bytes 16 | tf_op jit(solution)/shard_map/psum | solution.py:35
  256.1 14.0 %all-reduce.6 = (f32[]{:T(128)}, f32[]{:T(128)}) all-reduce(f32[]{:T(128)} %get-tuple-element.61, f32[]{:T(128)} %get-tuple-element.62), channel_id=1, replica_groups=mesh['gx'=2,'gy'=4,'gz_0'=4,'gz_1'=4] {'gz_1'}, use_global_device_ids=true, to_apply=%region_19.20 | all-reduce | flops 2 | bytes 16 | tf_op jit(solution)/shard_map/psum | solution.py:35
  287.3 5.4 collective-permute-done.28
  293.3 23.2 %gather_fusion.4 = f32[12096,3]{1,0:T(8,128)} fusion(f32[1000,3]{1,0:T(8,128)S(1)} %copy.245, s32[12288]{0:T(1024)S(1)} %pad_clamp_fusion), kind=kCustom, calls=%fused_computation.4 | custom fusion | bytes 338688 | tf_op jit(solution)/shard_map/gather | solution.py:96
  325.5 11.3 %all-reduce.21 = (f32[]{:T(128)}, f32[]{:T(128)}) all-reduce(f32[]{:T(128)} %get-tuple-element.91, f32[]{:T(128)} %get-tuple-element.92), channel_id=1, replica_groups=mesh['gx'=2,'gy'=4,'gz_0'=4,'gz_1'=4] {'gy'}, use_global_device_ids=true, to_apply=%region_29.30 | all-reduce | flops 2 | bytes 16 | tf_op jit(solution)/shard_map/psum | solution.py:35
  336.8 8.3 %all-reduce.13 = (f32[]{:T(128)}, f32[]{:T(128)}) all-reduce(f32[]{:T(128)} %get-tuple-element.75, f32[]{:T(128)} %get-tuple-element.76), channel_id=1, replica_groups=mesh['gx'=2,'gy'=4,'gz_0'=4,'gz_1'=4] {'gz_0'}, use_global_device_ids=true, to_apply=%region_30.31 | all-reduce | flops 2 | bytes 16 | tf_op jit(solution)/shard_map/psum | solution.py:35
  345.2 14.0 %all-reduce.5 = (f32[]{:T(128)}, f32[]{:T(128)}) all-reduce(f32[]{:T(128)} %get-tuple-element.59, f32[]{:T(128)} %get-tuple-element.60), channel_id=1, replica_groups=mesh['gx'=2,'gy'=4,'gz_0'=4,'gz_1'=4] {'gz_1'}, use_global_device_ids=true, to_apply=%region_31.32 | all-reduce | flops 2 | bytes 16 | tf_op jit(solution)/shard_map/psum | solution.py:35
  370.3 5.3 collective-permute-start.35
  375.7 5.4 collective-permute-done.34
  381.7 23.2 %gather_fusion.5 = f32[12096,3]{1,0:T(8,128)} fusion(f32[1000,3]{1,0:T(8,128)S(1)} %copy.251, s32[12288]{0:T(1024)S(1)} %pad_clamp_fusion), kind=kCustom, calls=%fused_computation.5 | custom fusion | bytes 338688 | tf_op jit(solution)/shard_map/gather | solution.py:96
  413.7 11.3 %all-reduce.20 = (f32[]{:T(128)}, f32[]{:T(128)}) all-reduce(f32[]{:T(128)} %get-tuple-element.89, f32[]{:T(128)} %get-tuple-element.90), channel_id=1, replica_groups=mesh['gx'=2,'gy'=4,'gz_0'=4,'gz_1'=4] {'gy'}, use_global_device_ids=true, to_apply=%region_41.42 | all-reduce | flops 2 | bytes 16 | tf_op jit(solution)/shard_map/psum | solution.py:35
  425.0 8.3 %all-reduce.12 = (f32[]{:T(128)}, f32[]{:T(128)}) all-reduce(f32[]{:T(128)} %get-tuple-element.73, f32[]{:T(128)} %get-tuple-element.74), channel_id=1, replica_groups=mesh['gx'=2,'gy'=4,'gz_0'=4,'gz_1'=4] {'gz_0'}, use_global_device_ids=true, to_apply=%region_42.43 | all-reduce | flops 2 | bytes 16 | tf_op jit(solution)/shard_map/psum | solution.py:35
  433.4 14.0 %all-reduce.4 = (f32[]{:T(128)}, f32[]{:T(128)}) all-reduce(f32[]{:T(128)} %get-tuple-element.57, f32[]{:T(128)} %get-tuple-element.58), channel_id=1, replica_groups=mesh['gx'=2,'gy'=4,'gz_0'=4,'gz_1'=4] {'gz_1'}, use_global_device_ids=true, to_apply=%region_43.44 | all-reduce | flops 2 | bytes 16 | tf_op jit(solution)/shard_map/psum | solution.py:35
  458.6 5.3 collective-permute-start.41
  463.9 5.4 collective-permute-done.40
  469.9 23.2 %gather_fusion.6 = f32[12096,3]{1,0:T(8,128)} fusion(f32[1000,3]{1,0:T(8,128)S(1)} %copy.257, s32[12288]{0:T(1024)S(1)} %pad_clamp_fusion), kind=kCustom, calls=%fused_computation.6 | custom fusion | bytes 338688 | tf_op jit(solution)/shard_map/gather | solution.py:96
  502.0 11.3 %all-reduce.19 = (f32[]{:T(128)}, f32[]{:T(128)}) all-reduce(f32[]{:T(128)} %get-tuple-element.87, f32[]{:T(128)} %get-tuple-element.88), channel_id=1, replica_groups=mesh['gx'=2,'gy'=4,'gz_0'=4,'gz_1'=4] {'gy'}, use_global_device_ids=true, to_apply=%region_53.54 | all-reduce | flops 2 | bytes 16 | tf_op jit(solution)/shard_map/psum | solution.py:35
  513.3 8.3 %all-reduce.11 = (f32[]{:T(128)}, f32[]{:T(128)}) all-reduce(f32[]{:T(128)} %get-tuple-element.71, f32[]{:T(128)} %get-tuple-element.72), channel_id=1, replica_groups=mesh['gx'=2,'gy'=4,'gz_0'=4,'gz_1'=4] {'gz_0'}, use_global_device_ids=true, to_apply=%region_54.55 | all-reduce | flops 2 | bytes 16 | tf_op jit(solution)/shard_map/psum | solution.py:35
  521.6 14.0 %all-reduce.3 = (f32[]{:T(128)}, f32[]{:T(128)}) all-reduce(f32[]{:T(128)} %get-tuple-element.55, f32[]{:T(128)} %get-tuple-element.56), channel_id=1, replica_groups=mesh['gx'=2,'gy'=4,'gz_0'=4,'gz_1'=4] {'gz_1'}, use_global_device_ids=true, to_apply=%region_55.56 | all-reduce | flops 2 | bytes 16 | tf_op jit(solution)/shard_map/psum | solution.py:35
  546.8 5.6 collective-permute-start.47
  558.2 23.2 %gather_fusion.7 = f32[12096,3]{1,0:T(8,128)} fusion(f32[1000,3]{1,0:T(8,128)S(1)} %copy.263, s32[12288]{0:T(1024)S(1)} %pad_clamp_fusion), kind=kCustom, calls=%fused_computation.7 | custom fusion | bytes 338688 | tf_op jit(solution)/shard_map/gather | solution.py:96
  590.2 11.3 %all-reduce.18 = (f32[]{:T(128)}, f32[]{:T(128)}) all-reduce(f32[]{:T(128)} %get-tuple-element.85, f32[]{:T(128)} %get-tuple-element.86), channel_id=1, replica_groups=mesh['gx'=2,'gy'=4,'gz_0'=4,'gz_1'=4] {'gy'}, use_global_device_ids=true, to_apply=%region_65.66 | all-reduce | flops 2 | bytes 16 | tf_op jit(solution)/shard_map/psum | solution.py:35
  601.5 8.3 %all-reduce.10 = (f32[]{:T(128)}, f32[]{:T(128)}) all-reduce(f32[]{:T(128)} %get-tuple-element.69, f32[]{:T(128)} %get-tuple-element.70), channel_id=1, replica_groups=mesh['gx'=2,'gy'=4,'gz_0'=4,'gz_1'=4] {'gz_0'}, use_global_device_ids=true, to_apply=%region_66.67 | all-reduce | flops 2 | bytes 16 | tf_op jit(solution)/shard_map/psum | solution.py:35
  609.8 14.2 %all-reduce.2 = (f32[]{:T(128)}, f32[]{:T(128)}) all-reduce(f32[]{:T(128)} %get-tuple-element.53, f32[]{:T(128)} %get-tuple-element.54), channel_id=1, replica_groups=mesh['gx'=2,'gy'=4,'gz_0'=4,'gz_1'=4] {'gz_1'}, use_global_device_ids=true, to_apply=%region_67.68 | all-reduce | flops 2 | bytes 16 | tf_op jit(solution)/shard_map/psum | solution.py:35
  635.3 5.3 collective-permute-start.53
  640.6 5.4 collective-permute-done.52
  646.6 23.2 %gather_fusion.8 = f32[12096,3]{1,0:T(8,128)} fusion(f32[1000,3]{1,0:T(8,128)S(1)} %copy.269, s32[12288]{0:T(1024)S(1)} %pad_clamp_fusion), kind=kCustom, calls=%fused_computation.8 | custom fusion | bytes 338688 | tf_op jit(solution)/shard_map/gather | solution.py:96
  678.6 11.3 %all-reduce.17 = (f32[]{:T(128)}, f32[]{:T(128)}) all-reduce(f32[]{:T(128)} %get-tuple-element.83, f32[]{:T(128)} %get-tuple-element.84), channel_id=1, replica_groups=mesh['gx'=2,'gy'=4,'gz_0'=4,'gz_1'=4] {'gy'}, use_global_device_ids=true, to_apply=%region_77.78 | all-reduce | flops 2 | bytes 16 | tf_op jit(solution)/shard_map/psum | solution.py:35
  690.0 8.3 %all-reduce.9 = (f32[]{:T(128)}, f32[]{:T(128)}) all-reduce(f32[]{:T(128)} %get-tuple-element.67, f32[]{:T(128)} %get-tuple-element.68), channel_id=1, replica_groups=mesh['gx'=2,'gy'=4,'gz_0'=4,'gz_1'=4] {'gz_0'}, use_global_device_ids=true, to_apply=%region_78.79 | all-reduce | flops 2 | bytes 16 | tf_op jit(solution)/shard_map/psum | solution.py:35
  698.3 14.0 %all-reduce.1 = (f32[]{:T(128)}, f32[]{:T(128)}) all-reduce(f32[]{:T(128)} %get-tuple-element.51, f32[]{:T(128)} %get-tuple-element.52), channel_id=1, replica_groups=mesh['gx'=2,'gy'=4,'gz_0'=4,'gz_1'=4] {'gz_1'}, use_global_device_ids=true, to_apply=%region_79.80 | all-reduce | flops 2 | bytes 16 | tf_op jit(solution)/shard_map/psum | solution.py:35
  728.8 5.4 collective-permute-done.58
  734.8 23.2 %gather_fusion.9 = f32[12096,3]{1,0:T(8,128)} fusion(f32[1000,3]{1,0:T(8,128)S(1)} %copy.275, s32[12288]{0:T(1024)S(1)} %pad_clamp_fusion), kind=kCustom, calls=%fused_computation.9 | custom fusion | bytes 338688 | tf_op jit(solution)/shard_map/gather | solution.py:96
  766.9 11.3 %all-reduce.16 = (f32[]{:T(128)}, f32[]{:T(128)}) all-reduce(f32[]{:T(128)} %get-tuple-element.81, f32[]{:T(128)} %get-tuple-element.82), channel_id=1, replica_groups=mesh['gx'=2,'gy'=4,'gz_0'=4,'gz_1'=4] {'gy'}, use_global_device_ids=true, to_apply=%region_89.90 | all-reduce | flops 2 | bytes 16 | tf_op jit(solution)/shard_map/psum | solution.py:35
  778.2 8.3 %all-reduce.8 = (f32[]{:T(128)}, f32[]{:T(128)}) all-reduce(f32[]{:T(128)} %get-tuple-element.65, f32[]{:T(128)} %get-tuple-element.66), channel_id=1, replica_groups=mesh['gx'=2,'gy'=4,'gz_0'=4,'gz_1'=4] {'gz_0'}, use_global_device_ids=true, to_apply=%region_90.91 | all-reduce | flops 2 | bytes 16 | tf_op jit(solution)/shard_map/psum | solution.py:35
  786.6 14.0 %all-reduce = (f32[]{:T(128)}, f32[]{:T(128)}) all-reduce(f32[]{:T(128)} %get-tuple-element.49, f32[]{:T(128)} %get-tuple-element.50), channel_id=1, replica_groups=mesh['gx'=2,'gy'=4,'gz_0'=4,'gz_1'=4] {'gz_1'}, use_global_device_ids=true, to_apply=%region_91.92 | all-reduce | flops 2 | bytes 16 | tf_op jit(solution)/shard_map/psum | solution.py:35
  (306 shorter events, 196.3 us)
Async XLA Ops:
  2.7 6.4 collective-permute-start.6
  2.8 6.2 collective-permute-start.7
  4.9 7.5 collective-permute-start
  5.0 7.4 collective-permute-start.1
  9.1 7.4 collective-permute-start.8
  10.8 5.7 collective-permute-start.9
  13.2 10.3 %collective-permute-start.2 = (f32[10,2,6,4]{2,3,1,0:T(4,128)S(1)}, f32[10,2,6,4]{2,3,1,0:T(4,128)S(1)}, u32[]{:S(2)}, u32[]{:S(2)}) collective-permute-start(f32[10,2,6,4]{2,3,1,0:T(4,128)S(1)} %get-tuple-element.149), channel_id=1, source_target_pairs={{0,16},{16,32},{32,48},{48,0},{1,17},{17,33},{33,49},{49,1},{2,18}... | collective-permute-start | bytes 5768 | tf_op jit(solution)/shard_map/ppermute | solution.py:24
  13.7 9.8 %collective-permute-start.3 = (f32[10,2,6,4]{2,3,1,0:T(4,128)S(1)}, f32[10,2,6,4]{2,3,1,0:T(4,128)S(1)}, u32[]{:S(2)}, u32[]{:S(2)}) collective-permute-start(f32[10,2,6,4]{2,3,1,0:T(4,128)S(1)} %get-tuple-element.150), channel_id=1, source_target_pairs={{16,0},{32,16},{48,32},{0,48},{17,1},{33,17},{49,33},{1,49},{18,2}... | collective-permute-start | bytes 5768 | tf_op jit(solution)/shard_map/ppermute | solution.py:26
  16.7 13.4 %collective-permute-start.10 = (f32[10,10,2,3]{2,1,0,3:T(8,128)S(1)}, f32[10,10,2,3]{2,1,0,3:T(8,128)S(1)}, u32[]{:S(2)}, u32[]{:S(2)}) collective-permute-start(f32[10,10,2,3]{2,1,0,3:T(8,128)S(1)} %get-tuple-element.144), channel_id=1, source_target_pairs={{0,1},{1,2},{2,3},{3,4},{4,5},{5,6},{6,7},{7,8},{8,9},{9,10},{10,1... | collective-permute-start | bytes 7208 | tf_op jit(solution)/shard_map/ppermute | solution.py:24
  18.5 11.6 %collective-permute-start.11 = (f32[10,10,2,3]{2,1,0,3:T(8,128)S(1)}, f32[10,10,2,3]{2,1,0,3:T(8,128)S(1)}, u32[]{:S(2)}, u32[]{:S(2)}) collective-permute-start(f32[10,10,2,3]{2,1,0,3:T(8,128)S(1)} %get-tuple-element.145), channel_id=1, source_target_pairs={{1,0},{2,1},{3,2},{4,3},{5,4},{6,5},{7,6},{8,7},{9,8},{10,9},{11,1... | collective-permute-start | bytes 7208 | tf_op jit(solution)/shard_map/ppermute | solution.py:26
  24.7 34.2 %collective-permute-start.4 = (f32[10,10,2,4]{2,3,1,0:T(4,128)S(1)}, f32[10,10,2,4]{2,3,1,0:T(4,128)S(1)}, u32[]{:S(2)}, u32[]{:S(2)}) collective-permute-start(f32[10,10,2,4]{2,3,1,0:T(4,128)S(1)} %get-tuple-element.146), channel_id=1, source_target_pairs={{0,1},{1,2},{2,3},{3,4},{4,5},{5,6},{6,7},{7,8},{8,9},{9,10},{10,1... | collective-permute-start | bytes 9608 | tf_op jit(solution)/shard_map/ppermute | solution.py:24
  24.8 34.1 %collective-permute-start.5 = (f32[10,10,2,4]{2,3,1,0:T(4,128)S(1)}, f32[10,10,2,4]{2,3,1,0:T(4,128)S(1)}, u32[]{:S(2)}, u32[]{:S(2)}) collective-permute-start(f32[10,10,2,4]{2,3,1,0:T(4,128)S(1)} %get-tuple-element.147), channel_id=1, source_target_pairs={{1,0},{2,1},{3,2},{4,3},{5,4},{6,5},{7,6},{8,7},{9,8},{10,9},{11,1... | collective-permute-start | bytes 9608 | tf_op jit(solution)/shard_map/ppermute | solution.py:26
  100.3 1.4 collective-permute-start.13
  101.7 5.3 collective-permute-start.14
  102.0 5.1 collective-permute-start.15
  107.3 10.8 %collective-permute-start.16 = (f32[10,10,2,3]{2,1,0,3:T(8,128)S(1)}, f32[10,10,2,3]{2,1,0,3:T(8,128)S(1)}, u32[]{:S(2)}, u32[]{:S(2)}) collective-permute-start(f32[10,10,2,3]{2,1,0,3:T(8,128)S(1)} %get-tuple-element.142), channel_id=1, source_target_pairs={{0,1},{1,2},{2,3},{3,4},{4,5},{5,6},{6,7},{7,8},{8,9},{9,10},{10,1... | collective-permute-start | bytes 7208 | tf_op jit(solution)/shard_map/ppermute | solution.py:24
  107.3 10.7 %collective-permute-start.17 = (f32[10,10,2,3]{2,1,0,3:T(8,128)S(1)}, f32[10,10,2,3]{2,1,0,3:T(8,128)S(1)}, u32[]{:S(2)}, u32[]{:S(2)}) collective-permute-start(f32[10,10,2,3]{2,1,0,3:T(8,128)S(1)} %get-tuple-element.143), channel_id=1, source_target_pairs={{1,0},{2,1},{3,2},{4,3},{5,4},{6,5},{7,6},{8,7},{9,8},{10,9},{11,1... | collective-permute-start | bytes 7208 | tf_op jit(solution)/shard_map/ppermute | solution.py:26
  186.0 1.4 collective-permute-start.19
  187.5 5.2 collective-permute-start.20
  187.6 5.1 collective-permute-start.21
  192.8 10.8 %collective-permute-start.22 = (f32[10,10,2,3]{2,1,0,3:T(8,128)S(1)}, f32[10,10,2,3]{2,1,0,3:T(8,128)S(1)}, u32[]{:S(2)}, u32[]{:S(2)}) collective-permute-start(f32[10,10,2,3]{2,1,0,3:T(8,128)S(1)} %get-tuple-element.140), channel_id=1, source_target_pairs={{0,1},{1,2},{2,3},{3,4},{4,5},{5,6},{6,7},{7,8},{8,9},{9,10},{10,1... | collective-permute-start | bytes 7208 | tf_op jit(solution)/shard_map/ppermute | solution.py:24
  192.9 10.7 %collective-permute-start.23 = (f32[10,10,2,3]{2,1,0,3:T(8,128)S(1)}, f32[10,10,2,3]{2,1,0,3:T(8,128)S(1)}, u32[]{:S(2)}, u32[]{:S(2)}) collective-permute-start(f32[10,10,2,3]{2,1,0,3:T(8,128)S(1)} %get-tuple-element.141), channel_id=1, source_target_pairs={{1,0},{2,1},{3,2},{4,3},{5,4},{6,5},{7,6},{8,7},{9,8},{10,9},{11,1... | collective-permute-start | bytes 7208 | tf_op jit(solution)/shard_map/ppermute | solution.py:26
  275.0 1.4 collective-permute-start.25
  276.5 5.2 collective-permute-start.26
  276.6 5.1 collective-permute-start.27
  281.9 10.8 %collective-permute-start.28 = (f32[10,10,2,3]{2,1,0,3:T(8,128)S(1)}, f32[10,10,2,3]{2,1,0,3:T(8,128)S(1)}, u32[]{:S(2)}, u32[]{:S(2)}) collective-permute-start(f32[10,10,2,3]{2,1,0,3:T(8,128)S(1)} %get-tuple-element.138), channel_id=1, source_target_pairs={{0,1},{1,2},{2,3},{3,4},{4,5},{5,6},{6,7},{7,8},{8,9},{9,10},{10,1... | collective-permute-start | bytes 7208 | tf_op jit(solution)/shard_map/ppermute | solution.py:24
  281.9 10.7 %collective-permute-start.29 = (f32[10,10,2,3]{2,1,0,3:T(8,128)S(1)}, f32[10,10,2,3]{2,1,0,3:T(8,128)S(1)}, u32[]{:S(2)}, u32[]{:S(2)}) collective-permute-start(f32[10,10,2,3]{2,1,0,3:T(8,128)S(1)} %get-tuple-element.139), channel_id=1, source_target_pairs={{1,0},{2,1},{3,2},{4,3},{5,4},{6,5},{7,6},{8,7},{9,8},{10,9},{11,1... | collective-permute-start | bytes 7208 | tf_op jit(solution)/shard_map/ppermute | solution.py:26
  364.9 5.2 collective-permute-start.32
  365.0 5.1 collective-permute-start.33
  370.3 10.8 %collective-permute-start.34 = (f32[10,10,2,3]{2,1,0,3:T(8,128)S(1)}, f32[10,10,2,3]{2,1,0,3:T(8,128)S(1)}, u32[]{:S(2)}, u32[]{:S(2)}) collective-permute-start(f32[10,10,2,3]{2,1,0,3:T(8,128)S(1)} %get-tuple-element.136), channel_id=1, source_target_pairs={{0,1},{1,2},{2,3},{3,4},{4,5},{5,6},{6,7},{7,8},{8,9},{9,10},{10,1... | collective-permute-start | bytes 7208 | tf_op jit(solution)/shard_map/ppermute | solution.py:24
  370.3 10.7 %collective-permute-start.35 = (f32[10,10,2,3]{2,1,0,3:T(8,128)S(1)}, f32[10,10,2,3]{2,1,0,3:T(8,128)S(1)}, u32[]{:S(2)}, u32[]{:S(2)}) collective-permute-start(f32[10,10,2,3]{2,1,0,3:T(8,128)S(1)} %get-tuple-element.137), channel_id=1, source_target_pairs={{1,0},{2,1},{3,2},{4,3},{5,4},{6,5},{7,6},{8,7},{9,8},{10,9},{11,1... | collective-permute-start | bytes 7208 | tf_op jit(solution)/shard_map/ppermute | solution.py:26
  451.7 1.4 collective-permute-start.37
  453.1 5.2 collective-permute-start.38
  453.2 5.1 collective-permute-start.39
  458.5 10.8 %collective-permute-start.40 = (f32[10,10,2,3]{2,1,0,3:T(8,128)S(1)}, f32[10,10,2,3]{2,1,0,3:T(8,128)S(1)}, u32[]{:S(2)}, u32[]{:S(2)}) collective-permute-start(f32[10,10,2,3]{2,1,0,3:T(8,128)S(1)} %get-tuple-element.134), channel_id=1, source_target_pairs={{0,1},{1,2},{2,3},{3,4},{4,5},{5,6},{6,7},{7,8},{8,9},{9,10},{10,1... | collective-permute-start | bytes 7208 | tf_op jit(solution)/shard_map/ppermute | solution.py:24
  458.6 10.7 %collective-permute-start.41 = (f32[10,10,2,3]{2,1,0,3:T(8,128)S(1)}, f32[10,10,2,3]{2,1,0,3:T(8,128)S(1)}, u32[]{:S(2)}, u32[]{:S(2)}) collective-permute-start(f32[10,10,2,3]{2,1,0,3:T(8,128)S(1)} %get-tuple-element.135), channel_id=1, source_target_pairs={{1,0},{2,1},{3,2},{4,3},{5,4},{6,5},{7,6},{8,7},{9,8},{10,9},{11,1... | collective-permute-start | bytes 7208 | tf_op jit(solution)/shard_map/ppermute | solution.py:26
  541.4 5.2 collective-permute-start.44
  541.4 5.1 collective-permute-start.45
  546.7 10.8 %collective-permute-start.46 = (f32[10,10,2,3]{2,1,0,3:T(8,128)S(1)}, f32[10,10,2,3]{2,1,0,3:T(8,128)S(1)}, u32[]{:S(2)}, u32[]{:S(2)}) collective-permute-start(f32[10,10,2,3]{2,1,0,3:T(8,128)S(1)} %get-tuple-element.132), channel_id=1, source_target_pairs={{0,1},{1,2},{2,3},{3,4},{4,5},{5,6},{6,7},{7,8},{8,9},{9,10},{10,1... | collective-permute-start | bytes 7208 | tf_op jit(solution)/shard_map/ppermute | solution.py:24
  546.8 10.7 %collective-permute-start.47 = (f32[10,10,2,3]{2,1,0,3:T(8,128)S(1)}, f32[10,10,2,3]{2,1,0,3:T(8,128)S(1)}, u32[]{:S(2)}, u32[]{:S(2)}) collective-permute-start(f32[10,10,2,3]{2,1,0,3:T(8,128)S(1)} %get-tuple-element.133), channel_id=1, source_target_pairs={{1,0},{2,1},{3,2},{4,3},{5,4},{6,5},{7,6},{8,7},{9,8},{10,9},{11,1... | collective-permute-start | bytes 7208 | tf_op jit(solution)/shard_map/ppermute | solution.py:26
  629.8 5.2 collective-permute-start.50
  629.9 5.1 collective-permute-start.51
  635.2 10.8 %collective-permute-start.52 = (f32[10,10,2,3]{2,1,0,3:T(8,128)S(1)}, f32[10,10,2,3]{2,1,0,3:T(8,128)S(1)}, u32[]{:S(2)}, u32[]{:S(2)}) collective-permute-start(f32[10,10,2,3]{2,1,0,3:T(8,128)S(1)} %get-tuple-element.130), channel_id=1, source_target_pairs={{0,1},{1,2},{2,3},{3,4},{4,5},{5,6},{6,7},{7,8},{8,9},{9,10},{10,1... | collective-permute-start | bytes 7208 | tf_op jit(solution)/shard_map/ppermute | solution.py:24
  635.3 10.7 %collective-permute-start.53 = (f32[10,10,2,3]{2,1,0,3:T(8,128)S(1)}, f32[10,10,2,3]{2,1,0,3:T(8,128)S(1)}, u32[]{:S(2)}, u32[]{:S(2)}) collective-permute-start(f32[10,10,2,3]{2,1,0,3:T(8,128)S(1)} %get-tuple-element.131), channel_id=1, source_target_pairs={{1,0},{2,1},{3,2},{4,3},{5,4},{6,5},{7,6},{8,7},{9,8},{10,9},{11,1... | collective-permute-start | bytes 7208 | tf_op jit(solution)/shard_map/ppermute | solution.py:26
  718.1 5.2 collective-permute-start.56
  718.1 5.1 collective-permute-start.57
  723.4 10.8 %collective-permute-start.58 = (f32[10,10,2,3]{2,1,0,3:T(8,128)S(1)}, f32[10,10,2,3]{2,1,0,3:T(8,128)S(1)}, u32[]{:S(2)}, u32[]{:S(2)}) collective-permute-start(f32[10,10,2,3]{2,1,0,3:T(8,128)S(1)} %get-tuple-element.128), channel_id=1, source_target_pairs={{0,1},{1,2},{2,3},{3,4},{4,5},{5,6},{6,7},{7,8},{8,9},{9,10},{10,1... | collective-permute-start | bytes 7208 | tf_op jit(solution)/shard_map/ppermute | solution.py:24
  723.5 10.7 %collective-permute-start.59 = (f32[10,10,2,3]{2,1,0,3:T(8,128)S(1)}, f32[10,10,2,3]{2,1,0,3:T(8,128)S(1)}, u32[]{:S(2)}, u32[]{:S(2)}) collective-permute-start(f32[10,10,2,3]{2,1,0,3:T(8,128)S(1)} %get-tuple-element.129), channel_id=1, source_target_pairs={{1,0},{2,1},{3,2},{4,3},{5,4},{6,5},{7,6},{8,7},{9,8},{10,9},{11,1... | collective-permute-start | bytes 7208 | tf_op jit(solution)/shard_map/ppermute | solution.py:26
  (16 other events, 89.0 us)
where the time goes:
time: 818 us; the launch traced here: 807 us
  local copies, waits for them, and re-layouts  307 us (38%)
  blocking collectives  295 us (36%)
  starting transfers between devices  95.1 us (12%)
  waiting for transfers between devices  64.2 us (8%)
  between operations  31.9 us (4%)
  other arithmetic  14.6 us (2%)
    psum x32, blocking collectives, by_axis(): shard = lax.psum(shard, axis)  295 us
    gather x18, local copies, waits for them, and re-layouts, operate(): values = ghosts.reshape(padded_count, 3)[clipped]  253 us
    ppermute x30, starting transfers between devices, padded_2(): lax.ppermute(head, axis, [((i + 1) % count, i) for i in range(ends)])  89 us
    ppermute x30, waiting for transfers between devices, padded_2(): lax.ppermute(tail, axis, [(i, (i + 1) % count) for i in range(ends)])  61.7 us
    gather x1, local copies, waits for them, and re-layouts, per_device(): remote = flattened[clipped]  23.2 us
  transfers between devices with their start and end apart: 60, of which 32 were waited for; matrix products, arithmetic and copies ran while one was open for 5% of the time, Pallas kernels for 0%

commit v1 on v0

v1 whole, which is shorter than its diff:
```python
import jax
import jax.numpy as jnp
from jax import lax
from jax.experimental import pallas as pl
from jax.experimental.pallas import tpu as pltpu
from jax.sharding import Mesh
from jax.sharding import PartitionSpec as P

ITERS = 8
BASIS = ITERS + 1
THOLE = 0.39
SPACING = 3.5
EDGE = 6
NX = 12
WIDE = 42
GZ = ("gz_0", "gz_1")
F32 = jnp.float32

OFFSETS = [
    (a, b, c)
    for a in range(-2, 3)
    for b in range(-2, 3)
    for c in range(-2, 3)
    if 1 <= a * a + b * b + c * c <= 5
]
FORWARD = [d for d in OFFSETS if d > (0, 0, 0)]
PLANES = sorted({d[1:] for d in OFFSETS})
GROUPS, PER = 5, 7


def lane_iota():
    return lax.broadcasted_iota(jnp.int32, (8, 128), 1)


def third_masks():
    lane = lane_iota()
    return lane < WIDE, lane >= 2 * WIDE


def roll_lanes(v, ahead):
    ahead = ahead % 128
    return v if ahead == 0 else pltpu.roll(v, 128 - ahead, 1)


def roll_rows(v, ahead):
    return pltpu.roll(v, (-ahead) % 8, 0)


def shifted(v, dy, dz, first, last):
    if dy == 0:
        return roll_lanes(v, dz)
    if dy == 1:
        return jnp.where(
            last, roll_rows(roll_lanes(v, dz - 2 * WIDE), 1), roll_lanes(v, dz + WIDE)
        )
    if dy == 2:
        return jnp.where(
            first, roll_lanes(v, dz + 2 * WIDE), roll_rows(roll_lanes(v, dz - WIDE), 1)
        )
    if dy == -1:
        return jnp.where(
            first, roll_rows(roll_lanes(v, dz + 2 * WIDE), -1), roll_lanes(v, dz - WIDE)
        )
    return jnp.where(
        last, roll_lanes(v, dz - 2 * WIDE), roll_rows(roll_lanes(v, dz + WIDE), -1)
    )


def wrap(x):
    return jnp.where(x >= NX, x - NX, jnp.where(x < 0, x + NX, x))


def total(v):
    return jnp.sum(jnp.sum(v, axis=0, keepdims=True), axis=1, keepdims=True)


def region_kernel(
    own, a1, a2, a3, b1, b2, b3, basis_out, start_out, polar_out, info_out,
    chan, near, coef, moved, basis, inverse,
):
    gx = lax.axis_index("gx")
    gy = lax.axis_index("gy")
    gz = lax.axis_index("gz_0") * 4 + lax.axis_index("gz_1")
    lane = lane_iota()
    first, last = third_masks()
    along = lane - jnp.where(last, 2 * WIDE, jnp.where(first, 0, WIDE))
    is_low = (lane * 0 + gx) == 0

    def gather(x, carry):
        for group in range(GROUPS):
            blocks = [
                jnp.where(is_low, b3[x, group], a3[x, group]),
                jnp.where(is_low, b2[x, group], a2[x, group]),
                jnp.where(is_low, b1[x, group], a1[x, group]),
                own[x, group],
                jnp.where(is_low, a1[x, group], b1[x, group]),
                jnp.where(is_low, a2[x, group], b2[x, group]),
                jnp.where(is_low, a3[x, group], b3[x, group]),
            ]
            blocks = [pltpu.roll(v, 2 * gy, 0) for v in blocks]
            for member in range(PER):
                acc = roll_lanes(blocks[0], 6 * member)
                for k in range(1, 7):
                    acc = jnp.where(along >= 6 * k, roll_lanes(blocks[k], 6 * (member - k)), acc)
                if group * PER + member == 3:
                    acc = jnp.where(lane >= 3 * WIDE, 1.0, acc)
                    inverse[x] = 1.0 / acc
                chan[group * PER + member, x] = acc
        return carry

    lax.fori_loop(0, NX, gather, 0)

    def spread(x, carry):
        for c in range(4):
            v = chan[3 + c, x]
            for number, (dy, dz) in enumerate(PLANES):
                near[number, c, x] = shifted(v, dy, dz, first, last)
        return carry

    lax.fori_loop(0, NX, spread, 0)

    def pairs(x, carry):
        polar = chan[3, x]
        jit = [chan[4 + c, x] for c in range(3)]
        for number, d in enumerate(FORWARD):
            other = wrap(x + d[0])
            place = PLANES.index(d[1:])
            sep = [((near[place, 1 + c, other] - jit[c]) + float(d[c])) * SPACING for c in range(3)]
            dist_sq = sep[0] * sep[0] + sep[1] * sep[1] + sep[2] * sep[2]
            over = lax.rsqrt(dist_sq)
            cube = dist_sq * dist_sq * over
            over_sq = over * over
            over_cube = over_sq * over
            damping = THOLE * cube * lax.rsqrt(polar * near[place, 0, other])
            falloff = jnp.exp(-damping)
            iso = (1.0 - falloff) * over_cube
            radial = 3.0 * (1.0 - (1.0 + damping) * falloff) * over_cube * over_sq
            root = jnp.sqrt(radial)
            here = chan[7 + number, x] > 0.5
            values = [jnp.where(here, s * root, 0.0) for s in sep] + [jnp.where(here, iso, 0.0)]
            ahead = OFFSETS.index(d)
            behind = OFFSETS.index((-d[0], -d[1], -d[2]))
            for c in range(4):
                coef[ahead, c, x] = values[c]
                coef[behind, c, other] = shifted(values[c], -d[1], -d[2], first, last)
        return carry

    lax.fori_loop(0, NX, pairs, 0)

    def spread_vector(load):
        def one(x, carry):
            for c in range(3):
                v = load(c, x)
                by_y = {dy: shifted(v, dy, 0, first, last) for dy in range(-2, 3)}
                for number, (dy, dz) in enumerate(PLANES):
                    moved[number, c, x] = roll_lanes(by_y[dy], dz)
            return carry

        lax.fori_loop(0, NX, one, 0)

    def couple(x):
        acc = [jnp.zeros((8, 128), F32) for _ in range(3)]
        for number, d in enumerate(OFFSETS):
            other = wrap(x + d[0])
            place = PLANES.index(d[1:])
            v = [moved[place, c, other] for c in range(3)]
            s = [coef[number, c, x] for c in range(3)]
            iso = coef[number, 3, x]
            dot = s[0] * v[0] + s[1] * v[1] + s[2] * v[2]
            acc = [acc[c] + (s[c] * dot - iso * v[c]) for c in range(3)]
        polar = chan[3, x]
        return [polar * t for t in acc]

    zero = jnp.zeros((8, 128), F32)
    mine = (along >= 18) & (along < 24)

    spread_vector(lambda c, x: chan[3, x] * chan[c, x])

    def begin(x, carry):
        out = couple(x)
        for c in range(3):
            basis[0, c, x] = zero
            basis[1, c, x] = out[c]
            carry = carry + out[c] * out[c] * inverse[x]
        return carry

    norm = total(jnp.where(mine, lax.fori_loop(0, NX, begin, zero), 0.0))

    def extend(k, carry):
        info, norm, before, mixed = carry
        spread_vector(lambda c, x: basis[k + 1, c, x])

        def one(x, sums):
            out = couple(x)
            for c in range(3):
                basis[k + 2, c, x] = out[c]
                weighted = out[c] * inverse[x]
                sums = (
                    sums[0] + weighted * basis[k + 1, c, x],
                    sums[1] + weighted * basis[k, c, x],
                    sums[2] + weighted * out[c],
                )
            return sums

        sums = lax.fori_loop(0, NX, one, (zero, zero, zero))
        now, past, full = [total(jnp.where(mine, s, 0.0)) for s in sums]
        tiny = 1e-30
        al = jnp.where(norm > tiny, now / jnp.maximum(norm, tiny), 0.0)
        be = jnp.where(before > tiny, past / jnp.maximum(before, tiny), 0.0)
        rest = (
            full - 2.0 * al * now - 2.0 * be * past
            + al * al * norm + be * be * before + 2.0 * al * be * mixed
        )
        rest = jnp.maximum(rest, 1e-10 * full)
        good = (rest > tiny) & (norm > tiny)
        inv = jnp.where(good, jnp.sqrt(rest / jnp.maximum(norm, tiny)), 1.0)
        inv = jnp.minimum(jnp.maximum(inv, 1e-6), 1e3)
        sc = 1.0 / inv

        def scale(x, sums):
            for c in range(3):
                u = basis[k + 1, c, x]
                new = (basis[k + 2, c, x] - al * u - be * basis[k, c, x]) * sc
                basis[k + 2, c, x] = new
                weighted = new * inverse[x]
                sums = (sums[0] + weighted * new, sums[1] + weighted * u)
            return sums

        sums = lax.fori_loop(0, NX, scale, (zero, zero))
        after, mixed = [total(jnp.where(mine, s, 0.0)) for s in sums]
        info = jnp.where(lane == 45 + k, al, info)
        info = jnp.where(lane == 53 + k, be, info)
        info = jnp.where(lane == 61 + k, inv, info)
        return info, after, norm, mixed

    none = jnp.zeros((1, 1), F32)
    info, _, _, _ = lax.fori_loop(0, ITERS, extend, (zero, norm, none, none))

    number = 0
    for low, high in ((0, 3), (3, BASIS)):
        entries = [(i, j) for i in range(low, high) for j in range(i, BASIS)]

        def one(x, sums):
            sums = list(sums)
            for c in range(3):
                u = {j: basis[j + 1, c, x] for j in range(low, BASIS)}
                for i in range(low, high):
                    weighted = u[i] * inverse[x]
                    for n, (p, q) in enumerate(entries):
                        if p == i:
                            sums[n] = sums[n] + weighted * u[q]
            return tuple(sums)

        sums = lax.fori_loop(0, NX, one, (zero,) * len(entries))
        for n in range(len(entries)):
            info = jnp.where(lane == number, total(jnp.where(mine, sums[n], 0.0)), info)
            number += 1

    row = lax.broadcasted_iota(jnp.int32, (8, 128), 0)
    info_out[0:8, :] = jnp.where(row == gz, info, 0.0)
    info_out[8:16, :] = jnp.where(row + 8 == gz, info, 0.0)

    def keep(x, carry):
        far = x + EDGE * gx

        def front(v):
            return pltpu.roll(roll_lanes(v, 18), 8 - 2 * gy, 0)

        for c in range(3):
            for k in range(BASIS):
                basis_out[k, c, x] = front(basis[k + 1, c, far])
            start_out[c, x] = front(chan[3, far] * chan[c, far])
        polar_out[x] = front(inverse[far])
        return carry

    lax.fori_loop(0, EDGE, keep, 0)


def finish_kernel(basis, start, inverse, info, dip_out, res_out, len_out, table):
    gz = lax.axis_index("gz_0") * 4 + lax.axis_index("gz_1")
    wide = jnp.concatenate([info[...], jnp.zeros((112, 128), F32)], axis=0)
    table[...] = wide.T
    rows = {}
    number = 0
    for low, high in ((0, 3), (3, BASIS)):
        for i in range(low, high):
            for j in range(i, BASIS):
                rows[i, j] = rows[j, i] = table[number : number + 1, :]
                number += 1
    al = [table[45 + k : 46 + k, :] for k in range(ITERS)]
    be = [table[53 + k : 54 + k, :] for k in range(ITERS)]
    inv = [table[61 + k : 62 + k, :] for k in range(ITERS)]
    lane = lax.broadcasted_iota(jnp.int32, (1, 128), 1)
    zero = jnp.zeros((1, 128), F32)
    one = jnp.where(lane < 16, 1.0, 0.0)

    def summed(v):
        return jnp.sum(v, axis=1, keepdims=True)

    def form(left, right, size_left, size_right):
        acc = zero
        for i in range(size_left):
            inner = zero
            for j in range(size_right):
                inner = inner + rows[i, j] * right[j]
            acc = acc + left[i] * inner
        return summed(acc)

    search = [one] + [zero] * ITERS
    resid = [one] + [zero] * ITERS
    moves = [zero] * BASIS
    gamma = summed(rows[0, 0])
    lengths = jnp.zeros((8, 128), F32)
    lanes = lane_iota()
    for k in range(ITERS):
        image = list(search)
        for j in range(k + 1):
            image[j] = image[j] - al[j] * search[j]
            image[j + 1] = image[j + 1] - inv[j] * search[j]
            if j:
                image[j - 1] = image[j - 1] - be[j] * search[j]
        step = gamma / form(search, image, k + 1, k + 2)
        lengths = jnp.where(lanes == k, step, lengths)
        moves = [moves[j] + step * search[j] for j in range(BASIS)]
        resid = [resid[j] - step * image[j] for j in range(BASIS)]
        if k + 1 < ITERS:
            after = form(resid, resid, k + 2, k + 2)
            ratio = after / gamma
            search = [resid[j] + ratio * search[j] for j in range(BASIS)]
            gamma = after
    len_out[...] = lengths
    here = lane == gz
    moves = [summed(jnp.where(here, v, 0.0)) for v in moves]
    resid = [summed(jnp.where(here, v, 0.0)) for v in resid]
    for x in range(EDGE):
        for c in range(3):
            dip = start[c, x]
            res = jnp.zeros((8, 128), F32)
            for k in range(BASIS):
                u = basis[k, c, x]
                if k < ITERS:
                    dip = dip + moves[k] * u
                res = res + resid[k] * u
            dip_out[c, x] = dip
            res_out[c, x] = res * inverse[x]


def per_device(permanent_field, polar, jitter, neighbors):
    grid = lambda dim: lax.broadcasted_iota(jnp.int32, (EDGE, EDGE, EDGE, 1), dim)
    home = ((grid(0) + 2) * 10 + grid(1) + 2) * 10 + grid(2) + 2
    relative = neighbors - home
    codes = [d[0] * 100 + d[1] * 10 + d[2] for d in FORWARD]
    flags = jnp.stack(
        [jnp.max((relative == code).astype(F32), axis=-1) for code in codes], axis=-1
    )
    sites = jnp.concatenate([permanent_field, polar[..., None], jitter, flags], axis=-1)
    packed = sites.reshape(EDGE, 2, 3, EDGE, GROUPS, PER).transpose(0, 4, 1, 2, 5, 3)
    packed = packed.reshape(EDGE, GROUPS, 2, 126)
    packed = jnp.pad(packed, ((0, 0), (0, 0), (0, 0), (0, 2)))

    both = lax.all_gather(packed, "gx", axis=0, tiled=True)
    around = [both] + [
        lax.ppermute(both, "gy", [((i + k) % 4, i) for i in range(4)]) for k in (1, 2, 3)
    ]
    own = jnp.concatenate(around, axis=2)

    def fetch(k):
        pairs = [((i + k) % 16, i) for i in range(16)]
        pairs += [(16 + (i - k) % 16, 16 + i) for i in range(16)]
        return lax.ppermute(own, ("gx",) + GZ, pairs)

    direct = [fetch(k) for k in (1, 2, 3)]
    passed = [lax.ppermute(v, "gx", [(0, 1), (1, 0)]) for v in direct]

    vreg = (8, 128)
    basis, start, inverse, info = pl.pallas_call(
        region_kernel,
        out_shape=(
            jax.ShapeDtypeStruct((BASIS, 3, EDGE) + vreg, F32),
            jax.ShapeDtypeStruct((3, EDGE) + vreg, F32),
            jax.ShapeDtypeStruct((EDGE,) + vreg, F32),
            jax.ShapeDtypeStruct((16, 128), F32),
        ),
        scratch_shapes=[
            pltpu.VMEM((GROUPS * PER, NX) + vreg, F32),
            pltpu.VMEM((len(PLANES), 4, NX) + vreg, F32),
            pltpu.VMEM((len(OFFSETS), 4, NX) + vreg, F32),
            pltpu.VMEM((len(PLANES), 3, NX) + vreg, F32),
            pltpu.VMEM((BASIS + 1, 3, NX) + vreg, F32),
            pltpu.VMEM((NX,) + vreg, F32),
        ],
        compiler_params=pltpu.CompilerParams(vmem_limit_bytes=48 * 1024 * 1024),
        name="region",
    )(own, *direct, *passed)

    info = lax.psum(lax.psum(info, "gz_1"), "gz_0")

    dip, res, lengths = pl.pallas_call(
        finish_kernel,
        out_shape=(
            jax.ShapeDtypeStruct((3, EDGE) + vreg, F32),
            jax.ShapeDtypeStruct((3, EDGE) + vreg, F32),
            jax.ShapeDtypeStruct(vreg, F32),
        ),
        scratch_shapes=[pltpu.VMEM((128, 128), F32)],
        name="finish",
    )(basis, start, inverse, info)

    def unpack(v):
        v = v[:, :, :2, :126].reshape(3, EDGE, 2, 3, WIDE)[..., :EDGE]
        return v.reshape(3, EDGE, EDGE, EDGE).transpose(1, 2, 3, 0)

    return unpack(dip), unpack(res), lengths[0, :ITERS]


def solution(mesh):
    finer = Mesh(
        mesh.devices.reshape(mesh.shape["gx"], mesh.shape["gy"], 4, 4), ("gx", "gy", "gz_0", "gz_1")
    )
    return jax.shard_map(
        per_device,
        mesh=finer,
        in_specs=(
            P("gx", "gy", GZ, None),
            P("gx", "gy", GZ),
            P("gx", "gy", GZ, None),
            P("gx", "gy", GZ, None),
        ),
        out_specs=(P("gx", "gy", GZ, None), P("gx", "gy", GZ, None), P()),
        check_vma=False,
    )
```

time: 818 us -> 168 us (0.21); the launches traced: 807 us -> 167 us
  blocking collectives: 295 us -> 21 us
  local copies, waits for them, and re-layouts: 307 us -> 35.2 us
  starting transfers between devices: 95.1 us -> 15.6 us
  Pallas kernels: 0 us -> 79 us
  waiting for transfers between devices: 64.2 us -> 13.3 us
  between operations: 31.9 us -> 0.76 us
  other arithmetic: 14.6 us -> 2.03 us
    gather x19 -> x0, local copies, waits for them, and re-layouts: 276 us -> none  [the longest x18 253 us: operate(): values = ghosts.reshape(padded_count, 3)[clipped]]
    psum x32 -> x2, blocking collectives: 295 us -> 19.1 us  [per_device(): info = lax.psum(lax.psum(info, 'gz_1'), 'gz_0')]
    ppermute x60 -> x9, starting transfers between devices: 95.1 us -> 15.6 us  [the longest x3 9.21 us: fetch(): return lax.ppermute(own, ('gx',) + GZ, pairs)]
    pallas_call x0 -> x2, Pallas kernels: none -> 79 us  [the longest x1 75.5 us: per_device(): pl.pallas_call(region_kernel, out_shape=(jax.ShapeDtypeStruct((BASIS, 3,...]
    ppermute x60 -> x9, waiting for transfers between devices: 64.2 us -> 13.3 us  [the longest x3 9.16 us: fetch(): return lax.ppermute(own, ('gx',) + GZ, pairs)]
    another operation x1 -> x28, local copies, waits for them, and re-layouts: 0.6 us -> 19.6 us  [per_device(): jnp.stack([jnp.max((relative == code).astype(F32), axis=-1) for code in c...]
    slice x38 -> x4, local copies, waits for them, and re-layouts: 10.4 us -> 1.81 us  [unpack(): v = v[:, :, :2, :126].reshape(3, EDGE, 2, 3, WIDE)[..., :EDGE]]
  transfers between devices with their start and end apart: 60 -> 9, of which waited for: 32 -> 6; matrix products, arithmetic and copies ran while one was open for 5% -> 0% of each run, Pallas kernels for 0% -> 0%
where the time goes in v1:
time: 168 us; the launch traced here: 167 us
  Pallas kernels  79 us (47%)
  local copies, waits for them, and re-layouts  35.2 us (21%)
  blocking collectives  21 us (12%)
  starting transfers between devices  15.6 us (9%)
  waiting for transfers between devices  13.3 us (8%)
  other arithmetic  2.03 us (1%)
    pallas_call x1, Pallas kernels, per_device(): pl.pallas_call(region_kernel, out_shape=(jax.ShapeDtypeStruct((BASIS, 3,...  75.5 us
    another operation x28, local copies, waits for them, and re-layouts, per_device(): jnp.stack([jnp.max((relative == code).astype(F32), axis=-1) for code in c...  19.6 us
    psum x2, blocking collectives, per_device(): info = lax.psum(lax.psum(info, 'gz_1'), 'gz_0')  19.1 us
    ppermute x3, starting transfers between devices, fetch(): return lax.ppermute(own, ('gx',) + GZ, pairs)  9.21 us
    ppermute x3, waiting for transfers between devices, fetch(): return lax.ppermute(own, ('gx',) + GZ, pairs)  9.16 us
    unnamed x16, local copies, waits for them, and re-layouts  6.07 us
    ppermute x3, starting transfers between devices, per_device(): lax.ppermute(both, 'gy', [((i + k) % 4, i) for i in range(4)])  5.83 us
    pallas_call x1, Pallas kernels, per_device(): pl.pallas_call(finish_kernel, out_shape=(jax.ShapeDtypeStruct((3, EDGE) +...  3.48 us
  transfers between devices with their start and end apart: 9, of which 6 were waited for; matrix products, arithmetic and copies ran while one was open for 0% of the time, Pallas kernels for 0%

profile of v1, /device:TPU:0, one launch (start us, length us, event | category | flops | bytes accessed | tf_op | source)
XLA Modules:
  0.0 166.9 jit_solution(7001507236068036237)
XLA Ops:
  0.7 1.2 copy.78
  2.0 0.3 copy.79
  2.3 0.6 copy-done.4
  2.8 0.3 copy.80
  3.2 0.6 copy-done.3
  3.7 1.8 %convert_reduce_fusion = (f32[6,6,6]{2,1,0:T(8,128)S(1)}, f32[6,6,6]{2,1,0:T(8,128)S(1)}, f32[6,6,6]{2,1,0:T(8,128)S(1)}, f32[6,6,6]{2,1,0:T(8,128)S(1)}, f32[6,...) fusion(s32[6,6,6,56]{3,2,1,0:T(8,128)S(1)} %copy-done.3, ...), kind=kLoop, calls=%fused_computation.1 | loop fusion | flops 1022112 | bytes 73440 | tf_op jit(solution)/shard_map/reduce_max | solution.py:354
  5.6 0.3 copy.107
  5.9 0.3 copy.108
  6.6 0.3 copy.105
  6.9 0.3 copy.104
  7.2 0.3 copy.103
  12.2 1.1 copy.88
  13.3 1.7 %copy.87 = f32[6,6,6,1]{3,2,1,0:T(8,128)} copy(f32[6,6,6,1]{2,1,0,3:T(8,128)} %bitcast.51) | data formatting | bytes 1728 | tf_op jit(solution)/shard_map/stack | solution.py:353
  15.0 1.7 %copy.86 = f32[6,6,6,1]{3,2,1,0:T(8,128)} copy(f32[6,6,6,1]{2,1,0,3:T(8,128)} %bitcast.50) | data formatting | bytes 1728 | tf_op jit(solution)/shard_map/stack | solution.py:353
  16.7 1.7 %copy.85 = f32[6,6,6,1]{3,2,1,0:T(8,128)} copy(f32[6,6,6,1]{2,1,0,3:T(8,128)} %bitcast.49) | data formatting | bytes 1728 | tf_op jit(solution)/shard_map/stack | solution.py:353
  18.4 1.7 %copy.84 = f32[6,6,6,1]{3,2,1,0:T(8,128)} copy(f32[6,6,6,1]{2,1,0,3:T(8,128)} %bitcast.48) | data formatting | bytes 1728 | tf_op jit(solution)/shard_map/stack | solution.py:353
  20.1 1.7 %copy.83 = f32[6,6,6,1]{3,2,1,0:T(8,128)} copy(f32[6,6,6,1]{2,1,0,3:T(8,128)} %bitcast.47) | data formatting | bytes 1728 | tf_op jit(solution)/shard_map/stack | solution.py:353
  21.8 1.7 %copy.82 = f32[6,6,6,1]{3,2,1,0:T(8,128)} copy(f32[6,6,6,1]{2,1,0,3:T(8,128)} %bitcast.46) | data formatting | bytes 1728 | tf_op jit(solution)/shard_map/stack | solution.py:353
  23.5 1.7 %copy.81 = f32[6,6,6,1]{3,2,1,0:T(8,128)} copy(f32[6,6,6,1]{2,1,0,3:T(8,128)} %bitcast.45) | data formatting | bytes 1728 | tf_op jit(solution)/shard_map/stack | solution.py:353
  25.2 3.4 %concatenate.6 = f32[6,6,6,35]{3,2,1,0:T(8,128)} concatenate(f32[6,6,6,3]{3,2,1,0:T(8,128)S(1)} %copy.78, f32[6,6,6,1]{3,2,1,0:T(8,128)S(1)} %copy.79, f32[6,6,6,3]{3,2,1,0:T(8,128)S(1)} %copy.80, f32[6,6,6,1]{3,2,1,0:T(8,128)} %copy.81, f32[6,6,6,1]{3,2,1,0:T(8,128)} %copy.82, f32[6,6,6,1]{3,2,1,0:T(8,128)} %copy.83, f32[6,6,6,1]{3,2,1,0:T(8,128)} %copy.84, ...), dimensions={3} | concatenate | bytes 60480 | tf_op jit(solution)/shard_map/concatenate | solution.py:356
  28.6 1.1 reshape.41
  29.7 1.2 copy.109
  31.2 1.9 %all_gather.3 = f32[12,5,2,128]{3,2,1,0:T(2,128)S(1)} all-gather(f32[6,5,2,128]{3,2,1,0:T(2,128)S(1)} %pad.4), channel_id=1, replica_groups=mesh['gx'=2,'gy'=4,'gz_0'=4,'gz_1'=4] {'gx'}, dimensions={0}, use_global_device_ids=true | all-gather | bytes 92160 | tf_op jit(solution)/shard_map/all_gather | solution.py:361
  33.1 1.7 collective-permute-start.2
  34.8 2.7 %collective-permute-start.1 = (f32[12,5,2,128]{3,2,1,0:T(2,128)S(1)}, f32[12,5,2,128]{3,2,1,0:T(2,128)S(1)}, u32[]{:S(2)}, u32[]{:S(2)}) collective-permute-start(f32[12,5,2,128]{3,2,1,0:T(2,128)S(1)} %all_gather.3), channel_id=1, source_target_pairs={{32,0},{48,16},{0,32},{16,48},{33,1},{49,17},{1,33},{17,49},{34,2}... | collective-permute-start | bytes 184328 | tf_op jit(solution)/shard_map/ppermute | solution.py:363
  37.5 1.4 collective-permute-start
  38.9 1.9 %collective-permute-done.1 = f32[12,5,2,128]{3,2,1,0:T(2,128)S(1)} collective-permute-done((f32[12,5,2,128]{3,2,1,0:T(2,128)S(1)}, f32[12,5,2,128]{3,2,1,0:T(2,128)S(1)}, u32[]{:S(2)}, u32[]{:S(2)}) %collective-permute-start.1) | collective-permute-done | bytes 61472 | tf_op jit(solution)/shard_map/ppermute | solution.py:363
  40.8 0.9 collective-permute-done
  41.8 5.1 %collective-permute-start.5 = (f32[12,5,8,128]{3,2,1,0:T(8,128)S(1)}, f32[12,5,8,128]{3,2,1,0:T(8,128)S(1)}, u32[]{:S(2)}, u32[]{:S(2)}) collective-permute-start(f32[12,5,8,128]{3,2,1,0:T(8,128)S(1)} %pad_maximum_fusion.own), channel_id=1, source_target_pairs={{3,0},{4,1},{5,2},{6,3},{7,4},{8,5},{9,6},{10,7},{11,8},{12,9},{13... | collective-permute-start | bytes 737288 | tf_op jit(solution)/shard_map/ppermute | solution.py:370
  47.0 2.7 %collective-permute-start.4 = (f32[12,5,8,128]{3,2,1,0:T(8,128)S(1)}, f32[12,5,8,128]{3,2,1,0:T(8,128)S(1)}, u32[]{:S(2)}, u32[]{:S(2)}) collective-permute-start(f32[12,5,8,128]{3,2,1,0:T(8,128)S(1)} %pad_maximum_fusion.own), channel_id=1, source_target_pairs={{2,0},{3,1},{4,2},{5,3},{6,4},{7,5},{8,6},{9,7},{10,8},{11,9},{12,... | collective-permute-start | bytes 737288 | tf_op jit(solution)/shard_map/ppermute | solution.py:370
  49.7 1.3 collective-permute-start.3
  51.0 2.2 %collective-permute-done.5.a3 = f32[12,5,8,128]{3,2,1,0:T(8,128)S(1)} collective-permute-done((f32[12,5,8,128]{3,2,1,0:T(8,128)S(1)}, f32[12,5,8,128]{3,2,1,0:T(8,128)S(1)}, u32[]{:S(2)}, u32[]{:S(2)}) %collective-permute-start.5) | collective-permute-done | bytes 245792 | tf_op jit(solution)/shard_map/ppermute | solution.py:370
  53.3 6.9 %collective-permute-done.4.a2 = f32[12,5,8,128]{3,2,1,0:T(8,128)S(1)} collective-permute-done((f32[12,5,8,128]{3,2,1,0:T(8,128)S(1)}, f32[12,5,8,128]{3,2,1,0:T(8,128)S(1)}, u32[]{:S(2)}, u32[]{:S(2)}) %collective-permute-start.4) | collective-permute-done | bytes 245792 | tf_op jit(solution)/shard_map/ppermute | solution.py:370
  60.2 0.5 collective-permute-start.6
  60.7 1.0 collective-permute-done.7.b2
  61.7 0.4 collective-permute-done.6.b1
  62.1 75.5 %region.1 = (f32[9,3,6,8,128]{4,3,2,1,0:T(8,128)S(1)}, f32[3,6,8,128]{3,2,1,0:T(8,128)S(1)}, f32[6,8,128]{2,1,0:T(8,128)S(1)}, f32[16,128]{1,0:T(8,128)S(1)}) custom-call(f32[12,5,8,128]{3,2,1,0:T(8,128)S(1)} %pad_maximum_fusion.own, f32[12,5,8,128]{3,2,1,0:T(8,128)S(1)} %collective-permute-done.3.a1, f32[12,5,8,128]{3,2,1,0:T(8,128)S(1)} %collective-permute-done.4.a2, ...), custom_call_target="tpu_custom_call" | custom-call | tf_op jit(solution)/shard_map/region/pallas_call | solution.py:376
  137.6 0.8 copy-done
  138.5 0.6 copy-done.1
  139.1 0.6 copy-done.2
  139.7 7.8 %psum.14 = f32[16,128]{1,0:T(8,128)S(1)} all-reduce(f32[16,128]{1,0:T(8,128)S(1)} %get-tuple-element.13), channel_id=1, replica_groups=mesh['gx'=2,'gy'=4,'gz_0'=4,'gz_1'=4] {'gz_1'}, use_global_device_ids=true, to_apply=%region_28.29 | all-reduce | flops 2048 | bytes 16384 | tf_op jit(solution)/shard_map/psum | solution.py:396
  147.5 11.3 %psum.15.info = f32[16,128]{1,0:T(8,128)} all-reduce(f32[16,128]{1,0:T(8,128)S(1)} %psum.14), channel_id=1, replica_groups=mesh['gx'=2,'gy'=4,'gz_0'=4,'gz_1'=4] {'gz_0'}, use_global_device_ids=true, to_apply=%region_29.30 | all-reduce | flops 2048 | bytes 16384 | tf_op jit(solution)/shard_map/psum | solution.py:396
  158.8 3.5 %finish.1 = (f32[3,6,8,128]{3,2,1,0:T(8,128)}, f32[3,6,8,128]{3,2,1,0:T(8,128)}, f32[8,128]{1,0:T(8,128)}) custom-call(f32[9,3,6,8,128]{4,3,2,1,0:T(8,128)} %copy-done, f32[3,6,8,128]{3,2,1,0:T(8,128)} %copy-done.1, f32[6,8,128]{2,1,0:T(8,128)} %copy-done.2, f32[16,128]{1,0:T(8,128)} %psum.15.info), custom_call_target="tpu_custom_call" | custom-call | tf_op jit(solution)/shard_map/finish/pallas_call | solution.py:398
  162.3 0.9 slice.15
  163.2 1.2 slice_bitcast_fusion
  164.4 0.9 slice.17
  165.4 0.7 copy.113
  166.2 0.7 copy.112
  (36 shorter events, 5.7 us)
Async XLA Ops:
  0.7 1.2 copy-start.5
  1.9 0.9 copy-start.4
  2.8 0.9 copy-start.3
  33.1 5.8 %collective-permute-start.2 = (f32[12,5,2,128]{3,2,1,0:T(2,128)S(1)}, f32[12,5,2,128]{3,2,1,0:T(2,128)S(1)}, u32[]{:S(2)}, u32[]{:S(2)}) collective-permute-start(f32[12,5,2,128]{3,2,1,0:T(2,128)S(1)} %all_gather.3), channel_id=1, source_target_pairs={{48,0},{0,16},{16,32},{32,48},{49,1},{1,17},{17,33},{33,49},{50,2}... | collective-permute-start | bytes 184328 | tf_op jit(solution)/shard_map/ppermute | solution.py:363
  34.8 6.1 %collective-permute-start.1 = (f32[12,5,2,128]{3,2,1,0:T(2,128)S(1)}, f32[12,5,2,128]{3,2,1,0:T(2,128)S(1)}, u32[]{:S(2)}, u32[]{:S(2)}) collective-permute-start(f32[12,5,2,128]{3,2,1,0:T(2,128)S(1)} %all_gather.3), channel_id=1, source_target_pairs={{32,0},{48,16},{0,32},{16,48},{33,1},{49,17},{1,33},{17,49},{34,2}... | collective-permute-start | bytes 184328 | tf_op jit(solution)/shard_map/ppermute | solution.py:363
  37.5 4.2 %collective-permute-start = (f32[12,5,2,128]{3,2,1,0:T(2,128)S(1)}, f32[12,5,2,128]{3,2,1,0:T(2,128)S(1)}, u32[]{:S(2)}, u32[]{:S(2)}) collective-permute-start(f32[12,5,2,128]{3,2,1,0:T(2,128)S(1)} %all_gather.3), channel_id=1, source_target_pairs={{16,0},{32,16},{48,32},{0,48},{17,1},{33,17},{49,33},{1,49},{18,2}... | collective-permute-start | bytes 184328 | tf_op jit(solution)/shard_map/ppermute | solution.py:363
  41.8 11.4 %collective-permute-start.5 = (f32[12,5,8,128]{3,2,1,0:T(8,128)S(1)}, f32[12,5,8,128]{3,2,1,0:T(8,128)S(1)}, u32[]{:S(2)}, u32[]{:S(2)}) collective-permute-start(f32[12,5,8,128]{3,2,1,0:T(8,128)S(1)} %pad_maximum_fusion.own), channel_id=1, source_target_pairs={{3,0},{4,1},{5,2},{6,3},{7,4},{8,5},{9,6},{10,7},{11,8},{12,9},{13... | collective-permute-start | bytes 737288 | tf_op jit(solution)/shard_map/ppermute | solution.py:370
  47.0 13.3 %collective-permute-start.4 = (f32[12,5,8,128]{3,2,1,0:T(8,128)S(1)}, f32[12,5,8,128]{3,2,1,0:T(8,128)S(1)}, u32[]{:S(2)}, u32[]{:S(2)}) collective-permute-start(f32[12,5,8,128]{3,2,1,0:T(8,128)S(1)} %pad_maximum_fusion.own), channel_id=1, source_target_pairs={{2,0},{3,1},{4,2},{5,3},{6,4},{7,5},{8,6},{9,7},{10,8},{11,9},{12,... | collective-permute-start | bytes 737288 | tf_op jit(solution)/shard_map/ppermute | solution.py:370
  49.7 10.5 %collective-permute-start.3 = (f32[12,5,8,128]{3,2,1,0:T(8,128)S(1)}, f32[12,5,8,128]{3,2,1,0:T(8,128)S(1)}, u32[]{:S(2)}, u32[]{:S(2)}) collective-permute-start(f32[12,5,8,128]{3,2,1,0:T(8,128)S(1)} %pad_maximum_fusion.own), channel_id=1, source_target_pairs={{1,0},{2,1},{3,2},{4,3},{5,4},{6,5},{7,6},{8,7},{9,8},{10,9},{11,1... | collective-permute-start | bytes 737288 | tf_op jit(solution)/shard_map/ppermute | solution.py:370
  53.3 7.4 %collective-permute-start.8 = (f32[12,5,8,128]{3,2,1,0:T(8,128)S(1)}, f32[12,5,8,128]{3,2,1,0:T(8,128)S(1)}, u32[]{:S(2)}, u32[]{:S(2)}) collective-permute-start(f32[12,5,8,128]{3,2,1,0:T(8,128)S(1)} %collective-permute-done.5.a3), channel_id=1, source_target_pairs={{0,64},{64,0},{1,65},{65,1},{2,66},{66,2},{3,67},{67,3},{4,68},{68... | collective-permute-start | bytes 737288 | tf_op jit(solution)/shard_map/ppermute | solution.py:373
  60.2 1.5 collective-permute-start.7
  60.2 1.9 %collective-permute-start.6 = (f32[12,5,8,128]{3,2,1,0:T(8,128)S(1)}, f32[12,5,8,128]{3,2,1,0:T(8,128)S(1)}, u32[]{:S(2)}, u32[]{:S(2)}) collective-permute-start(f32[12,5,8,128]{3,2,1,0:T(8,128)S(1)} %collective-permute-done.3.a1), channel_id=1, source_target_pairs={{0,64},{64,0},{1,65},{65,1},{2,66},{66,2},{3,67},{67,3},{4,68},{68... | collective-permute-start | bytes 737288 | tf_op jit(solution)/shard_map/ppermute | solution.py:373
  137.6 0.8 copy-start
  138.5 0.6 copy-start.1
  139.1 0.6 copy-start.2

commit v2 on v1

v2 whole, which is shorter than its diff:
```python
import jax
import jax.numpy as jnp
from jax import lax
from jax.experimental import pallas as pl
from jax.experimental.pallas import tpu as pltpu
from jax.sharding import Mesh
from jax.sharding import PartitionSpec as P

ITERS = 8
BASIS = ITERS + 1
THOLE = 0.39
SPACING = 3.5
EDGE = 6
NX = 12
WIDE = 42
GZ = ("gz_0", "gz_1")
F32 = jnp.float32

OFFSETS = [
    (a, b, c)
    for a in range(-2, 3)
    for b in range(-2, 3)
    for c in range(-2, 3)
    if 1 <= a * a + b * b + c * c <= 5
]
FORWARD = [d for d in OFFSETS if d > (0, 0, 0)]
PLANES = sorted({d[1:] for d in OFFSETS})
GROUPS, PER = 5, 7


def lane_iota():
    return lax.broadcasted_iota(jnp.int32, (8, 128), 1)


def third_masks():
    lane = lane_iota()
    return lane < WIDE, lane >= 2 * WIDE


def roll_lanes(v, ahead):
    ahead = ahead % 128
    return v if ahead == 0 else pltpu.roll(v, 128 - ahead, 1)


def roll_rows(v, ahead):
    return pltpu.roll(v, (-ahead) % 8, 0)


def shifted(v, dy, dz, first, last):
    if dy == 0:
        return roll_lanes(v, dz)
    if dy == 1:
        return jnp.where(
            last, roll_rows(roll_lanes(v, dz - 2 * WIDE), 1), roll_lanes(v, dz + WIDE)
        )
    if dy == 2:
        return jnp.where(
            first, roll_lanes(v, dz + 2 * WIDE), roll_rows(roll_lanes(v, dz - WIDE), 1)
        )
    if dy == -1:
        return jnp.where(
            first, roll_rows(roll_lanes(v, dz + 2 * WIDE), -1), roll_lanes(v, dz - WIDE)
        )
    return jnp.where(
        last, roll_lanes(v, dz - 2 * WIDE), roll_rows(roll_lanes(v, dz + WIDE), -1)
    )


def wrap(x):
    return jnp.where(x >= NX, x - NX, jnp.where(x < 0, x + NX, x))


def total(v):
    return jnp.sum(jnp.sum(v, axis=0, keepdims=True), axis=1, keepdims=True)


def unrolled(count, times, body, carry):
    def several(i, carry):
        for t in range(times):
            carry = body(i * times + t, carry)
        return carry

    return lax.fori_loop(0, count // times, several, carry)


def pack_kernel(field, polar, jitter, neighbors, out):
    lane = lax.broadcasted_iota(jnp.int32, (1, 128), 1)
    third = jnp.where(lane >= 2 * WIDE, 2, jnp.where(lane >= WIDE, 1, 0))
    inside = lane - third * WIDE
    member = inside // EDGE
    z = inside - member * EDGE
    wanted = []
    for group in range(1, GROUPS):
        code = jnp.full((1, 128), -5000, jnp.int32)
        for n in range(PER):
            d = FORWARD[(group - 1) * PER + n]
            code = jnp.where(member == n, d[0] * 100 + d[1] * 10 + d[2], code)
        wanted.append(jnp.where(lane < 3 * WIDE, code + third * 10 + z, -5000))
    row = lax.broadcasted_iota(jnp.int32, (EDGE, 128), 0)
    column = lax.broadcasted_iota(jnp.int32, (EDGE, 128), 1)
    pick = []
    for t in range(3):
        hit = column * 0 > 0
        for n in range(PER):
            hit = hit | (column == row + (t * WIDE + n * EDGE))
        pick.append(jnp.where(hit, 1.0, 0.0))

    def one(x, carry):
        for s in range(2):
            slots = jnp.zeros((56, 128), F32)
            values = jnp.zeros((1, 128), F32)
            for t in range(3):
                y = 3 * s + t
                slots = slots + lax.dot_general(
                    neighbors[x, y].astype(F32), pick[t], (((0,), (0,)), ((), ())),
                    precision=lax.Precision.HIGHEST, preferred_element_type=F32,
                )
                parts = [field[x, y, c : c + 1, :] for c in range(3)]
                parts += [polar[x, y : y + 1, :]]
                parts += [jitter[x, y, c : c + 1, :] for c in range(3)]
                for n in range(PER):
                    wide = jnp.concatenate([parts[n], jnp.zeros((1, 122), F32)], axis=1)
                    start = t * WIDE + n * EDGE
                    values = values + (pltpu.roll(wide, start, 1) if start else wide)
            out[x, 0, s : s + 1, :] = values
            home = (x + 2) * 100 + (2 + 3 * s) * 10 + 2
            for group in range(1, GROUPS):
                target = (wanted[group - 1] + home).astype(F32)
                flag = jnp.max(jnp.where(slots == target, 1.0, 0.0), axis=0, keepdims=True)
                out[x, group, s : s + 1, :] = flag
        return carry

    lax.fori_loop(0, EDGE, one, 0)


def region_kernel(
    own, a1, a2, a3, b1, b2, b3, kept_out, info_out,
    chan, near, coef, moved, basis,
):
    gx = lax.axis_index("gx")
    gy = lax.axis_index("gy")
    gz = lax.axis_index("gz_0") * 4 + lax.axis_index("gz_1")
    lane = lane_iota()
    first, last = third_masks()
    along = lane - jnp.where(last, 2 * WIDE, jnp.where(first, 0, WIDE))
    is_low = (lane * 0 + gx) == 0

    def gather(x, carry):
        for group in range(GROUPS):
            blocks = [
                jnp.where(is_low, b3[x, group], a3[x, group]),
                jnp.where(is_low, b2[x, group], a2[x, group]),
                jnp.where(is_low, b1[x, group], a1[x, group]),
                own[x, group],
                jnp.where(is_low, a1[x, group], b1[x, group]),
                jnp.where(is_low, a2[x, group], b2[x, group]),
                jnp.where(is_low, a3[x, group], b3[x, group]),
            ]
            blocks = [pltpu.roll(v, 2 * gy, 0) for v in blocks]
            for member in range(PER):
                acc = roll_lanes(blocks[0], 6 * member)
                for k in range(1, 7):
                    acc = jnp.where(along >= 6 * k, roll_lanes(blocks[k], 6 * (member - k)), acc)
                if group * PER + member == 3:
                    acc = jnp.where(lane >= 3 * WIDE, 1.0, acc)
                    chan[x, 35] = 1.0 / acc
                chan[x, group * PER + member] = acc
        return carry

    lax.fori_loop(0, NX, gather, 0)

    def spread(x, carry):
        for c in range(4):
            v = chan[x, 3 + c]
            for number, (dy, dz) in enumerate(PLANES):
                near[x, number * 4 + c] = shifted(v, dy, dz, first, last)
        return carry

    unrolled(NX, 3, spread, 0)

    def pairs(x, carry):
        polar = chan[x, 3]
        jit = [chan[x, 4 + c] for c in range(3)]
        for number, d in enumerate(FORWARD):
            other = wrap(x + d[0])
            place = PLANES.index(d[1:]) * 4
            sep = [((near[other, place + 1 + c] - jit[c]) + float(d[c])) * SPACING for c in range(3)]
            dist_sq = sep[0] * sep[0] + sep[1] * sep[1] + sep[2] * sep[2]
            over = lax.rsqrt(dist_sq)
            cube = dist_sq * dist_sq * over
            over_sq = over * over
            over_cube = over_sq * over
            damping = THOLE * cube * lax.rsqrt(polar * near[other, place])
            falloff = jnp.exp(-damping)
            iso = (1.0 - falloff) * over_cube
            radial = 3.0 * (1.0 - (1.0 + damping) * falloff) * over_cube * over_sq
            root = jnp.sqrt(radial)
            here = chan[x, 7 + number] > 0.5
            values = [jnp.where(here, s * root, 0.0) for s in sep] + [jnp.where(here, iso, 0.0)]
            ahead = OFFSETS.index(d) * 4
            behind = OFFSETS.index((-d[0], -d[1], -d[2])) * 4
            for c in range(4):
                coef[x, ahead + c] = values[c]
                coef[other, behind + c] = shifted(values[c], -d[1], -d[2], first, last)
        return carry

    lax.fori_loop(0, NX, pairs, 0)

    def move(x, c, v):
        by_y = {dy: shifted(v, dy, 0, first, last) for dy in range(-2, 3)}
        for number, (dy, dz) in enumerate(PLANES):
            moved[x, number * 3 + c] = roll_lanes(by_y[dy], dz)

    def couple(x):
        acc = [jnp.zeros((8, 128), F32) for _ in range(3)]
        for number, d in enumerate(OFFSETS):
            other = wrap(x + d[0])
            place = PLANES.index(d[1:]) * 3
            v = [moved[other, place + c] for c in range(3)]
            s = [coef[x, number * 4 + c] for c in range(3)]
            iso = coef[x, number * 4 + 3]
            dot = s[0] * v[0] + s[1] * v[1] + s[2] * v[2]
            acc = [acc[c] + (s[c] * dot - iso * v[c]) for c in range(3)]
        polar = chan[x, 3]
        return [polar * t for t in acc]

    zero = jnp.zeros((8, 128), F32)
    mine = (along >= 18) & (along < 24)

    def start(x, carry):
        for c in range(3):
            move(x, c, chan[x, 3] * chan[x, c])
        return carry

    unrolled(NX, 4, start, 0)

    def begin(x, carry):
        out = couple(x)
        for c in range(3):
            basis[0, x * 3 + c] = zero
            basis[1, x * 3 + c] = out[c]
        return carry

    lax.fori_loop(0, NX, begin, 0)

    def again(x, carry):
        for c in range(3):
            move(x, c, basis[1, x * 3 + c])
        return carry

    unrolled(NX, 4, again, 0)

    def extend(k, info):
        def one(x, sums):
            out = couple(x)
            over = chan[x, 35]
            sums = list(sums)
            for c in range(3):
                u = basis[k + 1, x * 3 + c]
                p = basis[k, x * 3 + c]
                basis[k + 2, x * 3 + c] = out[c]
                w = out[c] * over
                uw = u * over
                sums[0] = sums[0] + w * u
                sums[1] = sums[1] + w * p
                sums[2] = sums[2] + w * out[c]
                sums[3] = sums[3] + uw * u
                sums[4] = sums[4] + uw * p
                sums[5] = sums[5] + (p * over) * p
            return tuple(sums)

        sums = lax.fori_loop(0, NX, one, (zero,) * 6)
        now, past, full, norm, mixed, before = [total(jnp.where(mine, s, 0.0)) for s in sums]
        tiny = 1e-30
        al = jnp.where(norm > tiny, now / jnp.maximum(norm, tiny), 0.0)
        be = jnp.where(before > tiny, past / jnp.maximum(before, tiny), 0.0)
        rest = (
            full - 2.0 * al * now - 2.0 * be * past
            + al * al * norm + be * be * before + 2.0 * al * be * mixed
        )
        rest = jnp.maximum(rest, 1e-10 * full)
        good = (rest > tiny) & (norm > tiny)
        inv = jnp.where(good, jnp.sqrt(rest / jnp.maximum(norm, tiny)), 1.0)
        inv = jnp.minimum(jnp.maximum(inv, 1e-6), 1e3)
        sc = 1.0 / inv

        def scale(x, carry):
            for c in range(3):
                at = x * 3 + c
                new = (basis[k + 2, at] - al * basis[k + 1, at] - be * basis[k, at]) * sc
                basis[k + 2, at] = new
                move(x, c, new)
            return carry

        unrolled(NX, 4, scale, 0)
        info = jnp.where(lane == 45 + k, al, info)
        info = jnp.where(lane == 53 + k, be, info)
        return jnp.where(lane == 61 + k, inv, info)

    info = lax.fori_loop(0, ITERS, extend, zero)

    number = 0
    for low, high in ((0, 3), (3, BASIS)):
        entries = [(i, j) for i in range(low, high) for j in range(i, BASIS)]

        def one(x, sums):
            sums = list(sums)
            for c in range(3):
                u = {j: basis[j + 1, x * 3 + c] for j in range(low, BASIS)}
                for i in range(low, high):
                    weighted = u[i] * chan[x, 35]
                    for n, (p, q) in enumerate(entries):
                        if p == i:
                            sums[n] = sums[n] + weighted * u[q]
            return tuple(sums)

        sums = lax.fori_loop(0, NX, one, (zero,) * len(entries))
        for n in range(len(entries)):
            info = jnp.where(lane == number, total(jnp.where(mine, sums[n], 0.0)), info)
            number += 1

    row = lax.broadcasted_iota(jnp.int32, (8, 128), 0)
    info_out[0:8, :] = jnp.where(row == gz, info, 0.0)
    info_out[8:16, :] = jnp.where(row + 8 == gz, info, 0.0)

    def keep(x, carry):
        far = x + EDGE * gx

        def front(v):
            return pltpu.roll(roll_lanes(v, 18), 8 - 2 * gy, 0)

        for c in range(3):
            for k in range(BASIS):
                kept_out[x, k * 3 + c] = front(basis[k + 1, far * 3 + c])
            kept_out[x, 27 + c] = front(chan[far, 3] * chan[far, c])
        kept_out[x, 30] = front(chan[far, 35])
        return carry

    unrolled(EDGE, 2, keep, 0)


def finish_kernel(kept, info, dip_out, res_out, len_out, table):
    gz = lax.axis_index("gz_0") * 4 + lax.axis_index("gz_1")
    wide = jnp.concatenate([info[...], jnp.zeros((112, 128), F32)], axis=0)
    table[...] = wide.T
    rows = {}
    number = 0
    for low, high in ((0, 3), (3, BASIS)):
        for i in range(low, high):
            for j in range(i, BASIS):
                rows[i, j] = rows[j, i] = table[number : number + 1, :]
                number += 1
    al = [table[45 + k : 46 + k, :] for k in range(ITERS)]
    be = [table[53 + k : 54 + k, :] for k in range(ITERS)]
    inv = [table[61 + k : 62 + k, :] for k in range(ITERS)]
    lane = lax.broadcasted_iota(jnp.int32, (1, 128), 1)
    zero = jnp.zeros((1, 128), F32)
    one = jnp.where(lane < 16, 1.0, 0.0)

    def summed(v):
        return jnp.sum(v, axis=1, keepdims=True)

    def form(left, right, size_left, size_right):
        acc = zero
        for i in range(size_left):
            inner = zero
            for j in range(size_right):
                inner = inner + rows[i, j] * right[j]
            acc = acc + left[i] * inner
        return summed(acc)

    search = [one] + [zero] * ITERS
    resid = [one] + [zero] * ITERS
    moves = [zero] * BASIS
    gamma = summed(rows[0, 0])
    lengths = zero
    for k in range(ITERS):
        image = list(search)
        for j in range(k + 1):
            image[j] = image[j] - al[j] * search[j]
            image[j + 1] = image[j + 1] - inv[j] * search[j]
            if j:
                image[j - 1] = image[j - 1] - be[j] * search[j]
        step = gamma / form(search, image, k + 1, k + 2)
        lengths = jnp.where(lane == k, step, lengths)
        moves = [moves[j] + step * search[j] for j in range(BASIS)]
        resid = [resid[j] - step * image[j] for j in range(BASIS)]
        if k + 1 < ITERS:
            after = form(resid, resid, k + 2, k + 2)
            ratio = after / gamma
            search = [resid[j] + ratio * search[j] for j in range(BASIS)]
            gamma = after
    len_out[...] = lengths[:, :ITERS]
    here = lane == gz
    moves = [summed(jnp.where(here, v, 0.0)) for v in moves]
    resid = [summed(jnp.where(here, v, 0.0)) for v in resid]
    for x in range(EDGE):
        for c in range(3):
            dip = kept[x, 27 + c]
            res = jnp.zeros((8, 128), F32)
            for k in range(BASIS):
                u = kept[x, k * 3 + c]
                if k < ITERS:
                    dip = dip + moves[k] * u
                res = res + resid[k] * u
            res = res * kept[x, 30]
            for out, v in ((dip_out, dip), (res_out, res)):
                for t in range(3):
                    w = roll_lanes(v, t * WIDE)
                    for s in range(2):
                        out[x, 3 * s + t, c : c + 1, :] = w[s : s + 1, :EDGE]


def per_device(permanent_field, polar, jitter, neighbors):
    packed = pl.pallas_call(
        pack_kernel,
        out_shape=jax.ShapeDtypeStruct((EDGE, GROUPS, 2, 128), F32),
        name="pack",
    )(permanent_field.transpose(0, 1, 3, 2), polar, jitter.transpose(0, 1, 3, 2), neighbors)

    both = lax.all_gather(packed, "gx", axis=0, tiled=True)
    around = [both] + [
        lax.ppermute(both, "gy", [((i + k) % 4, i) for i in range(4)]) for k in (1, 2, 3)
    ]
    own = jnp.concatenate(around, axis=2)

    def fetch(k):
        pairs = [((i + k) % 16, i) for i in range(16)]
        pairs += [(16 + (i - k) % 16, 16 + i) for i in range(16)]
        return lax.ppermute(own, ("gx",) + GZ, pairs)

    direct = [fetch(k) for k in (1, 2, 3)]
    passed = [lax.ppermute(v, "gx", [(0, 1), (1, 0)]) for v in direct]

    vreg = (8, 128)
    kept, info = pl.pallas_call(
        region_kernel,
        out_shape=(
            jax.ShapeDtypeStruct((EDGE, 31) + vreg, F32),
            jax.ShapeDtypeStruct((16, 128), F32),
        ),
        scratch_shapes=[
            pltpu.VMEM((NX, 36) + vreg, F32),
            pltpu.VMEM((NX, 4 * len(PLANES)) + vreg, F32),
            pltpu.VMEM((NX, 4 * len(OFFSETS)) + vreg, F32),
            pltpu.VMEM((NX, 64) + vreg, F32),
            pltpu.VMEM((BASIS + 1, 3 * NX) + vreg, F32),
        ],
        compiler_params=pltpu.CompilerParams(vmem_limit_bytes=36 * 1024 * 1024),
        name="region",
    )(own, *direct, *passed)

    info = lax.psum(lax.psum(info, "gz_1"), "gz_0")

    dip, res, lengths = pl.pallas_call(
        finish_kernel,
        out_shape=(
            jax.ShapeDtypeStruct((EDGE, EDGE, 3, EDGE), F32),
            jax.ShapeDtypeStruct((EDGE, EDGE, 3, EDGE), F32),
            jax.ShapeDtypeStruct((1, ITERS), F32),
        ),
        scratch_shapes=[pltpu.VMEM((128, 128), F32)],
        compiler_params=pltpu.CompilerParams(vmem_limit_bytes=8 * 1024 * 1024),
        name="finish",
    )(kept, info)
    return dip.transpose(0, 1, 3, 2), res.transpose(0, 1, 3, 2), lengths.reshape(ITERS)


def solution(mesh):
    finer = Mesh(
        mesh.devices.reshape(mesh.shape["gx"], mesh.shape["gy"], 4, 4), ("gx", "gy", "gz_0", "gz_1")
    )
    return jax.shard_map(
        per_device,
        mesh=finer,
        in_specs=(
            P("gx", "gy", GZ, None),
            P("gx", "gy", GZ),
            P("gx", "gy", GZ, None),
            P("gx", "gy", GZ, None),
        ),
        out_specs=(P("gx", "gy", GZ, None), P("gx", "gy", GZ, None), P()),
        check_vma=False,
    )
```

time: 168 us -> 108 us (0.64)
  local copies, waits for them, and re-layouts: 35.2 us -> 0 us
  Pallas kernels: 79 us -> 58 us
  other arithmetic: 2.03 us -> 0.12 us
    pallas_call x2 -> x3, Pallas kernels: 79 us -> 58 us  [the longest x1 51 us: per_device(): pl.pallas_call(region_kernel, out_shape=(jax.ShapeDtypeStruct((EDGE, 31)...]
    another operation x28 -> x0, local copies, waits for them, and re-layouts: 19.6 us -> none  [per_device(): jnp.stack([jnp.max((relative == code).astype(F32), axis=-1) for code in c...]
    unnamed x16 -> x0, local copies, waits for them, and re-layouts: 6.07 us -> none
    concatenate x1 -> x0, local copies, waits for them, and re-layouts: 3.41 us -> none  [per_device(): jnp.concatenate([permanent_field, polar[..., None], jitter, flags], axis=-1)]
    reduce_max x1 -> x0, other arithmetic: 1.83 us -> none  [per_device(): jnp.max((relative == code).astype(F32), axis=-1)]
    slice x4 -> x0, local copies, waits for them, and re-layouts: 1.81 us -> none  [unpack(): v = v[:, :, :2, :126].reshape(3, EDGE, 2, 3, WIDE)[..., :EDGE]]
where the time goes in v2:
time: 108 us
  Pallas kernels  58 us (54%)
  blocking collectives  20.6 us (19%)
  starting transfers between devices  15.6 us (14%)
  waiting for transfers between devices  13.3 us (12%)
    pallas_call x1, Pallas kernels, per_device(): pl.pallas_call(region_kernel, out_shape=(jax.ShapeDtypeStruct((EDGE, 31)...  51 us
    psum x2, blocking collectives, per_device(): info = lax.psum(lax.psum(info, 'gz_1'), 'gz_0')  18.6 us
    ppermute x3, starting transfers between devices, fetch(): return lax.ppermute(own, ('gx',) + GZ, pairs)  9.21 us
    ppermute x3, waiting for transfers between devices, fetch(): return lax.ppermute(own, ('gx',) + GZ, pairs)  9.16 us
    ppermute x3, starting transfers between devices, per_device(): lax.ppermute(both, 'gy', [((i + k) % 4, i) for i in range(4)])  5.84 us
    pallas_call x1, Pallas kernels, per_device(): pl.pallas_call(pack_kernel, out_shape=jax.ShapeDtypeStruct((EDGE, GROUPS,...  4.58 us
    ppermute x3, waiting for transfers between devices, per_device(): lax.ppermute(both, 'gy', [((i + k) % 4, i) for i in range(4)])  2.79 us
    pallas_call x1, Pallas kernels, per_device(): pl.pallas_call(finish_kernel, out_shape=(jax.ShapeDtypeStruct((EDGE, EDGE...  2.46 us
  transfers between devices with their start and end apart: 9, of which 6 were waited for; matrix products, arithmetic and copies ran while one was open for 0% of the time, Pallas kernels for 0%

profile of v2, /device:TPU:0, one launch (start us, length us, event | category | flops | bytes accessed | tf_op | source)
XLA Modules:
  0.0 108.3 jit_solution(6710977144835684036)
XLA Ops:
  0.6 4.6 %pack.1 = f32[6,5,2,128]{3,2,1,0:T(2,128)} custom-call(f32[6,6,3,6]{3,2,1,0:T(4,128)} %bitcast.5, f32[6,6,6]{2,1,0:T(8,128)} %polar.1, f32[6,6,3,6]{3,2,1,0:T(4,128)} %bitcast.6, s32[6,6,6,56]{3,2,1,0:T(8,128)} %neighbors.1), custom_call_target="tpu_custom_call" | custom-call | tf_op jit(solution)/shard_map/pack/pallas_call | solution.py:415
  5.2 2.1 %all_gather.3 = f32[12,5,2,128]{3,2,1,0:T(2,128)S(1)} all-gather(f32[6,5,2,128]{3,2,1,0:T(2,128)} %pack.1), channel_id=1, replica_groups=mesh['gx'=2,'gy'=4,'gz_0'=4,'gz_1'=4] {'gx'}, dimensions={0}, use_global_device_ids=true | all-gather | bytes 92160 | tf_op jit(solution)/shard_map/all_gather | solution.py:421
  7.3 1.7 %collective-permute-start.2 = (f32[12,5,2,128]{3,2,1,0:T(2,128)S(1)}, f32[12,5,2,128]{3,2,1,0:T(2,128)S(1)}, u32[]{:S(2)}, u32[]{:S(2)}) collective-permute-start(f32[12,5,2,128]{3,2,1,0:T(2,128)S(1)} %all_gather.3), channel_id=1, source_target_pairs={{48,0},{0,16},{16,32},{32,48},{49,1},{1,17},{17,33},{33,49},{50,2}... | collective-permute-start | bytes 184328 | tf_op jit(solution)/shard_map/ppermute | solution.py:423
  8.9 2.7 %collective-permute-start.1 = (f32[12,5,2,128]{3,2,1,0:T(2,128)S(1)}, f32[12,5,2,128]{3,2,1,0:T(2,128)S(1)}, u32[]{:S(2)}, u32[]{:S(2)}) collective-permute-start(f32[12,5,2,128]{3,2,1,0:T(2,128)S(1)} %all_gather.3), channel_id=1, source_target_pairs={{32,0},{48,16},{0,32},{16,48},{33,1},{49,17},{1,33},{17,49},{34,2}... | collective-permute-start | bytes 184328 | tf_op jit(solution)/shard_map/ppermute | solution.py:423
  11.7 1.4 %collective-permute-start = (f32[12,5,2,128]{3,2,1,0:T(2,128)S(1)}, f32[12,5,2,128]{3,2,1,0:T(2,128)S(1)}, u32[]{:S(2)}, u32[]{:S(2)}) collective-permute-start(f32[12,5,2,128]{3,2,1,0:T(2,128)S(1)} %all_gather.3), channel_id=1, source_target_pairs={{16,0},{32,16},{48,32},{0,48},{17,1},{33,17},{49,33},{1,49},{18,2}... | collective-permute-start | bytes 184328 | tf_op jit(solution)/shard_map/ppermute | solution.py:423
  13.1 0.0 collective-permute-done.2
  13.1 1.9 %collective-permute-done.1 = f32[12,5,2,128]{3,2,1,0:T(2,128)S(1)} collective-permute-done((f32[12,5,2,128]{3,2,1,0:T(2,128)S(1)}, f32[12,5,2,128]{3,2,1,0:T(2,128)S(1)}, u32[]{:S(2)}, u32[]{:S(2)}) %collective-permute-start.1) | collective-permute-done | bytes 61472 | tf_op jit(solution)/shard_map/ppermute | solution.py:423
  15.0 0.9 collective-permute-done
  15.9 0.1 pad_maximum_fusion.own
  16.0 5.1 %collective-permute-start.5 = (f32[12,5,8,128]{3,2,1,0:T(8,128)S(1)}, f32[12,5,8,128]{3,2,1,0:T(8,128)S(1)}, u32[]{:S(2)}, u32[]{:S(2)}) collective-permute-start(f32[12,5,8,128]{3,2,1,0:T(8,128)S(1)} %pad_maximum_fusion.own), channel_id=1, source_target_pairs={{3,0},{4,1},{5,2},{6,3},{7,4},{8,5},{9,6},{10,7},{11,8},{12,9},{13... | collective-permute-start | bytes 737288 | tf_op jit(solution)/shard_map/ppermute | solution.py:430
  21.1 2.7 %collective-permute-start.4 = (f32[12,5,8,128]{3,2,1,0:T(8,128)S(1)}, f32[12,5,8,128]{3,2,1,0:T(8,128)S(1)}, u32[]{:S(2)}, u32[]{:S(2)}) collective-permute-start(f32[12,5,8,128]{3,2,1,0:T(8,128)S(1)} %pad_maximum_fusion.own), channel_id=1, source_target_pairs={{2,0},{3,1},{4,2},{5,3},{6,4},{7,5},{8,6},{9,7},{10,8},{11,9},{12,... | collective-permute-start | bytes 737288 | tf_op jit(solution)/shard_map/ppermute | solution.py:430
  23.9 1.3 %collective-permute-start.3 = (f32[12,5,8,128]{3,2,1,0:T(8,128)S(1)}, f32[12,5,8,128]{3,2,1,0:T(8,128)S(1)}, u32[]{:S(2)}, u32[]{:S(2)}) collective-permute-start(f32[12,5,8,128]{3,2,1,0:T(8,128)S(1)} %pad_maximum_fusion.own), channel_id=1, source_target_pairs={{1,0},{2,1},{3,2},{4,3},{5,4},{6,5},{7,6},{8,7},{9,8},{10,9},{11,1... | collective-permute-start | bytes 737288 | tf_op jit(solution)/shard_map/ppermute | solution.py:430
  25.2 2.2 %collective-permute-done.5.a3 = f32[12,5,8,128]{3,2,1,0:T(8,128)S(1)} collective-permute-done((f32[12,5,8,128]{3,2,1,0:T(8,128)S(1)}, f32[12,5,8,128]{3,2,1,0:T(8,128)S(1)}, u32[]{:S(2)}, u32[]{:S(2)}) %collective-permute-start.5) | collective-permute-done | bytes 245792 | tf_op jit(solution)/shard_map/ppermute | solution.py:430
  27.5 0.0 collective-permute-start.8
  27.5 6.9 %collective-permute-done.4.a2 = f32[12,5,8,128]{3,2,1,0:T(8,128)S(1)} collective-permute-done((f32[12,5,8,128]{3,2,1,0:T(8,128)S(1)}, f32[12,5,8,128]{3,2,1,0:T(8,128)S(1)}, u32[]{:S(2)}, u32[]{:S(2)}) %collective-permute-start.4) | collective-permute-done | bytes 245792 | tf_op jit(solution)/shard_map/ppermute | solution.py:430
  34.4 0.0 collective-permute-start.7
  34.4 0.0 collective-permute-done.3.a1
  34.4 0.5 collective-permute-start.6
  34.9 0.0 collective-permute-done.8.b3
  34.9 1.0 collective-permute-done.7.b2
  35.9 0.4 collective-permute-done.6.b1
  36.2 51.0 %region.1 = (f32[6,31,8,128]{3,2,1,0:T(8,128)S(1)}, f32[16,128]{1,0:T(8,128)S(1)}) custom-call(f32[12,5,8,128]{3,2,1,0:T(8,128)S(1)} %pad_maximum_fusion.own, f32[12,5,8,128]{3,2,1,0:T(8,128)S(1)} %collective-permute-done.3.a1, f32[12,5,8,128]{3,2,1,0:T(8,128)S(1)} %collective-permute-done.4.a2, f32[12,5,8,128]{3,2,1,0:T(8,128)S(1)} %collective-permute-done.5.a3, ...), custom_call_target="tpu_custom_call" | custom-call | tf_op jit(solution)/shard_map/region/pallas_call | solution.py:436
  87.2 7.8 %psum.14 = f32[16,128]{1,0:T(8,128)S(1)} all-reduce(f32[16,128]{1,0:T(8,128)S(1)} %get-tuple-element.9), channel_id=1, replica_groups=mesh['gx'=2,'gy'=4,'gz_0'=4,'gz_1'=4] {'gz_1'}, use_global_device_ids=true, to_apply=%region_0.0 | all-reduce | flops 2048 | bytes 16384 | tf_op jit(solution)/shard_map/psum | solution.py:453
  95.1 10.7 %psum.15.info = f32[16,128]{1,0:T(8,128)S(1)} all-reduce(f32[16,128]{1,0:T(8,128)S(1)} %psum.14), channel_id=1, replica_groups=mesh['gx'=2,'gy'=4,'gz_0'=4,'gz_1'=4] {'gz_0'}, use_global_device_ids=true, to_apply=%region_1.0 | all-reduce | flops 2048 | bytes 16384 | tf_op jit(solution)/shard_map/psum | solution.py:453
  105.8 2.5 %finish.1 = (f32[6,6,3,6]{3,2,1,0:T(4,128)}, f32[6,6,3,6]{3,2,1,0:T(4,128)}, f32[1,8]{1,0:T(1,128)}) custom-call(f32[6,31,8,128]{3,2,1,0:T(8,128)S(1)} %get-tuple-element.8.kept, f32[16,128]{1,0:T(8,128)S(1)} %psum.15.info), custom_call_target="tpu_custom_call" | custom-call | tf_op jit(solution)/shard_map/finish/pallas_call | solution.py:455
Async XLA Ops:
  7.3 5.8 %collective-permute-start.2 = (f32[12,5,2,128]{3,2,1,0:T(2,128)S(1)}, f32[12,5,2,128]{3,2,1,0:T(2,128)S(1)}, u32[]{:S(2)}, u32[]{:S(2)}) collective-permute-start(f32[12,5,2,128]{3,2,1,0:T(2,128)S(1)} %all_gather.3), channel_id=1, source_target_pairs={{48,0},{0,16},{16,32},{32,48},{49,1},{1,17},{17,33},{33,49},{50,2}... | collective-permute-start | bytes 184328 | tf_op jit(solution)/shard_map/ppermute | solution.py:423
  8.9 6.0 %collective-permute-start.1 = (f32[12,5,2,128]{3,2,1,0:T(2,128)S(1)}, f32[12,5,2,128]{3,2,1,0:T(2,128)S(1)}, u32[]{:S(2)}, u32[]{:S(2)}) collective-permute-start(f32[12,5,2,128]{3,2,1,0:T(2,128)S(1)} %all_gather.3), channel_id=1, source_target_pairs={{32,0},{48,16},{0,32},{16,48},{33,1},{49,17},{1,33},{17,49},{34,2}... | collective-permute-start | bytes 184328 | tf_op jit(solution)/shard_map/ppermute | solution.py:423
  11.7 4.2 %collective-permute-start = (f32[12,5,2,128]{3,2,1,0:T(2,128)S(1)}, f32[12,5,2,128]{3,2,1,0:T(2,128)S(1)}, u32[]{:S(2)}, u32[]{:S(2)}) collective-permute-start(f32[12,5,2,128]{3,2,1,0:T(2,128)S(1)} %all_gather.3), channel_id=1, source_target_pairs={{16,0},{32,16},{48,32},{0,48},{17,1},{33,17},{49,33},{1,49},{18,2}... | collective-permute-start | bytes 184328 | tf_op jit(solution)/shard_map/ppermute | solution.py:423
  16.0 11.4 %collective-permute-start.5 = (f32[12,5,8,128]{3,2,1,0:T(8,128)S(1)}, f32[12,5,8,128]{3,2,1,0:T(8,128)S(1)}, u32[]{:S(2)}, u32[]{:S(2)}) collective-permute-start(f32[12,5,8,128]{3,2,1,0:T(8,128)S(1)} %pad_maximum_fusion.own), channel_id=1, source_target_pairs={{3,0},{4,1},{5,2},{6,3},{7,4},{8,5},{9,6},{10,7},{11,8},{12,9},{13... | collective-permute-start | bytes 737288 | tf_op jit(solution)/shard_map/ppermute | solution.py:430
  21.1 13.3 %collective-permute-start.4 = (f32[12,5,8,128]{3,2,1,0:T(8,128)S(1)}, f32[12,5,8,128]{3,2,1,0:T(8,128)S(1)}, u32[]{:S(2)}, u32[]{:S(2)}) collective-permute-start(f32[12,5,8,128]{3,2,1,0:T(8,128)S(1)} %pad_maximum_fusion.own), channel_id=1, source_target_pairs={{2,0},{3,1},{4,2},{5,3},{6,4},{7,5},{8,6},{9,7},{10,8},{11,9},{12,... | collective-permute-start | bytes 737288 | tf_op jit(solution)/shard_map/ppermute | solution.py:430
  23.9 10.5 %collective-permute-start.3 = (f32[12,5,8,128]{3,2,1,0:T(8,128)S(1)}, f32[12,5,8,128]{3,2,1,0:T(8,128)S(1)}, u32[]{:S(2)}, u32[]{:S(2)}) collective-permute-start(f32[12,5,8,128]{3,2,1,0:T(8,128)S(1)} %pad_maximum_fusion.own), channel_id=1, source_target_pairs={{1,0},{2,1},{3,2},{4,3},{5,4},{6,5},{7,6},{8,7},{9,8},{10,9},{11,1... | collective-permute-start | bytes 737288 | tf_op jit(solution)/shard_map/ppermute | solution.py:430
  27.5 7.4 %collective-permute-start.8 = (f32[12,5,8,128]{3,2,1,0:T(8,128)S(1)}, f32[12,5,8,128]{3,2,1,0:T(8,128)S(1)}, u32[]{:S(2)}, u32[]{:S(2)}) collective-permute-start(f32[12,5,8,128]{3,2,1,0:T(8,128)S(1)} %collective-permute-done.5.a3), channel_id=1, source_target_pairs={{0,64},{64,0},{1,65},{65,1},{2,66},{66,2},{3,67},{67,3},{4,68},{68... | collective-permute-start | bytes 737288 | tf_op jit(solution)/shard_map/ppermute | solution.py:433
  34.4 1.5 %collective-permute-start.7 = (f32[12,5,8,128]{3,2,1,0:T(8,128)S(1)}, f32[12,5,8,128]{3,2,1,0:T(8,128)S(1)}, u32[]{:S(2)}, u32[]{:S(2)}) collective-permute-start(f32[12,5,8,128]{3,2,1,0:T(8,128)S(1)} %collective-permute-done.4.a2), channel_id=1, source_target_pairs={{0,64},{64,0},{1,65},{65,1},{2,66},{66,2},{3,67},{67,3},{4,68},{68... | collective-permute-start | bytes 737288 | tf_op jit(solution)/shard_map/ppermute | solution.py:433
  34.4 1.9 %collective-permute-start.6 = (f32[12,5,8,128]{3,2,1,0:T(8,128)S(1)}, f32[12,5,8,128]{3,2,1,0:T(8,128)S(1)}, u32[]{:S(2)}, u32[]{:S(2)}) collective-permute-start(f32[12,5,8,128]{3,2,1,0:T(8,128)S(1)} %collective-permute-done.3.a1), channel_id=1, source_target_pairs={{0,64},{64,0},{1,65},{65,1},{2,66},{66,2},{3,67},{67,3},{4,68},{68... | collective-permute-start | bytes 737288 | tf_op jit(solution)/shard_map/ppermute | solution.py:433

commit v3 on v2

--- a/solution.py
+++ b/solution.py
@@ -24,7 +24,6 @@
     if 1 <= a * a + b * b + c * c <= 5
 ]
 FORWARD = [d for d in OFFSETS if d > (0, 0, 0)]
-PLANES = sorted({d[1:] for d in OFFSETS})
 GROUPS, PER = 5, 7
 
 
@@ -156,11 +155,20 @@
                 jnp.where(is_low, a2[x, group], b2[x, group]),
                 jnp.where(is_low, a3[x, group], b3[x, group]),
             ]
-            blocks = [pltpu.roll(v, 2 * gy, 0) for v in blocks]
+            outs = [None] * PER
+            for gap in range(-6, 7):
+                members = [m for m in range(PER) if 0 <= m + gap < PER]
+                mixed = blocks[members[0] + gap]
+                for m in members[1:]:
+                    mixed = jnp.where(along >= 6 * m, blocks[m + gap], mixed)
+                mixed = roll_lanes(mixed, -6 * gap)
+                for m in members:
+                    outs[m] = (
+                        mixed if outs[m] is None
+                        else jnp.where(along >= 6 * (m + gap), mixed, outs[m])
+                    )
             for member in range(PER):
-                acc = roll_lanes(blocks[0], 6 * member)
-                for k in range(1, 7):
-                    acc = jnp.where(along >= 6 * k, roll_lanes(blocks[k], 6 * (member - k)), acc)
+                acc = pltpu.roll(outs[member], 2 * gy, 0)
                 if group * PER + member == 3:
                     acc = jnp.where(lane >= 3 * WIDE, 1.0, acc)
                     chan[x, 35] = 1.0 / acc
@@ -172,18 +180,18 @@
     def spread(x, carry):
         for c in range(4):
             v = chan[x, 3 + c]
-            for number, (dy, dz) in enumerate(PLANES):
-                near[x, number * 4 + c] = shifted(v, dy, dz, first, last)
+            for dy in range(-2, 3):
+                near[x, (dy + 2) * 4 + c] = shifted(v, dy, 0, first, last)
         return carry
 
     unrolled(NX, 3, spread, 0)
 
     def pairs(x, carry):
-        polar = chan[x, 3]
-        jit = [chan[x, 4 + c] for c in range(3)]
+        home = {dz: [roll_lanes(chan[x, 3 + c], -dz) for c in range(4)] for dz in range(-2, 3)}
         for number, d in enumerate(FORWARD):
             other = wrap(x + d[0])
-            place = PLANES.index(d[1:]) * 4
+            place = (d[1] + 2) * 4
+            polar, *jit = home[d[2]]
             sep = [((near[other, place + 1 + c] - jit[c]) + float(d[c])) * SPACING for c in range(3)]
             dist_sq = sep[0] * sep[0] + sep[1] * sep[1] + sep[2] * sep[2]
             over = lax.rsqrt(dist_sq)
@@ -195,34 +203,40 @@
             iso = (1.0 - falloff) * over_cube
             radial = 3.0 * (1.0 - (1.0 + damping) * falloff) * over_cube * over_sq
             root = jnp.sqrt(radial)
-            here = chan[x, 7 + number] > 0.5
+            here = roll_lanes(chan[x, 7 + number], -d[2]) > 0.5
             values = [jnp.where(here, s * root, 0.0) for s in sep] + [jnp.where(here, iso, 0.0)]
             ahead = OFFSETS.index(d) * 4
             behind = OFFSETS.index((-d[0], -d[1], -d[2])) * 4
             for c in range(4):
                 coef[x, ahead + c] = values[c]
-                coef[other, behind + c] = shifted(values[c], -d[1], -d[2], first, last)
+                coef[other, behind + c] = shifted(values[c], -d[1], d[2], first, last)
         return carry
 
     lax.fori_loop(0, NX, pairs, 0)
 
     def move(x, c, v):
-        by_y = {dy: shifted(v, dy, 0, first, last) for dy in range(-2, 3)}
-        for number, (dy, dz) in enumerate(PLANES):
-            moved[x, number * 3 + c] = roll_lanes(by_y[dy], dz)
+        for dy in range(-2, 3):
+            moved[x, (dy + 2) * 3 + c] = shifted(v, dy, 0, first, last)
 
     def couple(x):
-        acc = [jnp.zeros((8, 128), F32) for _ in range(3)]
-        for number, d in enumerate(OFFSETS):
-            other = wrap(x + d[0])
-            place = PLANES.index(d[1:]) * 3
-            v = [moved[other, place + c] for c in range(3)]
-            s = [coef[x, number * 4 + c] for c in range(3)]
-            iso = coef[x, number * 4 + 3]
-            dot = s[0] * v[0] + s[1] * v[1] + s[2] * v[2]
-            acc = [acc[c] + (s[c] * dot - iso * v[c]) for c in range(3)]
+        total_of = [None] * 3
+        for dz in (0, 1, -1, 2, -2):
+            acc = [None] * 3
+            for number, d in enumerate(OFFSETS):
+                if d[2] != dz:
+                    continue
+                other = wrap(x + d[0])
+                place = (d[1] + 2) * 3
+                v = [moved[other, place + c] for c in range(3)]
+                s = [coef[x, number * 4 + c] for c in range(3)]
+                iso = coef[x, number * 4 + 3]
+                dot = s[0] * v[0] + s[1] * v[1] + s[2] * v[2]
+                new = [s[c] * dot - iso * v[c] for c in range(3)]
+                acc = [new[c] if acc[c] is None else acc[c] + new[c] for c in range(3)]
+            acc = [roll_lanes(t, dz) for t in acc]
+            total_of = [acc[c] if total_of[c] is None else total_of[c] + acc[c] for c in range(3)]
         polar = chan[x, 3]
-        return [polar * t for t in acc]
+        return [polar * t for t in total_of]
 
     zero = jnp.zeros((8, 128), F32)
     mine = (along >= 18) & (along < 24)
@@ -327,7 +341,7 @@
         far = x + EDGE * gx
 
         def front(v):
-            return pltpu.roll(roll_lanes(v, 18), 8 - 2 * gy, 0)
+            return pltpu.roll(v, 8 - 2 * gy, 0)
 
         for c in range(3):
             for k in range(BASIS):
@@ -406,7 +420,7 @@
             res = res * kept[x, 30]
             for out, v in ((dip_out, dip), (res_out, res)):
                 for t in range(3):
-                    w = roll_lanes(v, t * WIDE)
+                    w = roll_lanes(v, t * WIDE + 18)
                     for s in range(2):
                         out[x, 3 * s + t, c : c + 1, :] = w[s : s + 1, :EDGE]
 
@@ -441,9 +455,9 @@
         ),
         scratch_shapes=[
             pltpu.VMEM((NX, 36) + vreg, F32),
-            pltpu.VMEM((NX, 4 * len(PLANES)) + vreg, F32),
+            pltpu.VMEM((NX, 20) + vreg, F32),
             pltpu.VMEM((NX, 4 * len(OFFSETS)) + vreg, F32),
-            pltpu.VMEM((NX, 64) + vreg, F32),
+            pltpu.VMEM((NX, 16) + vreg, F32),
             pltpu.VMEM((BASIS + 1, 3 * NX) + vreg, F32),
         ],
         compiler_params=pltpu.CompilerParams(vmem_limit_bytes=36 * 1024 * 1024),

time: 108 us -> 87.4 us (0.81)
  Pallas kernels: 58 us -> 37 us
    pallas_call x1, Pallas kernels: 51 us -> 29.9 us  [per_device(): pl.pallas_call(region_kernel, out_shape=(jax.ShapeDtypeStruct((EDGE, 31)...]
where the time goes in v3:
time: 87.4 us; the launch traced here: 87.3 us
  Pallas kernels  37 us (42%)
  blocking collectives  20.6 us (24%)
  starting transfers between devices  15.6 us (18%)
  waiting for transfers between devices  13.3 us (15%)
    pallas_call x1, Pallas kernels, per_device(): pl.pallas_call(region_kernel, out_shape=(jax.ShapeDtypeStruct((EDGE, 31)...  29.9 us
    psum x2, blocking collectives, per_device(): info = lax.psum(lax.psum(info, 'gz_1'), 'gz_0')  18.6 us
    ppermute x3, starting transfers between devices, fetch(): return lax.ppermute(own, ('gx',) + GZ, pairs)  9.21 us
    ppermute x3, waiting for transfers between devices, fetch(): return lax.ppermute(own, ('gx',) + GZ, pairs)  9.16 us
    ppermute x3, starting transfers between devices, per_device(): lax.ppermute(both, 'gy', [((i + k) % 4, i) for i in range(4)])  5.84 us
    pallas_call x1, Pallas kernels, per_device(): pl.pallas_call(pack_kernel, out_shape=jax.ShapeDtypeStruct((EDGE, GROUPS,...  4.58 us
    ppermute x3, waiting for transfers between devices, per_device(): lax.ppermute(both, 'gy', [((i + k) % 4, i) for i in range(4)])  2.79 us
    pallas_call x1, Pallas kernels, per_device(): pl.pallas_call(finish_kernel, out_shape=(jax.ShapeDtypeStruct((EDGE, EDGE...  2.49 us
  transfers between devices with their start and end apart: 9, of which 6 were waited for; matrix products, arithmetic and copies ran while one was open for 0% of the time, Pallas kernels for 0%

profile of v3, /device:TPU:0, one launch (start us, length us, event | category | flops | bytes accessed | tf_op | source)
XLA Modules:
  0.0 87.3 jit_solution(17858530198463375972)
XLA Ops:
  0.6 4.6 %pack.1 = f32[6,5,2,128]{3,2,1,0:T(2,128)} custom-call(f32[6,6,3,6]{3,2,1,0:T(4,128)} %bitcast.5, f32[6,6,6]{2,1,0:T(8,128)} %polar.1, f32[6,6,3,6]{3,2,1,0:T(4,128)} %bitcast.6, s32[6,6,6,56]{3,2,1,0:T(8,128)} %neighbors.1), custom_call_target="tpu_custom_call" | custom-call | tf_op jit(solution)/shard_map/pack/pallas_call | solution.py:429
  5.2 2.1 %all_gather.3 = f32[12,5,2,128]{3,2,1,0:T(2,128)S(1)} all-gather(f32[6,5,2,128]{3,2,1,0:T(2,128)} %pack.1), channel_id=1, replica_groups=mesh['gx'=2,'gy'=4,'gz_0'=4,'gz_1'=4] {'gx'}, dimensions={0}, use_global_device_ids=true | all-gather | bytes 92160 | tf_op jit(solution)/shard_map/all_gather | solution.py:435
  7.3 1.7 %collective-permute-start.2 = (f32[12,5,2,128]{3,2,1,0:T(2,128)S(1)}, f32[12,5,2,128]{3,2,1,0:T(2,128)S(1)}, u32[]{:S(2)}, u32[]{:S(2)}) collective-permute-start(f32[12,5,2,128]{3,2,1,0:T(2,128)S(1)} %all_gather.3), channel_id=1, source_target_pairs={{48,0},{0,16},{16,32},{32,48},{49,1},{1,17},{17,33},{33,49},{50,2}... | collective-permute-start | bytes 184328 | tf_op jit(solution)/shard_map/ppermute | solution.py:437
  8.9 2.7 %collective-permute-start.1 = (f32[12,5,2,128]{3,2,1,0:T(2,128)S(1)}, f32[12,5,2,128]{3,2,1,0:T(2,128)S(1)}, u32[]{:S(2)}, u32[]{:S(2)}) collective-permute-start(f32[12,5,2,128]{3,2,1,0:T(2,128)S(1)} %all_gather.3), channel_id=1, source_target_pairs={{32,0},{48,16},{0,32},{16,48},{33,1},{49,17},{1,33},{17,49},{34,2}... | collective-permute-start | bytes 184328 | tf_op jit(solution)/shard_map/ppermute | solution.py:437
  11.7 1.4 %collective-permute-start = (f32[12,5,2,128]{3,2,1,0:T(2,128)S(1)}, f32[12,5,2,128]{3,2,1,0:T(2,128)S(1)}, u32[]{:S(2)}, u32[]{:S(2)}) collective-permute-start(f32[12,5,2,128]{3,2,1,0:T(2,128)S(1)} %all_gather.3), channel_id=1, source_target_pairs={{16,0},{32,16},{48,32},{0,48},{17,1},{33,17},{49,33},{1,49},{18,2}... | collective-permute-start | bytes 184328 | tf_op jit(solution)/shard_map/ppermute | solution.py:437
  13.1 0.0 collective-permute-done.2
  13.1 1.9 %collective-permute-done.1 = f32[12,5,2,128]{3,2,1,0:T(2,128)S(1)} collective-permute-done((f32[12,5,2,128]{3,2,1,0:T(2,128)S(1)}, f32[12,5,2,128]{3,2,1,0:T(2,128)S(1)}, u32[]{:S(2)}, u32[]{:S(2)}) %collective-permute-start.1) | collective-permute-done | bytes 61472 | tf_op jit(solution)/shard_map/ppermute | solution.py:437
  15.0 0.9 %collective-permute-done = f32[12,5,2,128]{3,2,1,0:T(2,128)S(1)} collective-permute-done((f32[12,5,2,128]{3,2,1,0:T(2,128)S(1)}, f32[12,5,2,128]{3,2,1,0:T(2,128)S(1)}, u32[]{:S(2)}, u32[]{:S(2)}) %collective-permute-start) | collective-permute-done | bytes 61472 | tf_op jit(solution)/shard_map/ppermute | solution.py:437
  15.9 0.1 pad_maximum_fusion.own
  16.0 5.1 %collective-permute-start.5 = (f32[12,5,8,128]{3,2,1,0:T(8,128)S(1)}, f32[12,5,8,128]{3,2,1,0:T(8,128)S(1)}, u32[]{:S(2)}, u32[]{:S(2)}) collective-permute-start(f32[12,5,8,128]{3,2,1,0:T(8,128)S(1)} %pad_maximum_fusion.own), channel_id=1, source_target_pairs={{3,0},{4,1},{5,2},{6,3},{7,4},{8,5},{9,6},{10,7},{11,8},{12,9},{13... | collective-permute-start | bytes 737288 | tf_op jit(solution)/shard_map/ppermute | solution.py:444
  21.1 2.7 %collective-permute-start.4 = (f32[12,5,8,128]{3,2,1,0:T(8,128)S(1)}, f32[12,5,8,128]{3,2,1,0:T(8,128)S(1)}, u32[]{:S(2)}, u32[]{:S(2)}) collective-permute-start(f32[12,5,8,128]{3,2,1,0:T(8,128)S(1)} %pad_maximum_fusion.own), channel_id=1, source_target_pairs={{2,0},{3,1},{4,2},{5,3},{6,4},{7,5},{8,6},{9,7},{10,8},{11,9},{12,... | collective-permute-start | bytes 737288 | tf_op jit(solution)/shard_map/ppermute | solution.py:444
  23.9 1.3 %collective-permute-start.3 = (f32[12,5,8,128]{3,2,1,0:T(8,128)S(1)}, f32[12,5,8,128]{3,2,1,0:T(8,128)S(1)}, u32[]{:S(2)}, u32[]{:S(2)}) collective-permute-start(f32[12,5,8,128]{3,2,1,0:T(8,128)S(1)} %pad_maximum_fusion.own), channel_id=1, source_target_pairs={{1,0},{2,1},{3,2},{4,3},{5,4},{6,5},{7,6},{8,7},{9,8},{10,9},{11,1... | collective-permute-start | bytes 737288 | tf_op jit(solution)/shard_map/ppermute | solution.py:444
  25.2 2.2 %collective-permute-done.5.a3 = f32[12,5,8,128]{3,2,1,0:T(8,128)S(1)} collective-permute-done((f32[12,5,8,128]{3,2,1,0:T(8,128)S(1)}, f32[12,5,8,128]{3,2,1,0:T(8,128)S(1)}, u32[]{:S(2)}, u32[]{:S(2)}) %collective-permute-start.5) | collective-permute-done | bytes 245792 | tf_op jit(solution)/shard_map/ppermute | solution.py:444
  27.5 0.0 collective-permute-start.8
  27.5 6.9 %collective-permute-done.4.a2 = f32[12,5,8,128]{3,2,1,0:T(8,128)S(1)} collective-permute-done((f32[12,5,8,128]{3,2,1,0:T(8,128)S(1)}, f32[12,5,8,128]{3,2,1,0:T(8,128)S(1)}, u32[]{:S(2)}, u32[]{:S(2)}) %collective-permute-start.4) | collective-permute-done | bytes 245792 | tf_op jit(solution)/shard_map/ppermute | solution.py:444
  34.4 0.0 collective-permute-start.7
  34.4 0.0 collective-permute-done.3.a1
  34.4 0.5 collective-permute-start.6
  34.9 0.0 collective-permute-done.8.b3
  34.9 1.0 %collective-permute-done.7.b2 = f32[12,5,8,128]{3,2,1,0:T(8,128)S(1)} collective-permute-done((f32[12,5,8,128]{3,2,1,0:T(8,128)S(1)}, f32[12,5,8,128]{3,2,1,0:T(8,128)S(1)}, u32[]{:S(2)}, u32[]{:S(2)}) %collective-permute-start.7) | collective-permute-done | bytes 245792 | tf_op jit(solution)/shard_map/ppermute | solution.py:447
  35.9 0.4 collective-permute-done.6.b1
  36.2 29.9 %region.1 = (f32[6,31,8,128]{3,2,1,0:T(8,128)S(1)}, f32[16,128]{1,0:T(8,128)S(1)}) custom-call(f32[12,5,8,128]{3,2,1,0:T(8,128)S(1)} %pad_maximum_fusion.own, f32[12,5,8,128]{3,2,1,0:T(8,128)S(1)} %collective-permute-done.3.a1, f32[12,5,8,128]{3,2,1,0:T(8,128)S(1)} %collective-permute-done.4.a2, f32[12,5,8,128]{3,2,1,0:T(8,128)S(1)} %collective-permute-done.5.a3, ...), custom_call_target="tpu_custom_call" | custom-call | tf_op jit(solution)/shard_map/region/pallas_call | solution.py:450
  66.2 7.8 %psum.14 = f32[16,128]{1,0:T(8,128)S(1)} all-reduce(f32[16,128]{1,0:T(8,128)S(1)} %get-tuple-element.9), channel_id=1, replica_groups=mesh['gx'=2,'gy'=4,'gz_0'=4,'gz_1'=4] {'gz_1'}, use_global_device_ids=true, to_apply=%region_0.0 | all-reduce | flops 2048 | bytes 16384 | tf_op jit(solution)/shard_map/psum | solution.py:467
  74.0 10.7 %psum.15.info = f32[16,128]{1,0:T(8,128)S(1)} all-reduce(f32[16,128]{1,0:T(8,128)S(1)} %psum.14), channel_id=1, replica_groups=mesh['gx'=2,'gy'=4,'gz_0'=4,'gz_1'=4] {'gz_0'}, use_global_device_ids=true, to_apply=%region_1.0 | all-reduce | flops 2048 | bytes 16384 | tf_op jit(solution)/shard_map/psum | solution.py:467
  84.8 2.5 %finish.1 = (f32[6,6,3,6]{3,2,1,0:T(4,128)}, f32[6,6,3,6]{3,2,1,0:T(4,128)}, f32[1,8]{1,0:T(1,128)}) custom-call(f32[6,31,8,128]{3,2,1,0:T(8,128)S(1)} %get-tuple-element.8.kept, f32[16,128]{1,0:T(8,128)S(1)} %psum.15.info), custom_call_target="tpu_custom_call" | custom-call | tf_op jit(solution)/shard_map/finish/pallas_call | solution.py:469
Async XLA Ops:
  7.3 5.8 %collective-permute-start.2 = (f32[12,5,2,128]{3,2,1,0:T(2,128)S(1)}, f32[12,5,2,128]{3,2,1,0:T(2,128)S(1)}, u32[]{:S(2)}, u32[]{:S(2)}) collective-permute-start(f32[12,5,2,128]{3,2,1,0:T(2,128)S(1)} %all_gather.3), channel_id=1, source_target_pairs={{48,0},{0,16},{16,32},{32,48},{49,1},{1,17},{17,33},{33,49},{50,2}... | collective-permute-start | bytes 184328 | tf_op jit(solution)/shard_map/ppermute | solution.py:437
  8.9 6.0 %collective-permute-start.1 = (f32[12,5,2,128]{3,2,1,0:T(2,128)S(1)}, f32[12,5,2,128]{3,2,1,0:T(2,128)S(1)}, u32[]{:S(2)}, u32[]{:S(2)}) collective-permute-start(f32[12,5,2,128]{3,2,1,0:T(2,128)S(1)} %all_gather.3), channel_id=1, source_target_pairs={{32,0},{48,16},{0,32},{16,48},{33,1},{49,17},{1,33},{17,49},{34,2}... | collective-permute-start | bytes 184328 | tf_op jit(solution)/shard_map/ppermute | solution.py:437
  11.7 4.2 %collective-permute-start = (f32[12,5,2,128]{3,2,1,0:T(2,128)S(1)}, f32[12,5,2,128]{3,2,1,0:T(2,128)S(1)}, u32[]{:S(2)}, u32[]{:S(2)}) collective-permute-start(f32[12,5,2,128]{3,2,1,0:T(2,128)S(1)} %all_gather.3), channel_id=1, source_target_pairs={{16,0},{32,16},{48,32},{0,48},{17,1},{33,17},{49,33},{1,49},{18,2}... | collective-permute-start | bytes 184328 | tf_op jit(solution)/shard_map/ppermute | solution.py:437
  16.0 11.4 %collective-permute-start.5 = (f32[12,5,8,128]{3,2,1,0:T(8,128)S(1)}, f32[12,5,8,128]{3,2,1,0:T(8,128)S(1)}, u32[]{:S(2)}, u32[]{:S(2)}) collective-permute-start(f32[12,5,8,128]{3,2,1,0:T(8,128)S(1)} %pad_maximum_fusion.own), channel_id=1, source_target_pairs={{3,0},{4,1},{5,2},{6,3},{7,4},{8,5},{9,6},{10,7},{11,8},{12,9},{13... | collective-permute-start | bytes 737288 | tf_op jit(solution)/shard_map/ppermute | solution.py:444
  21.1 13.3 %collective-permute-start.4 = (f32[12,5,8,128]{3,2,1,0:T(8,128)S(1)}, f32[12,5,8,128]{3,2,1,0:T(8,128)S(1)}, u32[]{:S(2)}, u32[]{:S(2)}) collective-permute-start(f32[12,5,8,128]{3,2,1,0:T(8,128)S(1)} %pad_maximum_fusion.own), channel_id=1, source_target_pairs={{2,0},{3,1},{4,2},{5,3},{6,4},{7,5},{8,6},{9,7},{10,8},{11,9},{12,... | collective-permute-start | bytes 737288 | tf_op jit(solution)/shard_map/ppermute | solution.py:444
  23.9 10.5 %collective-permute-start.3 = (f32[12,5,8,128]{3,2,1,0:T(8,128)S(1)}, f32[12,5,8,128]{3,2,1,0:T(8,128)S(1)}, u32[]{:S(2)}, u32[]{:S(2)}) collective-permute-start(f32[12,5,8,128]{3,2,1,0:T(8,128)S(1)} %pad_maximum_fusion.own), channel_id=1, source_target_pairs={{1,0},{2,1},{3,2},{4,3},{5,4},{6,5},{7,6},{8,7},{9,8},{10,9},{11,1... | collective-permute-start | bytes 737288 | tf_op jit(solution)/shard_map/ppermute | solution.py:444
  27.5 7.4 %collective-permute-start.8 = (f32[12,5,8,128]{3,2,1,0:T(8,128)S(1)}, f32[12,5,8,128]{3,2,1,0:T(8,128)S(1)}, u32[]{:S(2)}, u32[]{:S(2)}) collective-permute-start(f32[12,5,8,128]{3,2,1,0:T(8,128)S(1)} %collective-permute-done.5.a3), channel_id=1, source_target_pairs={{0,64},{64,0},{1,65},{65,1},{2,66},{66,2},{3,67},{67,3},{4,68},{68... | collective-permute-start | bytes 737288 | tf_op jit(solution)/shard_map/ppermute | solution.py:447
  34.4 1.5 %collective-permute-start.7 = (f32[12,5,8,128]{3,2,1,0:T(8,128)S(1)}, f32[12,5,8,128]{3,2,1,0:T(8,128)S(1)}, u32[]{:S(2)}, u32[]{:S(2)}) collective-permute-start(f32[12,5,8,128]{3,2,1,0:T(8,128)S(1)} %collective-permute-done.4.a2), channel_id=1, source_target_pairs={{0,64},{64,0},{1,65},{65,1},{2,66},{66,2},{3,67},{67,3},{4,68},{68... | collective-permute-start | bytes 737288 | tf_op jit(solution)/shard_map/ppermute | solution.py:447
  34.4 1.9 %collective-permute-start.6 = (f32[12,5,8,128]{3,2,1,0:T(8,128)S(1)}, f32[12,5,8,128]{3,2,1,0:T(8,128)S(1)}, u32[]{:S(2)}, u32[]{:S(2)}) collective-permute-start(f32[12,5,8,128]{3,2,1,0:T(8,128)S(1)} %collective-permute-done.3.a1), channel_id=1, source_target_pairs={{0,64},{64,0},{1,65},{65,1},{2,66},{66,2},{3,67},{67,3},{4,68},{68... | collective-permute-start | bytes 737288 | tf_op jit(solution)/shard_map/ppermute | solution.py:447

commit v4 on v3

--- a/solution.py
+++ b/solution.py
@@ -138,7 +138,6 @@
 ):
     gx = lax.axis_index("gx")
     gy = lax.axis_index("gy")
-    gz = lax.axis_index("gz_0") * 4 + lax.axis_index("gz_1")
     lane = lane_iota()
     first, last = third_masks()
     along = lane - jnp.where(last, 2 * WIDE, jnp.where(first, 0, WIDE))
@@ -168,7 +167,7 @@
                         else jnp.where(along >= 6 * (m + gap), mixed, outs[m])
                     )
             for member in range(PER):
-                acc = pltpu.roll(outs[member], 2 * gy, 0)
+                acc = outs[member]
                 if group * PER + member == 3:
                     acc = jnp.where(lane >= 3 * WIDE, 1.0, acc)
                     chan[x, 35] = 1.0 / acc
@@ -333,9 +332,8 @@
             info = jnp.where(lane == number, total(jnp.where(mine, sums[n], 0.0)), info)
             number += 1
 
-    row = lax.broadcasted_iota(jnp.int32, (8, 128), 0)
-    info_out[0:8, :] = jnp.where(row == gz, info, 0.0)
-    info_out[8:16, :] = jnp.where(row + 8 == gz, info, 0.0)
+    for e in range(16):
+        info_out[e] = info
 
     def keep(x, carry):
         far = x + EDGE * gx
@@ -355,7 +353,7 @@
 
 def finish_kernel(kept, info, dip_out, res_out, len_out, table):
     gz = lax.axis_index("gz_0") * 4 + lax.axis_index("gz_1")
-    wide = jnp.concatenate([info[...], jnp.zeros((112, 128), F32)], axis=0)
+    wide = jnp.concatenate([info[e, 0:1, :] for e in range(16)] + [jnp.zeros((112, 128), F32)], axis=0)
     table[...] = wide.T
     rows = {}
     number = 0
@@ -432,11 +430,10 @@
         name="pack",
     )(permanent_field.transpose(0, 1, 3, 2), polar, jitter.transpose(0, 1, 3, 2), neighbors)
 
-    both = lax.all_gather(packed, "gx", axis=0, tiled=True)
-    around = [both] + [
-        lax.ppermute(both, "gy", [((i + k) % 4, i) for i in range(4)]) for k in (1, 2, 3)
-    ]
-    own = jnp.concatenate(around, axis=2)
+    copies = jnp.broadcast_to(packed[None], (8,) + packed.shape)
+    plane = lax.all_to_all(copies, ("gx", "gy"), 0, 0, tiled=True)
+    plane = plane.reshape(2, 4, EDGE, GROUPS, 2, 128).transpose(0, 2, 3, 1, 4, 5)
+    own = plane.reshape(NX, GROUPS, 8, 128)
 
     def fetch(k):
         pairs = [((i + k) % 16, i) for i in range(16)]
@@ -451,7 +448,7 @@
         region_kernel,
         out_shape=(
             jax.ShapeDtypeStruct((EDGE, 31) + vreg, F32),
-            jax.ShapeDtypeStruct((16, 128), F32),
+            jax.ShapeDtypeStruct((16,) + vreg, F32),
         ),
         scratch_shapes=[
             pltpu.VMEM((NX, 36) + vreg, F32),
@@ -464,7 +461,7 @@
         name="region",
     )(own, *direct, *passed)
 
-    info = lax.psum(lax.psum(info, "gz_1"), "gz_0")
+    info = lax.all_to_all(info, GZ, 0, 0, tiled=True)
 
     dip, res, lengths = pl.pallas_call(
         finish_kernel,

time: 87.4 us -> 82.7 us (0.946)
  starting transfers between devices: 15.6 us -> 9.72 us
  blocking collectives: 20.6 us -> 23 us
  waiting for transfers between devices: 13.3 us -> 11.1 us
  local copies, waits for them, and re-layouts: 0 us -> 0.96 us
    all_to_all x0 -> x2, blocking collectives: none -> 23 us  [the longest x1 12.1 us: per_device(): info = lax.all_to_all(info, GZ, 0, 0, tiled=True)]
    psum x2 -> x0, blocking collectives: 18.6 us -> none  [per_device(): info = lax.psum(lax.psum(info, 'gz_1'), 'gz_0')]
    ppermute x3 -> x0, starting transfers between devices: 5.84 us -> none  [per_device(): lax.ppermute(both, 'gy', [((i + k) % 4, i) for i in range(4)])]
    ppermute x3 -> x0, waiting for transfers between devices: 2.79 us -> none  [per_device(): lax.ppermute(both, 'gy', [((i + k) % 4, i) for i in range(4)])]
    all_gather x1 -> x0, blocking collectives: 2.05 us -> none  [per_device(): both = lax.all_gather(packed, 'gx', axis=0, tiled=True)]
  transfers between devices with their start and end apart: 9 -> 6, of which waited for: 6 -> 4; matrix products, arithmetic and copies ran while one was open for 0% -> 0% of each run, Pallas kernels for 0% -> 0%
where the time goes in v4:
time: 82.7 us; the launch traced here: 82.4 us
  Pallas kernels  37 us (45%)
  blocking collectives  23 us (28%)
  waiting for transfers between devices  11.1 us (13%)
  starting transfers between devices  9.72 us (12%)
  local copies, waits for them, and re-layouts  0.96 us (1%)
    pallas_call x1, Pallas kernels, per_device(): pl.pallas_call(region_kernel, out_shape=(jax.ShapeDtypeStruct((EDGE, 31)...  29.9 us
    all_to_all x1, blocking collectives, per_device(): info = lax.all_to_all(info, GZ, 0, 0, tiled=True)  12.1 us
    all_to_all x1, blocking collectives, per_device(): plane = lax.all_to_all(copies, ('gx', 'gy'), 0, 0, tiled=True)  10.8 us
    ppermute x3, waiting for transfers between devices, fetch(): return lax.ppermute(own, ('gx',) + GZ, pairs)  9.78 us
    ppermute x3, starting transfers between devices, fetch(): return lax.ppermute(own, ('gx',) + GZ, pairs)  9.21 us
    pallas_call x1, Pallas kernels, per_device(): pl.pallas_call(pack_kernel, out_shape=jax.ShapeDtypeStruct((EDGE, GROUPS,...  4.58 us
    pallas_call x1, Pallas kernels, per_device(): pl.pallas_call(finish_kernel, out_shape=(jax.ShapeDtypeStruct((EDGE, EDGE...  2.5 us
  transfers between devices with their start and end apart: 6, of which 4 were waited for; matrix products, arithmetic and copies ran while one was open for 0% of the time, Pallas kernels for 0%

profile of v4, /device:TPU:0, one launch (start us, length us, event | category | flops | bytes accessed | tf_op | source)
XLA Modules:
  0.0 82.4 jit_solution(193034861967816026)
XLA Ops:
  0.6 4.6 %pack.1 = f32[6,5,2,128]{3,2,1,0:T(2,128)} custom-call(f32[6,6,3,6]{3,2,1,0:T(4,128)} %bitcast.14, f32[6,6,6]{2,1,0:T(8,128)} %polar.1, f32[6,6,3,6]{3,2,1,0:T(4,128)} %bitcast.15, s32[6,6,6,56]{3,2,1,0:T(8,128)} %neighbors.1), custom_call_target="tpu_custom_call" | custom-call | tf_op jit(solution)/shard_map/pack/pallas_call | solution.py:427
  5.2 0.8 broadcast_in_dim.2
  6.0 10.8 %all_to_all.10 = f32[8,6,5,2,128]{4,3,2,1,0:T(2,128)S(1)} all-to-all(f32[8,6,5,2,128]{4,3,2,1,0:T(2,128)S(1)} %broadcast_in_dim.2), channel_id=1, replica_groups=mesh['gx'=2,'gy'=4,'gz_0'=4,'gz_1'=4] {'gx','gy'}, dimensions={0} | all-to-all | bytes 491520 | tf_op jit(solution)/shard_map/all_to_all | solution.py:434
  16.9 0.1 copy.9
  17.0 5.1 %collective-permute-start.2 = (f32[12,5,8,128]{3,2,1,0:T(8,128)S(1)}, f32[12,5,8,128]{3,2,1,0:T(8,128)S(1)}, u32[]{:S(2)}, u32[]{:S(2)}) collective-permute-start(f32[12,5,8,128]{3,2,1,0:T(8,128)S(1)} %bitcast.9), channel_id=1, source_target_pairs={{3,0},{4,1},{5,2},{6,3},{7,4},{8,5},{9,6},{10,7},{11,8},{12,9},{13... | collective-permute-start | bytes 737288 | tf_op jit(solution)/shard_map/ppermute | solution.py:441
  22.1 2.7 %collective-permute-start.1 = (f32[12,5,8,128]{3,2,1,0:T(8,128)S(1)}, f32[12,5,8,128]{3,2,1,0:T(8,128)S(1)}, u32[]{:S(2)}, u32[]{:S(2)}) collective-permute-start(f32[12,5,8,128]{3,2,1,0:T(8,128)S(1)} %bitcast.10), channel_id=1, source_target_pairs={{2,0},{3,1},{4,2},{5,3},{6,4},{7,5},{8,6},{9,7},{10,8},{11,9},{12,... | collective-permute-start | bytes 737288 | tf_op jit(solution)/shard_map/ppermute | solution.py:441
  24.9 1.3 %collective-permute-start = (f32[12,5,8,128]{3,2,1,0:T(8,128)S(1)}, f32[12,5,8,128]{3,2,1,0:T(8,128)S(1)}, u32[]{:S(2)}, u32[]{:S(2)}) collective-permute-start(f32[12,5,8,128]{3,2,1,0:T(8,128)S(1)} %bitcast.11), channel_id=1, source_target_pairs={{1,0},{2,1},{3,2},{4,3},{5,4},{6,5},{7,6},{8,7},{9,8},{10,9},{11,1... | collective-permute-start | bytes 737288 | tf_op jit(solution)/shard_map/ppermute | solution.py:441
  26.2 2.2 %collective-permute-done.2.a3 = f32[12,5,8,128]{3,2,1,0:T(8,128)S(1)} collective-permute-done((f32[12,5,8,128]{3,2,1,0:T(8,128)S(1)}, f32[12,5,8,128]{3,2,1,0:T(8,128)S(1)}, u32[]{:S(2)}, u32[]{:S(2)}) %collective-permute-start.2) | collective-permute-done | bytes 245792 | tf_op jit(solution)/shard_map/ppermute | solution.py:441
  28.4 0.0 collective-permute-start.5
  28.4 7.5 %collective-permute-done.1.a2 = f32[12,5,8,128]{3,2,1,0:T(8,128)S(1)} collective-permute-done((f32[12,5,8,128]{3,2,1,0:T(8,128)S(1)}, f32[12,5,8,128]{3,2,1,0:T(8,128)S(1)}, u32[]{:S(2)}, u32[]{:S(2)}) %collective-permute-start.1) | collective-permute-done | bytes 245792 | tf_op jit(solution)/shard_map/ppermute | solution.py:441
  36.0 0.0 collective-permute-start.4
  36.0 0.0 collective-permute-done.a1
  36.0 0.5 collective-permute-start.3
  36.5 0.0 collective-permute-done.5.b3
  36.5 1.0 %collective-permute-done.4.b2 = f32[12,5,8,128]{3,2,1,0:T(8,128)S(1)} collective-permute-done((f32[12,5,8,128]{3,2,1,0:T(8,128)S(1)}, f32[12,5,8,128]{3,2,1,0:T(8,128)S(1)}, u32[]{:S(2)}, u32[]{:S(2)}) %collective-permute-start.4) | collective-permute-done | bytes 245792 | tf_op jit(solution)/shard_map/ppermute | solution.py:444
  37.5 0.4 collective-permute-done.3.b1
  37.9 29.9 %region.1 = (f32[6,31,8,128]{3,2,1,0:T(8,128)S(1)}, f32[16,8,128]{2,1,0:T(8,128)S(1)}) custom-call(f32[12,5,8,128]{3,2,1,0:T(8,128)S(1)} %bitcast.12, f32[12,5,8,128]{3,2,1,0:T(8,128)S(1)} %collective-permute-done.a1, f32[12,5,8,128]{3,2,1,0:T(8,128)S(1)} %collective-permute-done.1.a2, f32[12,5,8,128]{3,2,1,0:T(8,128)S(1)} %collective-permute-done.2.a3, ...), custom_call_target="tpu_custom_call" | custom-call | tf_op jit(solution)/shard_map/region/pallas_call | solution.py:447
  67.8 12.1 %all_to_all.11.info = f32[16,8,128]{2,1,0:T(8,128)S(1)} all-to-all(f32[16,8,128]{2,1,0:T(8,128)S(1)} %get-tuple-element.9), channel_id=1, replica_groups=mesh['gx'=2,'gy'=4,'gz_0'=4,'gz_1'=4] {'gz_0','gz_1'}, dimensions={0} | all-to-all | bytes 131072 | tf_op jit(solution)/shard_map/all_to_all | solution.py:464
  79.9 2.5 %finish.1 = (f32[6,6,3,6]{3,2,1,0:T(4,128)}, f32[6,6,3,6]{3,2,1,0:T(4,128)}, f32[1,8]{1,0:T(1,128)}) custom-call(f32[6,31,8,128]{3,2,1,0:T(8,128)S(1)} %get-tuple-element.8.kept, f32[16,8,128]{2,1,0:T(8,128)S(1)} %all_to_all.11.info), custom_call_target="tpu_custom_call" | custom-call | tf_op jit(solution)/shard_map/finish/pallas_call | solution.py:466
  (1 shorter events, 0.0 us)
Async XLA Ops:
  17.0 11.4 %collective-permute-start.2 = (f32[12,5,8,128]{3,2,1,0:T(8,128)S(1)}, f32[12,5,8,128]{3,2,1,0:T(8,128)S(1)}, u32[]{:S(2)}, u32[]{:S(2)}) collective-permute-start(f32[12,5,8,128]{3,2,1,0:T(8,128)S(1)} %bitcast.9), channel_id=1, source_target_pairs={{3,0},{4,1},{5,2},{6,3},{7,4},{8,5},{9,6},{10,7},{11,8},{12,9},{13... | collective-permute-start | bytes 737288 | tf_op jit(solution)/shard_map/ppermute | solution.py:441
  22.1 13.9 %collective-permute-start.1 = (f32[12,5,8,128]{3,2,1,0:T(8,128)S(1)}, f32[12,5,8,128]{3,2,1,0:T(8,128)S(1)}, u32[]{:S(2)}, u32[]{:S(2)}) collective-permute-start(f32[12,5,8,128]{3,2,1,0:T(8,128)S(1)} %bitcast.10), channel_id=1, source_target_pairs={{2,0},{3,1},{4,2},{5,3},{6,4},{7,5},{8,6},{9,7},{10,8},{11,9},{12,... | collective-permute-start | bytes 737288 | tf_op jit(solution)/shard_map/ppermute | solution.py:441
  24.9 11.1 %collective-permute-start = (f32[12,5,8,128]{3,2,1,0:T(8,128)S(1)}, f32[12,5,8,128]{3,2,1,0:T(8,128)S(1)}, u32[]{:S(2)}, u32[]{:S(2)}) collective-permute-start(f32[12,5,8,128]{3,2,1,0:T(8,128)S(1)} %bitcast.11), channel_id=1, source_target_pairs={{1,0},{2,1},{3,2},{4,3},{5,4},{6,5},{7,6},{8,7},{9,8},{10,9},{11,1... | collective-permute-start | bytes 737288 | tf_op jit(solution)/shard_map/ppermute | solution.py:441
  28.4 8.1 %collective-permute-start.5 = (f32[12,5,8,128]{3,2,1,0:T(8,128)S(1)}, f32[12,5,8,128]{3,2,1,0:T(8,128)S(1)}, u32[]{:S(2)}, u32[]{:S(2)}) collective-permute-start(f32[12,5,8,128]{3,2,1,0:T(8,128)S(1)} %collective-permute-done.2.a3), channel_id=1, source_target_pairs={{0,64},{64,0},{1,65},{65,1},{2,66},{66,2},{3,67},{67,3},{4,68},{68... | collective-permute-start | bytes 737288 | tf_op jit(solution)/shard_map/ppermute | solution.py:444
  36.0 1.5 %collective-permute-start.4 = (f32[12,5,8,128]{3,2,1,0:T(8,128)S(1)}, f32[12,5,8,128]{3,2,1,0:T(8,128)S(1)}, u32[]{:S(2)}, u32[]{:S(2)}) collective-permute-start(f32[12,5,8,128]{3,2,1,0:T(8,128)S(1)} %collective-permute-done.1.a2), channel_id=1, source_target_pairs={{0,64},{64,0},{1,65},{65,1},{2,66},{66,2},{3,67},{67,3},{4,68},{68... | collective-permute-start | bytes 737288 | tf_op jit(solution)/shard_map/ppermute | solution.py:444
  36.0 1.9 %collective-permute-start.3 = (f32[12,5,8,128]{3,2,1,0:T(8,128)S(1)}, f32[12,5,8,128]{3,2,1,0:T(8,128)S(1)}, u32[]{:S(2)}, u32[]{:S(2)}) collective-permute-start(f32[12,5,8,128]{3,2,1,0:T(8,128)S(1)} %collective-permute-done.a1), channel_id=1, source_target_pairs={{0,64},{64,0},{1,65},{65,1},{2,66},{66,2},{3,67},{67,3},{4,68},{68... | collective-permute-start | bytes 737288 | tf_op jit(solution)/shard_map/ppermute | solution.py:444

commit v5 on v4

--- a/solution.py
+++ b/solution.py
@@ -102,7 +102,7 @@
         hit = column * 0 > 0
         for n in range(PER):
             hit = hit | (column == row + (t * WIDE + n * EDGE))
-        pick.append(jnp.where(hit, 1.0, 0.0))
+        pick.append((jnp.where(hit, 32.0, 0.0).astype(jnp.bfloat16), jnp.where(hit, 1.0, 0.0).astype(jnp.bfloat16)))
 
     def one(x, carry):
         for s in range(2):
@@ -110,10 +110,14 @@
             values = jnp.zeros((1, 128), F32)
             for t in range(3):
                 y = 3 * s + t
-                slots = slots + lax.dot_general(
-                    neighbors[x, y].astype(F32), pick[t], (((0,), (0,)), ((), ())),
-                    precision=lax.Precision.HIGHEST, preferred_element_type=F32,
-                )
+                entry = neighbors[x, y]
+                high = lax.shift_right_arithmetic(entry, 5)
+                low = entry & 31
+                for part, chosen in zip((high, low), pick[t]):
+                    slots = slots + lax.dot_general(
+                        part.astype(F32).astype(jnp.bfloat16), chosen, (((0,), (0,)), ((), ())),
+                        preferred_element_type=F32,
+                    )
                 parts = [field[x, y, c : c + 1, :] for c in range(3)]
                 parts += [polar[x, y : y + 1, :]]
                 parts += [jitter[x, y, c : c + 1, :] for c in range(3)]
@@ -129,31 +133,25 @@
                 out[x, group, s : s + 1, :] = flag
         return carry
 
-    lax.fori_loop(0, EDGE, one, 0)
-
-
-def region_kernel(
-    own, a1, a2, a3, b1, b2, b3, kept_out, info_out,
-    chan, near, coef, moved, basis,
-):
+    unrolled(EDGE, 2, one, 0)
+
+
+def region_kernel(*refs):
+    mine, theirs = refs[:7], refs[7:14]
+    kept_out, info_out, chan, near, coef, moved, basis = refs[14:]
     gx = lax.axis_index("gx")
     gy = lax.axis_index("gy")
     lane = lane_iota()
     first, last = third_masks()
     along = lane - jnp.where(last, 2 * WIDE, jnp.where(first, 0, WIDE))
-    is_low = (lane * 0 + gx) == 0
-
-    def gather(x, carry):
+
+    def gather(step, carry):
+        half = step // EDGE
+        at = step - half * EDGE
+        x = step
+        is_mine = (lane * 0 + gx) == half
         for group in range(GROUPS):
-            blocks = [
-                jnp.where(is_low, b3[x, group], a3[x, group]),
-                jnp.where(is_low, b2[x, group], a2[x, group]),
-                jnp.where(is_low, b1[x, group], a1[x, group]),
-                own[x, group],
-                jnp.where(is_low, a1[x, group], b1[x, group]),
-                jnp.where(is_low, a2[x, group], b2[x, group]),
-                jnp.where(is_low, a3[x, group], b3[x, group]),
-            ]
+            blocks = [jnp.where(is_mine, m[at, group], t[at, group]) for m, t in zip(mine, theirs)]
             outs = [None] * PER
             for gap in range(-6, 7):
                 members = [m for m in range(PER) if 0 <= m + gap < PER]
@@ -167,7 +165,7 @@
                         else jnp.where(along >= 6 * (m + gap), mixed, outs[m])
                     )
             for member in range(PER):
-                acc = outs[member]
+                acc = pltpu.roll(outs[member], 2 * gy, 0)
                 if group * PER + member == 3:
                     acc = jnp.where(lane >= 3 * WIDE, 1.0, acc)
                     chan[x, 35] = 1.0 / acc
@@ -218,27 +216,27 @@
             moved[x, (dy + 2) * 3 + c] = shifted(v, dy, 0, first, last)
 
     def couple(x):
-        total_of = [None] * 3
-        for dz in (0, 1, -1, 2, -2):
-            acc = [None] * 3
-            for number, d in enumerate(OFFSETS):
-                if d[2] != dz:
-                    continue
-                other = wrap(x + d[0])
-                place = (d[1] + 2) * 3
-                v = [moved[other, place + c] for c in range(3)]
-                s = [coef[x, number * 4 + c] for c in range(3)]
-                iso = coef[x, number * 4 + 3]
-                dot = s[0] * v[0] + s[1] * v[1] + s[2] * v[2]
-                new = [s[c] * dot - iso * v[c] for c in range(3)]
-                acc = [new[c] if acc[c] is None else acc[c] + new[c] for c in range(3)]
-            acc = [roll_lanes(t, dz) for t in acc]
-            total_of = [acc[c] if total_of[c] is None else total_of[c] + acc[c] for c in range(3)]
-        polar = chan[x, 3]
-        return [polar * t for t in total_of]
+        acc = {dz: [None] * 3 for dz in range(-2, 3)}
+        for dx in range(-2, 3):
+            other = wrap(x + dx)
+            for dy in range(-2, 3):
+                v = [moved[other, (dy + 2) * 3 + c] for c in range(3)]
+                for dz in range(-2, 3):
+                    if (dx, dy, dz) not in OFFSETS:
+                        continue
+                    number = OFFSETS.index((dx, dy, dz)) * 4
+                    s = [coef[x, number + c] for c in range(3)]
+                    iso = coef[x, number + 3]
+                    dot = s[0] * v[0] + s[1] * v[1] + s[2] * v[2]
+                    new = [s[c] * dot - iso * v[c] for c in range(3)]
+                    acc[dz] = [n if t is None else t + n for t, n in zip(acc[dz], new)]
+        out = acc[0]
+        for dz in (1, -1, 2, -2):
+            out = [o + roll_lanes(t, dz) for o, t in zip(out, acc[dz])]
+        return out
 
     zero = jnp.zeros((8, 128), F32)
-    mine = (along >= 18) & (along < 24)
+    slab = (along >= 18) & (along < 24)
 
     def start(x, carry):
         for c in range(3):
@@ -249,12 +247,13 @@
 
     def begin(x, carry):
         out = couple(x)
+        polar = chan[x, 3]
         for c in range(3):
             basis[0, x * 3 + c] = zero
-            basis[1, x * 3 + c] = out[c]
-        return carry
-
-    lax.fori_loop(0, NX, begin, 0)
+            basis[1, x * 3 + c] = polar * out[c]
+        return carry
+
+    unrolled(NX, 3, begin, 0)
 
     def again(x, carry):
         for c in range(3):
@@ -263,34 +262,30 @@
 
     unrolled(NX, 4, again, 0)
 
-    def extend(k, info):
+    def extend(k, carry):
+        info, before = carry
+
         def one(x, sums):
             out = couple(x)
+            polar = chan[x, 3]
             over = chan[x, 35]
             sums = list(sums)
             for c in range(3):
                 u = basis[k + 1, x * 3 + c]
-                p = basis[k, x * 3 + c]
-                basis[k + 2, x * 3 + c] = out[c]
-                w = out[c] * over
-                uw = u * over
-                sums[0] = sums[0] + w * u
-                sums[1] = sums[1] + w * p
-                sums[2] = sums[2] + w * out[c]
-                sums[3] = sums[3] + uw * u
-                sums[4] = sums[4] + uw * p
-                sums[5] = sums[5] + (p * over) * p
+                w = polar * out[c]
+                basis[k + 2, x * 3 + c] = w
+                sums[0] = sums[0] + out[c] * u
+                sums[1] = sums[1] + out[c] * basis[k, x * 3 + c]
+                sums[2] = sums[2] + out[c] * w
+                sums[3] = sums[3] + (u * over) * u
             return tuple(sums)
 
-        sums = lax.fori_loop(0, NX, one, (zero,) * 6)
-        now, past, full, norm, mixed, before = [total(jnp.where(mine, s, 0.0)) for s in sums]
-        tiny = 1e-30
+        sums = unrolled(NX, 3, one, (zero,) * 4)
+        now, past, full, norm = [total(jnp.where(slab, s, 0.0)) for s in sums]
+        tiny = 1e-36
         al = jnp.where(norm > tiny, now / jnp.maximum(norm, tiny), 0.0)
         be = jnp.where(before > tiny, past / jnp.maximum(before, tiny), 0.0)
-        rest = (
-            full - 2.0 * al * now - 2.0 * be * past
-            + al * al * norm + be * be * before + 2.0 * al * be * mixed
-        )
+        rest = full - al * now - be * past
         rest = jnp.maximum(rest, 1e-10 * full)
         good = (rest > tiny) & (norm > tiny)
         inv = jnp.where(good, jnp.sqrt(rest / jnp.maximum(norm, tiny)), 1.0)
@@ -308,9 +303,9 @@
         unrolled(NX, 4, scale, 0)
         info = jnp.where(lane == 45 + k, al, info)
         info = jnp.where(lane == 53 + k, be, info)
-        return jnp.where(lane == 61 + k, inv, info)
-
-    info = lax.fori_loop(0, ITERS, extend, zero)
+        return jnp.where(lane == 61 + k, inv, info), norm
+
+    info, _ = lax.fori_loop(0, ITERS, extend, (zero, jnp.zeros((1, 1), F32)))
 
     number = 0
     for low, high in ((0, 3), (3, BASIS)):
@@ -327,9 +322,9 @@
                             sums[n] = sums[n] + weighted * u[q]
             return tuple(sums)
 
-        sums = lax.fori_loop(0, NX, one, (zero,) * len(entries))
+        sums = unrolled(NX, 2, one, (zero,) * len(entries))
         for n in range(len(entries)):
-            info = jnp.where(lane == number, total(jnp.where(mine, sums[n], 0.0)), info)
+            info = jnp.where(lane == number, total(jnp.where(slab, sums[n], 0.0)), info)
             number += 1
 
     for e in range(16):
@@ -423,25 +418,29 @@
                         out[x, 3 * s + t, c : c + 1, :] = w[s : s + 1, :EDGE]
 
 
+REGION_IN = 14
+
+
 def per_device(permanent_field, polar, jitter, neighbors):
     packed = pl.pallas_call(
         pack_kernel,
         out_shape=jax.ShapeDtypeStruct((EDGE, GROUPS, 2, 128), F32),
+        compiler_params=pltpu.CompilerParams(vmem_limit_bytes=8 * 1024 * 1024),
         name="pack",
     )(permanent_field.transpose(0, 1, 3, 2), polar, jitter.transpose(0, 1, 3, 2), neighbors)
 
-    copies = jnp.broadcast_to(packed[None], (8,) + packed.shape)
-    plane = lax.all_to_all(copies, ("gx", "gy"), 0, 0, tiled=True)
-    plane = plane.reshape(2, 4, EDGE, GROUPS, 2, 128).transpose(0, 2, 3, 1, 4, 5)
-    own = plane.reshape(NX, GROUPS, 8, 128)
-
-    def fetch(k):
-        pairs = [((i + k) % 16, i) for i in range(16)]
-        pairs += [(16 + (i - k) % 16, 16 + i) for i in range(16)]
-        return lax.ppermute(own, ("gx",) + GZ, pairs)
-
-    direct = [fetch(k) for k in (1, 2, 3)]
-    passed = [lax.ppermute(v, "gx", [(0, 1), (1, 0)]) for v in direct]
+    around = [packed] + [
+        lax.ppermute(packed, "gy", [((i + k) % 4, i) for i in range(4)]) for k in (1, 2, 3)
+    ]
+    own = jnp.concatenate(around, axis=2)
+
+    def swap(v):
+        return lax.ppermute(v, "gx", [(0, 1), (1, 0)])
+
+    far = {k: lax.ppermute(own, GZ, [((i + k) % 16, i) for i in range(16)]) for k in (3, -3, 2, -2, 1, -1)}
+    far[0] = own
+    mine = [far[k] for k in range(-3, 4)]
+    theirs = [swap(v) for v in mine]
 
     vreg = (8, 128)
     kept, info = pl.pallas_call(
@@ -459,7 +458,7 @@
         ],
         compiler_params=pltpu.CompilerParams(vmem_limit_bytes=36 * 1024 * 1024),
         name="region",
-    )(own, *direct, *passed)
+    )(*mine, *theirs)
 
     info = lax.all_to_all(info, GZ, 0, 0, tiled=True)
 

time: 82.7 us -> 79.8 us (0.965)
  blocking collectives: 23 us -> 10.2 us
  starting transfers between devices: 9.72 us -> 21.1 us
  Pallas kernels: 37 us -> 31.9 us
  local copies, waits for them, and re-layouts: 0.96 us -> 3.41 us
  waiting for transfers between devices: 11.1 us -> 12.1 us
    ppermute x6 -> x16, starting transfers between devices: 9.72 us -> 21.1 us  [the longest x6 13.6 us: per_device(): lax.ppermute(own, GZ, [((i + k) % 16, i) for i in range(16)])]
    all_to_all x1 -> x0, blocking collectives: 10.8 us -> none  [per_device(): plane = lax.all_to_all(copies, ('gx', 'gy'), 0, 0, tiled=True)]
    pallas_call x1, Pallas kernels: 4.58 us -> 1.07 us  [per_device(): pl.pallas_call(pack_kernel, out_shape=jax.ShapeDtypeStruct((EDGE, GROUPS,...]
    unnamed x0 -> x8, local copies, waits for them, and re-layouts: none -> 3.41 us
    all_to_all x1, blocking collectives: 12.1 us -> 10.2 us  [per_device(): info = lax.all_to_all(info, GZ, 0, 0, tiled=True)]
    pallas_call x1, Pallas kernels: 29.9 us -> 28.4 us  [per_device(): pl.pallas_call(region_kernel, out_shape=(jax.ShapeDtypeStruct((EDGE, 31)...]
    ppermute x6 -> x16, waiting for transfers between devices: 11.1 us -> 12.1 us  [the longest x6 8.59 us: per_device(): lax.ppermute(own, GZ, [((i + k) % 16, i) for i in range(16)])]
  transfers between devices with their start and end apart: 6 -> 16, of which waited for: 4 -> 8; matrix products, arithmetic and copies ran while one was open for 0% -> 0% of each run, Pallas kernels for 0% -> 0%
where the time goes in v5:
time: 79.8 us; the launch traced here: 79.5 us
  Pallas kernels  31.9 us (40%)
  starting transfers between devices  21.1 us (26%)
  waiting for transfers between devices  12.1 us (15%)
  blocking collectives  10.2 us (13%)
  local copies, waits for them, and re-layouts  3.41 us (4%)
    pallas_call x1, Pallas kernels, per_device(): pl.pallas_call(region_kernel, out_shape=(jax.ShapeDtypeStruct((EDGE, 31)...  28.4 us
    ppermute x6, starting transfers between devices, per_device(): lax.ppermute(own, GZ, [((i + k) % 16, i) for i in range(16)])  13.6 us
    all_to_all x1, blocking collectives, per_device(): info = lax.all_to_all(info, GZ, 0, 0, tiled=True)  10.2 us
    ppermute x6, waiting for transfers between devices, per_device(): lax.ppermute(own, GZ, [((i + k) % 16, i) for i in range(16)])  8.59 us
    ppermute x3, starting transfers between devices, per_device(): lax.ppermute(packed, 'gy', [((i + k) % 4, i) for i in range(4)])  5.87 us
    unnamed x8, local copies, waits for them, and re-layouts  3.41 us
    pallas_call x1, Pallas kernels, per_device(): pl.pallas_call(finish_kernel, out_shape=(jax.ShapeDtypeStruct((EDGE, EDGE...  2.5 us
    ppermute x3, waiting for transfers between devices, per_device(): lax.ppermute(packed, 'gy', [((i + k) % 4, i) for i in range(4)])  2.46 us
  transfers between devices with their start and end apart: 16, of which 8 were waited for; matrix products, arithmetic and copies ran while one was open for 0% of the time, Pallas kernels for 0%

profile of v5, /device:TPU:0, one launch (start us, length us, event | category | flops | bytes accessed | tf_op | source)
XLA Modules:
  0.0 79.5 jit_solution(11168908147298298300)
XLA Ops:
  0.6 0.0 copy-start
  0.6 0.9 %copy-done = s32[6,6,6,56]{3,2,1,0:T(8,128)S(1)} copy-done((s32[6,6,6,56]{3,2,1,0:T(8,128)S(1)}, s32[6,6,6,56]{3,2,1,0:T(8,128)}, u32[]{:S(2)}) %copy-start) | copy-done | bytes 48408
  1.5 0.0 copy-start.1
  1.5 0.9 %copy-done.1 = f32[6,6,6,3]{2,3,1,0:T(4,128)S(1)} copy-done((f32[6,6,6,3]{2,3,1,0:T(4,128)S(1)}, f32[6,6,6,3]{2,3,1,0:T(4,128)}, u32[]{:S(2)}) %copy-start.1) | copy-done | bytes 2616
  2.4 0.0 copy-start.2
  2.4 0.9 %copy-done.2 = f32[6,6,6,3]{2,3,1,0:T(4,128)S(1)} copy-done((f32[6,6,6,3]{2,3,1,0:T(4,128)S(1)}, f32[6,6,6,3]{2,3,1,0:T(4,128)}, u32[]{:S(2)}) %copy-start.2) | copy-done | bytes 2616
  3.3 0.0 copy-start.3
  3.3 0.7 copy-done.3
  4.0 1.1 %pack.1 = f32[6,5,2,128]{3,2,1,0:T(2,128)S(1)} custom-call(f32[6,6,3,6]{3,2,1,0:T(4,128)S(1)} %bitcast.5, f32[6,6,6]{2,1,0:T(8,128)S(1)} %copy-done.3, f32[6,6,3,6]{3,2,1,0:T(4,128)S(1)} %bitcast.6, s32[6,6,6,56]{3,2,1,0:T(8,128)S(1)} %copy-done), custom_call_target="tpu_custom_call" | custom-call | tf_op jit(solution)/shard_map/pack/pallas_call | solution.py:425
  5.1 1.7 %collective-permute-start.2 = (f32[6,5,2,128]{3,2,1,0:T(2,128)S(1)}, f32[6,5,2,128]{3,2,1,0:T(2,128)S(1)}, u32[]{:S(2)}, u32[]{:S(2)}) collective-permute-start(f32[6,5,2,128]{3,2,1,0:T(2,128)S(1)} %pack.1), channel_id=1, source_target_pairs={{48,0},{0,16},{16,32},{32,48},{49,1},{1,17},{17,33},{33,49},{50,2}... | collective-permute-start | bytes 92168 | tf_op jit(solution)/shard_map/ppermute | solution.py:433
  6.8 2.7 %collective-permute-start.1 = (f32[6,5,2,128]{3,2,1,0:T(2,128)S(1)}, f32[6,5,2,128]{3,2,1,0:T(2,128)S(1)}, u32[]{:S(2)}, u32[]{:S(2)}) collective-permute-start(f32[6,5,2,128]{3,2,1,0:T(2,128)S(1)} %pack.1), channel_id=1, source_target_pairs={{32,0},{48,16},{0,32},{16,48},{33,1},{49,17},{1,33},{17,49},{34,2}... | collective-permute-start | bytes 92168 | tf_op jit(solution)/shard_map/ppermute | solution.py:433
  9.6 1.4 %collective-permute-start = (f32[6,5,2,128]{3,2,1,0:T(2,128)S(1)}, f32[6,5,2,128]{3,2,1,0:T(2,128)S(1)}, u32[]{:S(2)}, u32[]{:S(2)}) collective-permute-start(f32[6,5,2,128]{3,2,1,0:T(2,128)S(1)} %pack.1), channel_id=1, source_target_pairs={{16,0},{32,16},{48,32},{0,48},{17,1},{33,17},{49,33},{1,49},{18,2}... | collective-permute-start | bytes 92168 | tf_op jit(solution)/shard_map/ppermute | solution.py:433
  11.0 0.0 collective-permute-done.2
  11.0 1.2 %collective-permute-done.1 = f32[6,5,2,128]{3,2,1,0:T(2,128)S(1)} collective-permute-done((f32[6,5,2,128]{3,2,1,0:T(2,128)S(1)}, f32[6,5,2,128]{3,2,1,0:T(2,128)S(1)}, u32[]{:S(2)}, u32[]{:S(2)}) %collective-permute-start.1) | collective-permute-done | bytes 30752 | tf_op jit(solution)/shard_map/ppermute | solution.py:433
  12.2 1.2 %collective-permute-done = f32[6,5,2,128]{3,2,1,0:T(2,128)S(1)} collective-permute-done((f32[6,5,2,128]{3,2,1,0:T(2,128)S(1)}, f32[6,5,2,128]{3,2,1,0:T(2,128)S(1)}, u32[]{:S(2)}, u32[]{:S(2)}) %collective-permute-start) | collective-permute-done | bytes 30752 | tf_op jit(solution)/shard_map/ppermute | solution.py:433
  13.5 0.1 pad_maximum_fusion.refs_3_
  13.5 0.1 collective-permute-start.12
  13.6 5.1 %collective-permute-start.8 = (f32[6,5,8,128]{3,2,1,0:T(8,128)S(1)}, f32[6,5,8,128]{3,2,1,0:T(8,128)S(1)}, u32[]{:S(2)}, u32[]{:S(2)}) collective-permute-start(f32[6,5,8,128]{3,2,1,0:T(8,128)S(1)} %pad_maximum_fusion.refs_3_), channel_id=1, source_target_pairs={{3,0},{4,1},{5,2},{6,3},{7,4},{8,5},{9,6},{10,7},{11,8},{12,9},{13... | collective-permute-start | bytes 368648 | tf_op jit(solution)/shard_map/ppermute | solution.py:440
  18.7 2.7 %collective-permute-start.7 = (f32[6,5,8,128]{3,2,1,0:T(8,128)S(1)}, f32[6,5,8,128]{3,2,1,0:T(8,128)S(1)}, u32[]{:S(2)}, u32[]{:S(2)}) collective-permute-start(f32[6,5,8,128]{3,2,1,0:T(8,128)S(1)} %pad_maximum_fusion.refs_3_), channel_id=1, source_target_pairs={{2,0},{3,1},{4,2},{5,3},{6,4},{7,5},{8,6},{9,7},{10,8},{11,9},{12,... | collective-permute-start | bytes 368648 | tf_op jit(solution)/shard_map/ppermute | solution.py:440
  21.5 1.3 %collective-permute-start.6 = (f32[6,5,8,128]{3,2,1,0:T(8,128)S(1)}, f32[6,5,8,128]{3,2,1,0:T(8,128)S(1)}, u32[]{:S(2)}, u32[]{:S(2)}) collective-permute-start(f32[6,5,8,128]{3,2,1,0:T(8,128)S(1)} %pad_maximum_fusion.refs_3_), channel_id=1, source_target_pairs={{1,0},{2,1},{3,2},{4,3},{5,4},{6,5},{7,6},{8,7},{9,8},{10,9},{11,1... | collective-permute-start | bytes 368648 | tf_op jit(solution)/shard_map/ppermute | solution.py:440
  22.8 0.7 collective-permute-start.5
  23.5 0.0 collective-permute-done.12.refs_10_
  23.5 0.9 %collective-permute-start.4 = (f32[6,5,8,128]{3,2,1,0:T(8,128)S(1)}, f32[6,5,8,128]{3,2,1,0:T(8,128)S(1)}, u32[]{:S(2)}, u32[]{:S(2)}) collective-permute-start(f32[6,5,8,128]{3,2,1,0:T(8,128)S(1)} %pad_maximum_fusion.refs_3_), channel_id=1, source_target_pairs={{14,0},{15,1},{0,2},{1,3},{2,4},{3,5},{4,6},{5,7},{6,8},{7,9},{8,1... | collective-permute-start | bytes 368648 | tf_op jit(solution)/shard_map/ppermute | solution.py:440
  24.4 0.0 collective-permute-done.8.refs_6_
  24.4 2.8 %collective-permute-start.3 = (f32[6,5,8,128]{3,2,1,0:T(8,128)S(1)}, f32[6,5,8,128]{3,2,1,0:T(8,128)S(1)}, u32[]{:S(2)}, u32[]{:S(2)}) collective-permute-start(f32[6,5,8,128]{3,2,1,0:T(8,128)S(1)} %pad_maximum_fusion.refs_3_), channel_id=1, source_target_pairs={{13,0},{14,1},{15,2},{0,3},{1,4},{2,5},{3,6},{4,7},{5,8},{6,9},{7,... | collective-permute-start | bytes 368648 | tf_op jit(solution)/shard_map/ppermute | solution.py:440
  27.2 3.1 %collective-permute-done.7.refs_5_ = f32[6,5,8,128]{3,2,1,0:T(8,128)S(1)} collective-permute-done((f32[6,5,8,128]{3,2,1,0:T(8,128)S(1)}, f32[6,5,8,128]{3,2,1,0:T(8,128)S(1)}, u32[]{:S(2)}, u32[]{:S(2)}) %collective-permute-start.7) | collective-permute-done | bytes 122912 | tf_op jit(solution)/shard_map/ppermute | solution.py:440
  30.3 0.0 collective-permute-start.15
  30.3 0.0 collective-permute-done.6.refs_4_
  30.3 0.5 collective-permute-start.14
  30.9 5.5 %collective-permute-done.5.refs_2_ = f32[6,5,8,128]{3,2,1,0:T(8,128)S(1)} collective-permute-done((f32[6,5,8,128]{3,2,1,0:T(8,128)S(1)}, f32[6,5,8,128]{3,2,1,0:T(8,128)S(1)}, u32[]{:S(2)}, u32[]{:S(2)}) %collective-permute-start.5) | collective-permute-done | bytes 122912 | tf_op jit(solution)/shard_map/ppermute | solution.py:440
  36.3 0.0 collective-permute-start.13
  36.3 0.0 collective-permute-done.4.refs_1_
  36.3 0.5 collective-permute-start.11
  36.9 0.0 collective-permute-done.3.refs_0_
  36.9 0.1 collective-permute-start.10
  36.9 0.0 collective-permute-done.15.refs_13_
  36.9 0.4 collective-permute-start.9
  37.4 0.0 collective-permute-done.14.refs_12_
  37.4 0.3 collective-permute-done.13.refs_11_
  37.7 0.2 collective-permute-done.11.refs_9_
  37.8 0.3 collective-permute-done.10.refs_8_
  38.2 0.2 collective-permute-done.9.refs_7_
  38.4 28.4 %region.1 = (f32[6,31,8,128]{3,2,1,0:T(8,128)S(1)}, f32[16,8,128]{2,1,0:T(8,128)S(1)}) custom-call(f32[6,5,8,128]{3,2,1,0:T(8,128)S(1)} %collective-permute-done.3.refs_0_, f32[6,5,8,128]{3,2,1,0:T(8,128)S(1)} %collective-permute-done.4.refs_1_, f32[6,5,8,128]{3,2,1,0:T(8,128)S(1)} %collective-permute-done.5.refs_2_, ...), custom_call_target="tpu_custom_call" | custom-call | tf_op jit(solution)/shard_map/region/pallas_call | solution.py:446
  66.7 10.2 %all_to_all.5.info = f32[16,8,128]{2,1,0:T(8,128)S(1)} all-to-all(f32[16,8,128]{2,1,0:T(8,128)S(1)} %get-tuple-element.9), channel_id=1, replica_groups=mesh['gx'=2,'gy'=4,'gz_0'=4,'gz_1'=4] {'gz_0','gz_1'}, dimensions={0} | all-to-all | bytes 131072 | tf_op jit(solution)/shard_map/all_to_all | solution.py:463
  77.0 2.5 %finish.1 = (f32[6,6,3,6]{3,2,1,0:T(4,128)}, f32[6,6,3,6]{3,2,1,0:T(4,128)}, f32[1,8]{1,0:T(1,128)}) custom-call(f32[6,31,8,128]{3,2,1,0:T(8,128)S(1)} %get-tuple-element.8.kept, f32[16,8,128]{2,1,0:T(8,128)S(1)} %all_to_all.5.info), custom_call_target="tpu_custom_call" | custom-call | tf_op jit(solution)/shard_map/finish/pallas_call | solution.py:465
Async XLA Ops:
  0.6 0.9 %copy-start = (s32[6,6,6,56]{3,2,1,0:T(8,128)S(1)}, s32[6,6,6,56]{3,2,1,0:T(8,128)}, u32[]{:S(2)}) copy-start(s32[6,6,6,56]{3,2,1,0:T(8,128)} %neighbors.1) | copy-start | bytes 145156
  1.5 0.9 %copy-start.1 = (f32[6,6,6,3]{2,3,1,0:T(4,128)S(1)}, f32[6,6,6,3]{2,3,1,0:T(4,128)}, u32[]{:S(2)}) copy-start(f32[6,6,6,3]{2,3,1,0:T(4,128)} %param.4) | copy-start | bytes 7780
  2.4 0.9 %copy-start.2 = (f32[6,6,6,3]{2,3,1,0:T(4,128)S(1)}, f32[6,6,6,3]{2,3,1,0:T(4,128)}, u32[]{:S(2)}) copy-start(f32[6,6,6,3]{2,3,1,0:T(4,128)} %param.6) | copy-start | bytes 7780
  3.3 0.7 copy-start.3
  5.1 5.9 %collective-permute-start.2 = (f32[6,5,2,128]{3,2,1,0:T(2,128)S(1)}, f32[6,5,2,128]{3,2,1,0:T(2,128)S(1)}, u32[]{:S(2)}, u32[]{:S(2)}) collective-permute-start(f32[6,5,2,128]{3,2,1,0:T(2,128)S(1)} %pack.1), channel_id=1, source_target_pairs={{48,0},{0,16},{16,32},{32,48},{49,1},{1,17},{17,33},{33,49},{50,2}... | collective-permute-start | bytes 92168 | tf_op jit(solution)/shard_map/ppermute | solution.py:433
  6.8 5.4 %collective-permute-start.1 = (f32[6,5,2,128]{3,2,1,0:T(2,128)S(1)}, f32[6,5,2,128]{3,2,1,0:T(2,128)S(1)}, u32[]{:S(2)}, u32[]{:S(2)}) collective-permute-start(f32[6,5,2,128]{3,2,1,0:T(2,128)S(1)} %pack.1), channel_id=1, source_target_pairs={{32,0},{48,16},{0,32},{16,48},{33,1},{49,17},{1,33},{17,49},{34,2}... | collective-permute-start | bytes 92168 | tf_op jit(solution)/shard_map/ppermute | solution.py:433
  9.6 3.9 %collective-permute-start = (f32[6,5,2,128]{3,2,1,0:T(2,128)S(1)}, f32[6,5,2,128]{3,2,1,0:T(2,128)S(1)}, u32[]{:S(2)}, u32[]{:S(2)}) collective-permute-start(f32[6,5,2,128]{3,2,1,0:T(2,128)S(1)} %pack.1), channel_id=1, source_target_pairs={{16,0},{32,16},{48,32},{0,48},{17,1},{33,17},{49,33},{1,49},{18,2}... | collective-permute-start | bytes 92168 | tf_op jit(solution)/shard_map/ppermute | solution.py:433
  13.5 10.0 %collective-permute-start.12 = (f32[6,5,8,128]{3,2,1,0:T(8,128)S(1)}, f32[6,5,8,128]{3,2,1,0:T(8,128)S(1)}, u32[]{:S(2)}, u32[]{:S(2)}) collective-permute-start(f32[6,5,8,128]{3,2,1,0:T(8,128)S(1)} %pad_maximum_fusion.refs_3_), channel_id=1, source_target_pairs={{0,64},{64,0},{1,65},{65,1},{2,66},{66,2},{3,67},{67,3},{4,68},{68... | collective-permute-start | bytes 368648 | tf_op jit(solution)/shard_map/ppermute | solution.py:438
  13.6 10.8 %collective-permute-start.8 = (f32[6,5,8,128]{3,2,1,0:T(8,128)S(1)}, f32[6,5,8,128]{3,2,1,0:T(8,128)S(1)}, u32[]{:S(2)}, u32[]{:S(2)}) collective-permute-start(f32[6,5,8,128]{3,2,1,0:T(8,128)S(1)} %pad_maximum_fusion.refs_3_), channel_id=1, source_target_pairs={{3,0},{4,1},{5,2},{6,3},{7,4},{8,5},{9,6},{10,7},{11,8},{12,9},{13... | collective-permute-start | bytes 368648 | tf_op jit(solution)/shard_map/ppermute | solution.py:440
  18.7 11.6 %collective-permute-start.7 = (f32[6,5,8,128]{3,2,1,0:T(8,128)S(1)}, f32[6,5,8,128]{3,2,1,0:T(8,128)S(1)}, u32[]{:S(2)}, u32[]{:S(2)}) collective-permute-start(f32[6,5,8,128]{3,2,1,0:T(8,128)S(1)} %pad_maximum_fusion.refs_3_), channel_id=1, source_target_pairs={{2,0},{3,1},{4,2},{5,3},{6,4},{7,5},{8,6},{9,7},{10,8},{11,9},{12,... | collective-permute-start | bytes 368648 | tf_op jit(solution)/shard_map/ppermute | solution.py:440
  21.5 8.9 %collective-permute-start.6 = (f32[6,5,8,128]{3,2,1,0:T(8,128)S(1)}, f32[6,5,8,128]{3,2,1,0:T(8,128)S(1)}, u32[]{:S(2)}, u32[]{:S(2)}) collective-permute-start(f32[6,5,8,128]{3,2,1,0:T(8,128)S(1)} %pad_maximum_fusion.refs_3_), channel_id=1, source_target_pairs={{1,0},{2,1},{3,2},{4,3},{5,4},{6,5},{7,6},{8,7},{9,8},{10,9},{11,1... | collective-permute-start | bytes 368648 | tf_op jit(solution)/shard_map/ppermute | solution.py:440
  22.8 13.5 %collective-permute-start.5 = (f32[6,5,8,128]{3,2,1,0:T(8,128)S(1)}, f32[6,5,8,128]{3,2,1,0:T(8,128)S(1)}, u32[]{:S(2)}, u32[]{:S(2)}) collective-permute-start(f32[6,5,8,128]{3,2,1,0:T(8,128)S(1)} %pad_maximum_fusion.refs_3_), channel_id=1, source_target_pairs={{15,0},{0,1},{1,2},{2,3},{3,4},{4,5},{5,6},{6,7},{7,8},{8,9},{9,10... | collective-permute-start | bytes 368648 | tf_op jit(solution)/shard_map/ppermute | solution.py:440
  23.5 12.8 %collective-permute-start.4 = (f32[6,5,8,128]{3,2,1,0:T(8,128)S(1)}, f32[6,5,8,128]{3,2,1,0:T(8,128)S(1)}, u32[]{:S(2)}, u32[]{:S(2)}) collective-permute-start(f32[6,5,8,128]{3,2,1,0:T(8,128)S(1)} %pad_maximum_fusion.refs_3_), channel_id=1, source_target_pairs={{14,0},{15,1},{0,2},{1,3},{2,4},{3,5},{4,6},{5,7},{6,8},{7,9},{8,1... | collective-permute-start | bytes 368648 | tf_op jit(solution)/shard_map/ppermute | solution.py:440
  24.4 12.4 %collective-permute-start.3 = (f32[6,5,8,128]{3,2,1,0:T(8,128)S(1)}, f32[6,5,8,128]{3,2,1,0:T(8,128)S(1)}, u32[]{:S(2)}, u32[]{:S(2)}) collective-permute-start(f32[6,5,8,128]{3,2,1,0:T(8,128)S(1)} %pad_maximum_fusion.refs_3_), channel_id=1, source_target_pairs={{13,0},{14,1},{15,2},{0,3},{1,4},{2,5},{3,6},{4,7},{5,8},{6,9},{7,... | collective-permute-start | bytes 368648 | tf_op jit(solution)/shard_map/ppermute | solution.py:440
  30.3 6.6 %collective-permute-start.15 = (f32[6,5,8,128]{3,2,1,0:T(8,128)S(1)}, f32[6,5,8,128]{3,2,1,0:T(8,128)S(1)}, u32[]{:S(2)}, u32[]{:S(2)}) collective-permute-start(f32[6,5,8,128]{3,2,1,0:T(8,128)S(1)} %collective-permute-done.8.refs_6_), channel_id=1, source_target_pairs={{0,64},{64,0},{1,65},{65,1},{2,66},{66,2},{3,67},{67,3},{4,68},{68... | collective-permute-start | bytes 368648 | tf_op jit(solution)/shard_map/ppermute | solution.py:438
  30.3 7.0 %collective-permute-start.14 = (f32[6,5,8,128]{3,2,1,0:T(8,128)S(1)}, f32[6,5,8,128]{3,2,1,0:T(8,128)S(1)}, u32[]{:S(2)}, u32[]{:S(2)}) collective-permute-start(f32[6,5,8,128]{3,2,1,0:T(8,128)S(1)} %collective-permute-done.7.refs_5_), channel_id=1, source_target_pairs={{0,64},{64,0},{1,65},{65,1},{2,66},{66,2},{3,67},{67,3},{4,68},{68... | collective-permute-start | bytes 368648 | tf_op jit(solution)/shard_map/ppermute | solution.py:438
  36.3 1.3 %collective-permute-start.13 = (f32[6,5,8,128]{3,2,1,0:T(8,128)S(1)}, f32[6,5,8,128]{3,2,1,0:T(8,128)S(1)}, u32[]{:S(2)}, u32[]{:S(2)}) collective-permute-start(f32[6,5,8,128]{3,2,1,0:T(8,128)S(1)} %collective-permute-done.6.refs_4_), channel_id=1, source_target_pairs={{0,64},{64,0},{1,65},{65,1},{2,66},{66,2},{3,67},{67,3},{4,68},{68... | collective-permute-start | bytes 368648 | tf_op jit(solution)/shard_map/ppermute | solution.py:438
  36.3 1.5 %collective-permute-start.11 = (f32[6,5,8,128]{3,2,1,0:T(8,128)S(1)}, f32[6,5,8,128]{3,2,1,0:T(8,128)S(1)}, u32[]{:S(2)}, u32[]{:S(2)}) collective-permute-start(f32[6,5,8,128]{3,2,1,0:T(8,128)S(1)} %collective-permute-done.5.refs_2_), channel_id=1, source_target_pairs={{0,64},{64,0},{1,65},{65,1},{2,66},{66,2},{3,67},{67,3},{4,68},{68... | collective-permute-start | bytes 368648 | tf_op jit(solution)/shard_map/ppermute | solution.py:438
  36.9 1.3 %collective-permute-start.10 = (f32[6,5,8,128]{3,2,1,0:T(8,128)S(1)}, f32[6,5,8,128]{3,2,1,0:T(8,128)S(1)}, u32[]{:S(2)}, u32[]{:S(2)}) collective-permute-start(f32[6,5,8,128]{3,2,1,0:T(8,128)S(1)} %collective-permute-done.4.refs_1_), channel_id=1, source_target_pairs={{0,64},{64,0},{1,65},{65,1},{2,66},{66,2},{3,67},{67,3},{4,68},{68... | collective-permute-start | bytes 368648 | tf_op jit(solution)/shard_map/ppermute | solution.py:438
  36.9 1.4 %collective-permute-start.9 = (f32[6,5,8,128]{3,2,1,0:T(8,128)S(1)}, f32[6,5,8,128]{3,2,1,0:T(8,128)S(1)}, u32[]{:S(2)}, u32[]{:S(2)}) collective-permute-start(f32[6,5,8,128]{3,2,1,0:T(8,128)S(1)} %collective-permute-done.3.refs_0_), channel_id=1, source_target_pairs={{0,64},{64,0},{1,65},{65,1},{2,66},{66,2},{3,67},{67,3},{4,68},{68... | collective-permute-start | bytes 368648 | tf_op jit(solution)/shard_map/ppermute | solution.py:438

commit v6 on v5

--- a/solution.py
+++ b/solution.py
@@ -82,7 +82,14 @@
     return lax.fori_loop(0, count // times, several, carry)
 
 
-def pack_kernel(field, polar, jitter, neighbors, out):
+def pack_kernel(
+    field_in, polar_in, jitter_in, neighbors_in, out, field, polar, jitter, neighbors, arrived
+):
+    given = (neighbors_in, field_in, jitter_in, polar_in)
+    kept = (neighbors, field, jitter, polar)
+    copies = [pltpu.make_async_copy(g, k, arrived.at[n]) for n, (g, k) in enumerate(zip(given, kept))]
+    for copy in copies:
+        copy.start()
     lane = lax.broadcasted_iota(jnp.int32, (1, 128), 1)
     third = jnp.where(lane >= 2 * WIDE, 2, jnp.where(lane >= WIDE, 1, 0))
     inside = lane - third * WIDE
@@ -103,6 +110,9 @@
         for n in range(PER):
             hit = hit | (column == row + (t * WIDE + n * EDGE))
         pick.append((jnp.where(hit, 32.0, 0.0).astype(jnp.bfloat16), jnp.where(hit, 1.0, 0.0).astype(jnp.bfloat16)))
+
+    for copy in copies:
+        copy.wait()
 
     def one(x, carry):
         for s in range(2):
@@ -136,22 +146,25 @@
     unrolled(EDGE, 2, one, 0)
 
 
-def region_kernel(*refs):
-    mine, theirs = refs[:7], refs[7:14]
-    kept_out, info_out, chan, near, coef, moved, basis = refs[14:]
+def region_kernel(
+    own, a1, a2, a3, b1, b2, b3, kept_out, info_out, chan, near, coef, moved, basis,
+):
     gx = lax.axis_index("gx")
     gy = lax.axis_index("gy")
     lane = lane_iota()
     first, last = third_masks()
     along = lane - jnp.where(last, 2 * WIDE, jnp.where(first, 0, WIDE))
-
-    def gather(step, carry):
-        half = step // EDGE
-        at = step - half * EDGE
-        x = step
-        is_mine = (lane * 0 + gx) == half
+    is_low = (lane * 0 + gx) == 0
+
+    def gather(x, carry):
+        half = x // EDGE
+        within = x - half * EDGE
+        here = within + jnp.where(half == gx, 0, EDGE)
+        there = within + jnp.where(half == gx, EDGE, 0)
         for group in range(GROUPS):
-            blocks = [jnp.where(is_mine, m[at, group], t[at, group]) for m, t in zip(mine, theirs)]
+            ahead = [jnp.where(is_low, a[here, group], b[there, group]) for a, b in ((a1, b1), (a2, b2), (a3, b3))]
+            back = [jnp.where(is_low, b[there, group], a[here, group]) for a, b in ((a3, b3), (a2, b2), (a1, b1))]
+            blocks = back + [own[here, group]] + ahead
             outs = [None] * PER
             for gap in range(-6, 7):
                 members = [m for m in range(PER) if 0 <= m + gap < PER]
@@ -418,29 +431,39 @@
                         out[x, 3 * s + t, c : c + 1, :] = w[s : s + 1, :EDGE]
 
 
-REGION_IN = 14
-
-
 def per_device(permanent_field, polar, jitter, neighbors):
     packed = pl.pallas_call(
         pack_kernel,
         out_shape=jax.ShapeDtypeStruct((EDGE, GROUPS, 2, 128), F32),
-        compiler_params=pltpu.CompilerParams(vmem_limit_bytes=8 * 1024 * 1024),
+        in_specs=[pl.BlockSpec(memory_space=pltpu.HBM)] * 4,
+        scratch_shapes=[
+            pltpu.VMEM((EDGE, EDGE, 3, EDGE), F32),
+            pltpu.VMEM((EDGE, EDGE, EDGE), F32),
+            pltpu.VMEM((EDGE, EDGE, 3, EDGE), F32),
+            pltpu.VMEM((EDGE, EDGE, EDGE, 56), jnp.int32),
+            pltpu.SemaphoreType.DMA((4,)),
+        ],
+        compiler_params=pltpu.CompilerParams(vmem_limit_bytes=60 * 1024 * 1024),
         name="pack",
     )(permanent_field.transpose(0, 1, 3, 2), polar, jitter.transpose(0, 1, 3, 2), neighbors)
 
     around = [packed] + [
         lax.ppermute(packed, "gy", [((i + k) % 4, i) for i in range(4)]) for k in (1, 2, 3)
     ]
-    own = jnp.concatenate(around, axis=2)
+    half = jnp.concatenate(around, axis=2)
 
     def swap(v):
         return lax.ppermute(v, "gx", [(0, 1), (1, 0)])
 
-    far = {k: lax.ppermute(own, GZ, [((i + k) % 16, i) for i in range(16)]) for k in (3, -3, 2, -2, 1, -1)}
-    far[0] = own
-    mine = [far[k] for k in range(-3, 4)]
-    theirs = [swap(v) for v in mine]
+    own = jnp.concatenate([half, swap(half)], axis=0)
+
+    def fetch(k):
+        pairs = [((i + k) % 16, i) for i in range(16)]
+        pairs += [(16 + (i - k) % 16, 16 + i) for i in range(16)]
+        return lax.ppermute(own, ("gx",) + GZ, pairs)
+
+    direct = [fetch(k) for k in (1, 2, 3)]
+    passed = [swap(v) for v in direct]
 
     vreg = (8, 128)
     kept, info = pl.pallas_call(
@@ -458,7 +481,7 @@
         ],
         compiler_params=pltpu.CompilerParams(vmem_limit_bytes=36 * 1024 * 1024),
         name="region",
-    )(*mine, *theirs)
+    )(own, *direct, *passed)
 
     info = lax.all_to_all(info, GZ, 0, 0, tiled=True)
 

time: 79.8 us -> 78.1 us (0.979)
  starting transfers between devices: 21.1 us -> 15.7 us
  local copies, waits for them, and re-layouts: 3.41 us -> 0.01 us
  waiting for transfers between devices: 12.1 us -> 15.1 us
  blocking collectives: 10.2 us -> 12.2 us
  Pallas kernels: 31.9 us -> 33.4 us
  other arithmetic: 0.06 us -> 0.88 us
    ppermute x6 -> x3, starting transfers between devices: 13.6 us -> 9.21 us  [fetch(): return lax.ppermute(own, ('gx',) + GZ, pairs)]
    unnamed x8 -> x2, local copies, waits for them, and re-layouts: 3.41 us -> 0.01 us
    all_to_all x1, blocking collectives: 10.2 us -> 12.2 us  [per_device(): info = lax.all_to_all(info, GZ, 0, 0, tiled=True)]
    ppermute x7 -> x4, waiting for transfers between devices: 1 us -> 2.67 us  [swap(): return lax.ppermute(v, 'gx', [(0, 1), (1, 0)])]
    pallas_call x1, Pallas kernels: 1.07 us -> 2.59 us  [per_device(): pl.pallas_call(pack_kernel, out_shape=jax.ShapeDtypeStruct((EDGE, GROUPS,...]
    ppermute x6 -> x3, waiting for transfers between devices: 8.59 us -> 9.73 us  [fetch(): return lax.ppermute(own, ('gx',) + GZ, pairs)]
    ppermute x7 -> x4, starting transfers between devices: 1.62 us -> 0.6 us  [swap(): return lax.ppermute(v, 'gx', [(0, 1), (1, 0)])]
    concatenate x1 -> x2, other arithmetic: 0.06 us -> 0.88 us  [the longest x1 0.81 us: per_device(): half = jnp.concatenate(around, axis=2)]
  transfers between devices with their start and end apart: 16 -> 10, of which waited for: 8 -> 7; matrix products, arithmetic and copies ran while one was open for 0% -> 0% of each run, Pallas kernels for 0% -> 0%
where the time goes in v6:
time: 78.1 us; the launch traced here: 77.9 us
  Pallas kernels  33.4 us (43%)
  starting transfers between devices  15.7 us (20%)
  waiting for transfers between devices  15.1 us (19%)
  blocking collectives  12.2 us (16%)
  other arithmetic  0.88 us (1%)
    pallas_call x1, Pallas kernels, per_device(): pl.pallas_call(region_kernel, out_shape=(jax.ShapeDtypeStruct((EDGE, 31)...  28.3 us
    all_to_all x1, blocking collectives, per_device(): info = lax.all_to_all(info, GZ, 0, 0, tiled=True)  12.2 us
    ppermute x3, waiting for transfers between devices, fetch(): return lax.ppermute(own, ('gx',) + GZ, pairs)  9.73 us
    ppermute x3, starting transfers between devices, fetch(): return lax.ppermute(own, ('gx',) + GZ, pairs)  9.21 us
    ppermute x3, starting transfers between devices, per_device(): lax.ppermute(packed, 'gy', [((i + k) % 4, i) for i in range(4)])  5.87 us
    ppermute x4, waiting for transfers between devices, swap(): return lax.ppermute(v, 'gx', [(0, 1), (1, 0)])  2.67 us
    ppermute x3, waiting for transfers between devices, per_device(): lax.ppermute(packed, 'gy', [((i + k) % 4, i) for i in range(4)])  2.67 us
    pallas_call x1, Pallas kernels, per_device(): pl.pallas_call(pack_kernel, out_shape=jax.ShapeDtypeStruct((EDGE, GROUPS,...  2.59 us
  transfers between devices with their start and end apart: 10, of which 7 were waited for; matrix products, arithmetic and copies ran while one was open for 0% of the time, Pallas kernels for 0%

profile of v6, /device:TPU:0, one launch (start us, length us, event | category | flops | bytes accessed | tf_op | source)
XLA Modules:
  0.0 77.9 jit_solution(12692493219520890723)
XLA Ops:
  0.6 2.6 %pack.1 = f32[6,5,2,128]{3,2,1,0:T(2,128)} custom-call(f32[6,6,3,6]{3,2,1,0:T(4,128)} %bitcast.5, f32[6,6,6]{2,1,0:T(8,128)} %polar_in.1, f32[6,6,3,6]{3,2,1,0:T(4,128)} %bitcast.6, s32[6,6,6,56]{3,2,1,0:T(8,128)} %neighbors_in.1), custom_call_target="tpu_custom_call" | custom-call | tf_op jit(solution)/shard_map/pack/pallas_call | solution.py:435
  3.2 0.0 copy-start
  3.2 1.7 %collective-permute-start.2 = (f32[6,5,2,128]{3,2,1,0:T(2,128)}, f32[6,5,2,128]{3,2,1,0:T(2,128)S(1)}, u32[]{:S(2)}, u32[]{:S(2)}) collective-permute-start(f32[6,5,2,128]{3,2,1,0:T(2,128)} %pack.1), channel_id=1, source_target_pairs={{48,0},{0,16},{16,32},{32,48},{49,1},{1,17},{17,33},{33,49},{50,2}... | collective-permute-start | bytes 92168 | tf_op jit(solution)/shard_map/ppermute | solution.py:451
  4.9 2.7 %collective-permute-start.1 = (f32[6,5,2,128]{3,2,1,0:T(2,128)}, f32[6,5,2,128]{3,2,1,0:T(2,128)S(1)}, u32[]{:S(2)}, u32[]{:S(2)}) collective-permute-start(f32[6,5,2,128]{3,2,1,0:T(2,128)} %pack.1), channel_id=1, source_target_pairs={{32,0},{48,16},{0,32},{16,48},{33,1},{49,17},{1,33},{17,49},{34,2}... | collective-permute-start | bytes 92168 | tf_op jit(solution)/shard_map/ppermute | solution.py:451
  7.7 1.4 %collective-permute-start = (f32[6,5,2,128]{3,2,1,0:T(2,128)}, f32[6,5,2,128]{3,2,1,0:T(2,128)S(1)}, u32[]{:S(2)}, u32[]{:S(2)}) collective-permute-start(f32[6,5,2,128]{3,2,1,0:T(2,128)} %pack.1), channel_id=1, source_target_pairs={{16,0},{32,16},{48,32},{0,48},{17,1},{33,17},{49,33},{1,49},{18,2}... | collective-permute-start | bytes 92168 | tf_op jit(solution)/shard_map/ppermute | solution.py:451
  9.1 0.0 collective-permute-done.2
  9.1 1.4 %collective-permute-done.1 = f32[6,5,2,128]{3,2,1,0:T(2,128)S(1)} collective-permute-done((f32[6,5,2,128]{3,2,1,0:T(2,128)}, f32[6,5,2,128]{3,2,1,0:T(2,128)S(1)}, u32[]{:S(2)}, u32[]{:S(2)}) %collective-permute-start.1) | collective-permute-done | bytes 30752 | tf_op jit(solution)/shard_map/ppermute | solution.py:451
  10.6 1.2 %collective-permute-done = f32[6,5,2,128]{3,2,1,0:T(2,128)S(1)} collective-permute-done((f32[6,5,2,128]{3,2,1,0:T(2,128)}, f32[6,5,2,128]{3,2,1,0:T(2,128)S(1)}, u32[]{:S(2)}, u32[]{:S(2)}) %collective-permute-start) | collective-permute-done | bytes 30752 | tf_op jit(solution)/shard_map/ppermute | solution.py:451
  11.8 0.8 %pad_maximum_fusion.1 = f32[6,5,8,128]{3,2,1,0:T(8,128)S(1)} fusion(f32[6,5,2,128]{3,2,1,0:T(2,128)S(1)} %collective-permute-done.2, f32[6,5,2,128]{3,2,1,0:T(2,128)S(1)} %collective-permute-done.1, f32[6,5,2,128]{3,2,1,0:T(2,128)S(1)} %collective-permute-done, f32[6,5,2,128]{3,2,1,0:T(2,128)} %pack.1), kind=kLoop, calls=%fused_computation.1 | loop fusion | flops 92160 | bytes 245760 | tf_op jit(solution)/shard_map/concatenate | solution.py:453
  12.6 0.1 collective-permute-start.3
  12.7 1.3 %collective-permute-done.3 = f32[6,5,8,128]{3,2,1,0:T(8,128)S(1)} collective-permute-done((f32[6,5,8,128]{3,2,1,0:T(8,128)S(1)}, f32[6,5,8,128]{3,2,1,0:T(8,128)S(1)}, u32[]{:S(2)}, u32[]{:S(2)}) %collective-permute-start.3) | collective-permute-done | bytes 122912 | tf_op jit(solution)/shard_map/ppermute | solution.py:456
  14.0 0.0 copy-done
  14.0 0.1 pad_maximum_fusion.own
  14.1 5.1 %collective-permute-start.6 = (f32[12,5,8,128]{3,2,1,0:T(8,128)S(1)}, f32[12,5,8,128]{3,2,1,0:T(8,128)S(1)}, u32[]{:S(2)}, u32[]{:S(2)}) collective-permute-start(f32[12,5,8,128]{3,2,1,0:T(8,128)S(1)} %pad_maximum_fusion.own), channel_id=1, source_target_pairs={{3,0},{4,1},{5,2},{6,3},{7,4},{8,5},{9,6},{10,7},{11,8},{12,9},{13... | collective-permute-start | bytes 737288 | tf_op jit(solution)/shard_map/ppermute | solution.py:463
  19.2 2.7 %collective-permute-start.5 = (f32[12,5,8,128]{3,2,1,0:T(8,128)S(1)}, f32[12,5,8,128]{3,2,1,0:T(8,128)S(1)}, u32[]{:S(2)}, u32[]{:S(2)}) collective-permute-start(f32[12,5,8,128]{3,2,1,0:T(8,128)S(1)} %pad_maximum_fusion.own), channel_id=1, source_target_pairs={{2,0},{3,1},{4,2},{5,3},{6,4},{7,5},{8,6},{9,7},{10,8},{11,9},{12,... | collective-permute-start | bytes 737288 | tf_op jit(solution)/shard_map/ppermute | solution.py:463
  21.9 1.3 %collective-permute-start.4 = (f32[12,5,8,128]{3,2,1,0:T(8,128)S(1)}, f32[12,5,8,128]{3,2,1,0:T(8,128)S(1)}, u32[]{:S(2)}, u32[]{:S(2)}) collective-permute-start(f32[12,5,8,128]{3,2,1,0:T(8,128)S(1)} %pad_maximum_fusion.own), channel_id=1, source_target_pairs={{1,0},{2,1},{3,2},{4,3},{5,4},{6,5},{7,6},{8,7},{9,8},{10,9},{11,1... | collective-permute-start | bytes 737288 | tf_op jit(solution)/shard_map/ppermute | solution.py:463
  23.3 2.2 %collective-permute-done.6.a3 = f32[12,5,8,128]{3,2,1,0:T(8,128)S(1)} collective-permute-done((f32[12,5,8,128]{3,2,1,0:T(8,128)S(1)}, f32[12,5,8,128]{3,2,1,0:T(8,128)S(1)}, u32[]{:S(2)}, u32[]{:S(2)}) %collective-permute-start.6) | collective-permute-done | bytes 245792 | tf_op jit(solution)/shard_map/ppermute | solution.py:463
  25.5 0.0 collective-permute-start.9
  25.5 7.5 %collective-permute-done.5.a2 = f32[12,5,8,128]{3,2,1,0:T(8,128)S(1)} collective-permute-done((f32[12,5,8,128]{3,2,1,0:T(8,128)S(1)}, f32[12,5,8,128]{3,2,1,0:T(8,128)S(1)}, u32[]{:S(2)}, u32[]{:S(2)}) %collective-permute-start.5) | collective-permute-done | bytes 245792 | tf_op jit(solution)/shard_map/ppermute | solution.py:463
  33.0 0.0 collective-permute-start.8
  33.0 0.0 collective-permute-done.4.a1
  33.0 0.5 collective-permute-start.7
  33.5 0.0 collective-permute-done.9.b3
  33.5 1.0 %collective-permute-done.8.b2 = f32[12,5,8,128]{3,2,1,0:T(8,128)S(1)} collective-permute-done((f32[12,5,8,128]{3,2,1,0:T(8,128)S(1)}, f32[12,5,8,128]{3,2,1,0:T(8,128)S(1)}, u32[]{:S(2)}, u32[]{:S(2)}) %collective-permute-start.8) | collective-permute-done | bytes 245792 | tf_op jit(solution)/shard_map/ppermute | solution.py:456
  34.5 0.4 collective-permute-done.7.b1
  34.9 28.3 %region.1 = (f32[6,31,8,128]{3,2,1,0:T(8,128)S(1)}, f32[16,8,128]{2,1,0:T(8,128)S(1)}) custom-call(f32[12,5,8,128]{3,2,1,0:T(8,128)S(1)} %pad_maximum_fusion.own, f32[12,5,8,128]{3,2,1,0:T(8,128)S(1)} %collective-permute-done.4.a1, f32[12,5,8,128]{3,2,1,0:T(8,128)S(1)} %collective-permute-done.5.a2, f32[12,5,8,128]{3,2,1,0:T(8,128)S(1)} %collective-permute-done.6.a3, ...), custom_call_target="tpu_custom_call" | custom-call | tf_op jit(solution)/shard_map/region/pallas_call | solution.py:469
  63.2 12.2 %all_to_all.5.info = f32[16,8,128]{2,1,0:T(8,128)S(1)} all-to-all(f32[16,8,128]{2,1,0:T(8,128)S(1)} %get-tuple-element.9), channel_id=1, replica_groups=mesh['gx'=2,'gy'=4,'gz_0'=4,'gz_1'=4] {'gz_0','gz_1'}, dimensions={0} | all-to-all | bytes 131072 | tf_op jit(solution)/shard_map/all_to_all | solution.py:486
  75.4 2.5 %finish.1 = (f32[6,6,3,6]{3,2,1,0:T(4,128)}, f32[6,6,3,6]{3,2,1,0:T(4,128)}, f32[1,8]{1,0:T(1,128)}) custom-call(f32[6,31,8,128]{3,2,1,0:T(8,128)S(1)} %get-tuple-element.8.kept, f32[16,8,128]{2,1,0:T(8,128)S(1)} %all_to_all.5.info), custom_call_target="tpu_custom_call" | custom-call | tf_op jit(solution)/shard_map/finish/pallas_call | solution.py:488
Async XLA Ops:
  3.2 10.8 %copy-start = (f32[6,5,2,128]{3,2,1,0:T(2,128)S(1)}, f32[6,5,2,128]{3,2,1,0:T(2,128)}, u32[]{:S(2)}) copy-start(f32[6,5,2,128]{3,2,1,0:T(2,128)} %pack.1) | copy-start | bytes 92164
  3.2 5.9 %collective-permute-start.2 = (f32[6,5,2,128]{3,2,1,0:T(2,128)}, f32[6,5,2,128]{3,2,1,0:T(2,128)S(1)}, u32[]{:S(2)}, u32[]{:S(2)}) collective-permute-start(f32[6,5,2,128]{3,2,1,0:T(2,128)} %pack.1), channel_id=1, source_target_pairs={{48,0},{0,16},{16,32},{32,48},{49,1},{1,17},{17,33},{33,49},{50,2}... | collective-permute-start | bytes 92168 | tf_op jit(solution)/shard_map/ppermute | solution.py:451
  4.9 5.6 %collective-permute-start.1 = (f32[6,5,2,128]{3,2,1,0:T(2,128)}, f32[6,5,2,128]{3,2,1,0:T(2,128)S(1)}, u32[]{:S(2)}, u32[]{:S(2)}) collective-permute-start(f32[6,5,2,128]{3,2,1,0:T(2,128)} %pack.1), channel_id=1, source_target_pairs={{32,0},{48,16},{0,32},{16,48},{33,1},{49,17},{1,33},{17,49},{34,2}... | collective-permute-start | bytes 92168 | tf_op jit(solution)/shard_map/ppermute | solution.py:451
  7.7 4.1 %collective-permute-start = (f32[6,5,2,128]{3,2,1,0:T(2,128)}, f32[6,5,2,128]{3,2,1,0:T(2,128)S(1)}, u32[]{:S(2)}, u32[]{:S(2)}) collective-permute-start(f32[6,5,2,128]{3,2,1,0:T(2,128)} %pack.1), channel_id=1, source_target_pairs={{16,0},{32,16},{48,32},{0,48},{17,1},{33,17},{49,33},{1,49},{18,2}... | collective-permute-start | bytes 92168 | tf_op jit(solution)/shard_map/ppermute | solution.py:451
  12.6 1.4 %collective-permute-start.3 = (f32[6,5,8,128]{3,2,1,0:T(8,128)S(1)}, f32[6,5,8,128]{3,2,1,0:T(8,128)S(1)}, u32[]{:S(2)}, u32[]{:S(2)}) collective-permute-start(f32[6,5,8,128]{3,2,1,0:T(8,128)S(1)} %pad_maximum_fusion.1), channel_id=1, source_target_pairs={{0,64},{64,0},{1,65},{65,1},{2,66},{66,2},{3,67},{67,3},{4,68},{68... | collective-permute-start | bytes 368648 | tf_op jit(solution)/shard_map/ppermute | solution.py:456
  14.1 11.4 %collective-permute-start.6 = (f32[12,5,8,128]{3,2,1,0:T(8,128)S(1)}, f32[12,5,8,128]{3,2,1,0:T(8,128)S(1)}, u32[]{:S(2)}, u32[]{:S(2)}) collective-permute-start(f32[12,5,8,128]{3,2,1,0:T(8,128)S(1)} %pad_maximum_fusion.own), channel_id=1, source_target_pairs={{3,0},{4,1},{5,2},{6,3},{7,4},{8,5},{9,6},{10,7},{11,8},{12,9},{13... | collective-permute-start | bytes 737288 | tf_op jit(solution)/shard_map/ppermute | solution.py:463
  19.2 13.8 %collective-permute-start.5 = (f32[12,5,8,128]{3,2,1,0:T(8,128)S(1)}, f32[12,5,8,128]{3,2,1,0:T(8,128)S(1)}, u32[]{:S(2)}, u32[]{:S(2)}) collective-permute-start(f32[12,5,8,128]{3,2,1,0:T(8,128)S(1)} %pad_maximum_fusion.own), channel_id=1, source_target_pairs={{2,0},{3,1},{4,2},{5,3},{6,4},{7,5},{8,6},{9,7},{10,8},{11,9},{12,... | collective-permute-start | bytes 737288 | tf_op jit(solution)/shard_map/ppermute | solution.py:463
  21.9 11.1 %collective-permute-start.4 = (f32[12,5,8,128]{3,2,1,0:T(8,128)S(1)}, f32[12,5,8,128]{3,2,1,0:T(8,128)S(1)}, u32[]{:S(2)}, u32[]{:S(2)}) collective-permute-start(f32[12,5,8,128]{3,2,1,0:T(8,128)S(1)} %pad_maximum_fusion.own), channel_id=1, source_target_pairs={{1,0},{2,1},{3,2},{4,3},{5,4},{6,5},{7,6},{8,7},{9,8},{10,9},{11,1... | collective-permute-start | bytes 737288 | tf_op jit(solution)/shard_map/ppermute | solution.py:463
  25.5 8.0 %collective-permute-start.9 = (f32[12,5,8,128]{3,2,1,0:T(8,128)S(1)}, f32[12,5,8,128]{3,2,1,0:T(8,128)S(1)}, u32[]{:S(2)}, u32[]{:S(2)}) collective-permute-start(f32[12,5,8,128]{3,2,1,0:T(8,128)S(1)} %collective-permute-done.6.a3), channel_id=1, source_target_pairs={{0,64},{64,0},{1,65},{65,1},{2,66},{66,2},{3,67},{67,3},{4,68},{68... | collective-permute-start | bytes 737288 | tf_op jit(solution)/shard_map/ppermute | solution.py:456
  33.0 1.5 %collective-permute-start.8 = (f32[12,5,8,128]{3,2,1,0:T(8,128)S(1)}, f32[12,5,8,128]{3,2,1,0:T(8,128)S(1)}, u32[]{:S(2)}, u32[]{:S(2)}) collective-permute-start(f32[12,5,8,128]{3,2,1,0:T(8,128)S(1)} %collective-permute-done.5.a2), channel_id=1, source_target_pairs={{0,64},{64,0},{1,65},{65,1},{2,66},{66,2},{3,67},{67,3},{4,68},{68... | collective-permute-start | bytes 737288 | tf_op jit(solution)/shard_map/ppermute | solution.py:456
  33.0 1.9 %collective-permute-start.7 = (f32[12,5,8,128]{3,2,1,0:T(8,128)S(1)}, f32[12,5,8,128]{3,2,1,0:T(8,128)S(1)}, u32[]{:S(2)}, u32[]{:S(2)}) collective-permute-start(f32[12,5,8,128]{3,2,1,0:T(8,128)S(1)} %collective-permute-done.4.a1), channel_id=1, source_target_pairs={{0,64},{64,0},{1,65},{65,1},{2,66},{66,2},{3,67},{67,3},{4,68},{68... | collective-permute-start | bytes 737288 | tf_op jit(solution)/shard_map/ppermute | solution.py:456

commit v7 on v6

--- a/solution.py
+++ b/solution.py
@@ -5,6 +5,7 @@
 from jax.experimental.pallas import tpu as pltpu
 from jax.sharding import Mesh
 from jax.sharding import PartitionSpec as P
+
 
 ITERS = 8
 BASIS = ITERS + 1
@@ -447,9 +448,9 @@
         name="pack",
     )(permanent_field.transpose(0, 1, 3, 2), polar, jitter.transpose(0, 1, 3, 2), neighbors)
 
-    around = [packed] + [
-        lax.ppermute(packed, "gy", [((i + k) % 4, i) for i in range(4)]) for k in (1, 2, 3)
-    ]
+    around = [packed]
+    for k in (1, 2, 3):
+        around.append(lax.ppermute(packed, "gy", [((i + k) % 4, i) for i in range(4)]))
     half = jnp.concatenate(around, axis=2)
 
     def swap(v):
@@ -463,7 +464,9 @@
         return lax.ppermute(own, ("gx",) + GZ, pairs)
 
     direct = [fetch(k) for k in (1, 2, 3)]
-    passed = [swap(v) for v in direct]
+    passed = []
+    for v in direct:
+        passed.append(swap(v))
 
     vreg = (8, 128)
     kept, info = pl.pallas_call(

time: 78.1 us -> 77.5 us (level)
  no operation moved by 1% of the time
where the time goes in v7:
time: 77.5 us; the launch traced here: 77.3 us
  Pallas kernels  33.4 us (43%)
  starting transfers between devices  15.6 us (20%)
  waiting for transfers between devices  15.1 us (19%)
  blocking collectives  11.6 us (15%)
  other arithmetic  0.88 us (1%)
    pallas_call x1, Pallas kernels, per_device(): pl.pallas_call(region_kernel, out_shape=(jax.ShapeDtypeStruct((EDGE, 31)...  28.3 us
    all_to_all x1, blocking collectives, per_device(): info = lax.all_to_all(info, GZ, 0, 0, tiled=True)  11.6 us
    ppermute x3, waiting for transfers between devices, fetch(): return lax.ppermute(own, ('gx',) + GZ, pairs)  9.73 us
    ppermute x3, starting transfers between devices, fetch(): return lax.ppermute(own, ('gx',) + GZ, pairs)  9.21 us
    ppermute x3, starting transfers between devices, per_device(): lax.ppermute(packed, 'gy', [((i + k) % 4, i) for i in range(4)])  5.83 us
    ppermute x4, waiting for transfers between devices, swap(): return lax.ppermute(v, 'gx', [(0, 1), (1, 0)])  2.67 us
    ppermute x3, waiting for transfers between devices, per_device(): lax.ppermute(packed, 'gy', [((i + k) % 4, i) for i in range(4)])  2.67 us
    pallas_call x1, Pallas kernels, per_device(): pl.pallas_call(pack_kernel, out_shape=jax.ShapeDtypeStruct((EDGE, GROUPS,...  2.59 us
  transfers between devices with their start and end apart: 10, of which 7 were waited for; matrix products, arithmetic and copies ran while one was open for 0% of the time, Pallas kernels for 0%

profile of v7, /device:TPU:0, one launch (start us, length us, event | category | flops | bytes accessed | tf_op | source)
XLA Modules:
  0.0 77.3 jit_solution(12692493219520890723)
XLA Ops:
  0.6 2.6 %pack.1 = f32[6,5,2,128]{3,2,1,0:T(2,128)} custom-call(f32[6,6,3,6]{3,2,1,0:T(4,128)} %bitcast.5, f32[6,6,6]{2,1,0:T(8,128)} %polar_in.1, f32[6,6,3,6]{3,2,1,0:T(4,128)} %bitcast.6, s32[6,6,6,56]{3,2,1,0:T(8,128)} %neighbors_in.1), custom_call_target="tpu_custom_call" | custom-call | tf_op jit(solution)/shard_map/pack/pallas_call | solution.py:436
  3.2 0.0 copy-start
  3.2 1.7 %collective-permute-start.2 = (f32[6,5,2,128]{3,2,1,0:T(2,128)}, f32[6,5,2,128]{3,2,1,0:T(2,128)S(1)}, u32[]{:S(2)}, u32[]{:S(2)}) collective-permute-start(f32[6,5,2,128]{3,2,1,0:T(2,128)} %pack.1), channel_id=1, source_target_pairs={{48,0},{0,16},{16,32},{32,48},{49,1},{1,17},{17,33},{33,49},{50,2}... | collective-permute-start | bytes 92168 | tf_op jit(solution)/shard_map/ppermute | solution.py:453
  4.9 2.7 %collective-permute-start.1 = (f32[6,5,2,128]{3,2,1,0:T(2,128)}, f32[6,5,2,128]{3,2,1,0:T(2,128)S(1)}, u32[]{:S(2)}, u32[]{:S(2)}) collective-permute-start(f32[6,5,2,128]{3,2,1,0:T(2,128)} %pack.1), channel_id=1, source_target_pairs={{32,0},{48,16},{0,32},{16,48},{33,1},{49,17},{1,33},{17,49},{34,2}... | collective-permute-start | bytes 92168 | tf_op jit(solution)/shard_map/ppermute | solution.py:453
  7.6 1.4 %collective-permute-start = (f32[6,5,2,128]{3,2,1,0:T(2,128)}, f32[6,5,2,128]{3,2,1,0:T(2,128)S(1)}, u32[]{:S(2)}, u32[]{:S(2)}) collective-permute-start(f32[6,5,2,128]{3,2,1,0:T(2,128)} %pack.1), channel_id=1, source_target_pairs={{16,0},{32,16},{48,32},{0,48},{17,1},{33,17},{49,33},{1,49},{18,2}... | collective-permute-start | bytes 92168 | tf_op jit(solution)/shard_map/ppermute | solution.py:453
  9.1 0.0 collective-permute-done.2
  9.1 1.4 %collective-permute-done.1 = f32[6,5,2,128]{3,2,1,0:T(2,128)S(1)} collective-permute-done((f32[6,5,2,128]{3,2,1,0:T(2,128)}, f32[6,5,2,128]{3,2,1,0:T(2,128)S(1)}, u32[]{:S(2)}, u32[]{:S(2)}) %collective-permute-start.1) | collective-permute-done | bytes 30752 | tf_op jit(solution)/shard_map/ppermute | solution.py:453
  10.5 1.2 %collective-permute-done = f32[6,5,2,128]{3,2,1,0:T(2,128)S(1)} collective-permute-done((f32[6,5,2,128]{3,2,1,0:T(2,128)}, f32[6,5,2,128]{3,2,1,0:T(2,128)S(1)}, u32[]{:S(2)}, u32[]{:S(2)}) %collective-permute-start) | collective-permute-done | bytes 30752 | tf_op jit(solution)/shard_map/ppermute | solution.py:453
  11.7 0.8 %pad_maximum_fusion.1 = f32[6,5,8,128]{3,2,1,0:T(8,128)S(1)} fusion(f32[6,5,2,128]{3,2,1,0:T(2,128)S(1)} %collective-permute-done.2, f32[6,5,2,128]{3,2,1,0:T(2,128)S(1)} %collective-permute-done.1, f32[6,5,2,128]{3,2,1,0:T(2,128)S(1)} %collective-permute-done, f32[6,5,2,128]{3,2,1,0:T(2,128)} %pack.1), kind=kLoop, calls=%fused_computation.1 | loop fusion | flops 92160 | bytes 245760 | tf_op jit(solution)/shard_map/concatenate | solution.py:454
  12.6 0.1 collective-permute-start.3
  12.7 1.3 %collective-permute-done.3 = f32[6,5,8,128]{3,2,1,0:T(8,128)S(1)} collective-permute-done((f32[6,5,8,128]{3,2,1,0:T(8,128)S(1)}, f32[6,5,8,128]{3,2,1,0:T(8,128)S(1)}, u32[]{:S(2)}, u32[]{:S(2)}) %collective-permute-start.3) | collective-permute-done | bytes 122912 | tf_op jit(solution)/shard_map/ppermute | solution.py:457
  14.0 0.0 copy-done
  14.0 0.1 pad_maximum_fusion.own
  14.1 5.1 %collective-permute-start.6 = (f32[12,5,8,128]{3,2,1,0:T(8,128)S(1)}, f32[12,5,8,128]{3,2,1,0:T(8,128)S(1)}, u32[]{:S(2)}, u32[]{:S(2)}) collective-permute-start(f32[12,5,8,128]{3,2,1,0:T(8,128)S(1)} %pad_maximum_fusion.own), channel_id=1, source_target_pairs={{3,0},{4,1},{5,2},{6,3},{7,4},{8,5},{9,6},{10,7},{11,8},{12,9},{13... | collective-permute-start | bytes 737288 | tf_op jit(solution)/shard_map/ppermute | solution.py:464
  19.2 2.7 %collective-permute-start.5 = (f32[12,5,8,128]{3,2,1,0:T(8,128)S(1)}, f32[12,5,8,128]{3,2,1,0:T(8,128)S(1)}, u32[]{:S(2)}, u32[]{:S(2)}) collective-permute-start(f32[12,5,8,128]{3,2,1,0:T(8,128)S(1)} %pad_maximum_fusion.own), channel_id=1, source_target_pairs={{2,0},{3,1},{4,2},{5,3},{6,4},{7,5},{8,6},{9,7},{10,8},{11,9},{12,... | collective-permute-start | bytes 737288 | tf_op jit(solution)/shard_map/ppermute | solution.py:464
  21.9 1.3 %collective-permute-start.4 = (f32[12,5,8,128]{3,2,1,0:T(8,128)S(1)}, f32[12,5,8,128]{3,2,1,0:T(8,128)S(1)}, u32[]{:S(2)}, u32[]{:S(2)}) collective-permute-start(f32[12,5,8,128]{3,2,1,0:T(8,128)S(1)} %pad_maximum_fusion.own), channel_id=1, source_target_pairs={{1,0},{2,1},{3,2},{4,3},{5,4},{6,5},{7,6},{8,7},{9,8},{10,9},{11,1... | collective-permute-start | bytes 737288 | tf_op jit(solution)/shard_map/ppermute | solution.py:464
  23.3 2.3 %collective-permute-done.6.a3 = f32[12,5,8,128]{3,2,1,0:T(8,128)S(1)} collective-permute-done((f32[12,5,8,128]{3,2,1,0:T(8,128)S(1)}, f32[12,5,8,128]{3,2,1,0:T(8,128)S(1)}, u32[]{:S(2)}, u32[]{:S(2)}) %collective-permute-start.6) | collective-permute-done | bytes 245792 | tf_op jit(solution)/shard_map/ppermute | solution.py:464
  25.5 0.0 collective-permute-start.9
  25.5 7.5 %collective-permute-done.5.a2 = f32[12,5,8,128]{3,2,1,0:T(8,128)S(1)} collective-permute-done((f32[12,5,8,128]{3,2,1,0:T(8,128)S(1)}, f32[12,5,8,128]{3,2,1,0:T(8,128)S(1)}, u32[]{:S(2)}, u32[]{:S(2)}) %collective-permute-start.5) | collective-permute-done | bytes 245792 | tf_op jit(solution)/shard_map/ppermute | solution.py:464
  33.0 0.0 collective-permute-start.8
  33.0 0.0 collective-permute-done.4.a1
  33.0 0.5 collective-permute-start.7
  33.5 0.0 collective-permute-done.9.b3
  33.5 1.0 %collective-permute-done.8.b2 = f32[12,5,8,128]{3,2,1,0:T(8,128)S(1)} collective-permute-done((f32[12,5,8,128]{3,2,1,0:T(8,128)S(1)}, f32[12,5,8,128]{3,2,1,0:T(8,128)S(1)}, u32[]{:S(2)}, u32[]{:S(2)}) %collective-permute-start.8) | collective-permute-done | bytes 245792 | tf_op jit(solution)/shard_map/ppermute | solution.py:457
  34.5 0.4 collective-permute-done.7.b1
  34.9 28.3 %region.1 = (f32[6,31,8,128]{3,2,1,0:T(8,128)S(1)}, f32[16,8,128]{2,1,0:T(8,128)S(1)}) custom-call(f32[12,5,8,128]{3,2,1,0:T(8,128)S(1)} %pad_maximum_fusion.own, f32[12,5,8,128]{3,2,1,0:T(8,128)S(1)} %collective-permute-done.4.a1, f32[12,5,8,128]{3,2,1,0:T(8,128)S(1)} %collective-permute-done.5.a2, f32[12,5,8,128]{3,2,1,0:T(8,128)S(1)} %collective-permute-done.6.a3, ...), custom_call_target="tpu_custom_call" | custom-call | tf_op jit(solution)/shard_map/region/pallas_call | solution.py:472
  63.2 11.6 %all_to_all.5.info = f32[16,8,128]{2,1,0:T(8,128)S(1)} all-to-all(f32[16,8,128]{2,1,0:T(8,128)S(1)} %get-tuple-element.9), channel_id=1, replica_groups=mesh['gx'=2,'gy'=4,'gz_0'=4,'gz_1'=4] {'gz_0','gz_1'}, dimensions={0} | all-to-all | bytes 131072 | tf_op jit(solution)/shard_map/all_to_all | solution.py:489
  74.8 2.5 %finish.1 = (f32[6,6,3,6]{3,2,1,0:T(4,128)}, f32[6,6,3,6]{3,2,1,0:T(4,128)}, f32[1,8]{1,0:T(1,128)}) custom-call(f32[6,31,8,128]{3,2,1,0:T(8,128)S(1)} %get-tuple-element.8.kept, f32[16,8,128]{2,1,0:T(8,128)S(1)} %all_to_all.5.info), custom_call_target="tpu_custom_call" | custom-call | tf_op jit(solution)/shard_map/finish/pallas_call | solution.py:491
Async XLA Ops:
  3.2 10.8 %copy-start = (f32[6,5,2,128]{3,2,1,0:T(2,128)S(1)}, f32[6,5,2,128]{3,2,1,0:T(2,128)}, u32[]{:S(2)}) copy-start(f32[6,5,2,128]{3,2,1,0:T(2,128)} %pack.1) | copy-start | bytes 92164
  3.2 5.8 %collective-permute-start.2 = (f32[6,5,2,128]{3,2,1,0:T(2,128)}, f32[6,5,2,128]{3,2,1,0:T(2,128)S(1)}, u32[]{:S(2)}, u32[]{:S(2)}) collective-permute-start(f32[6,5,2,128]{3,2,1,0:T(2,128)} %pack.1), channel_id=1, source_target_pairs={{48,0},{0,16},{16,32},{32,48},{49,1},{1,17},{17,33},{33,49},{50,2}... | collective-permute-start | bytes 92168 | tf_op jit(solution)/shard_map/ppermute | solution.py:453
  4.9 5.6 %collective-permute-start.1 = (f32[6,5,2,128]{3,2,1,0:T(2,128)}, f32[6,5,2,128]{3,2,1,0:T(2,128)S(1)}, u32[]{:S(2)}, u32[]{:S(2)}) collective-permute-start(f32[6,5,2,128]{3,2,1,0:T(2,128)} %pack.1), channel_id=1, source_target_pairs={{32,0},{48,16},{0,32},{16,48},{33,1},{49,17},{1,33},{17,49},{34,2}... | collective-permute-start | bytes 92168 | tf_op jit(solution)/shard_map/ppermute | solution.py:453
  7.6 4.1 %collective-permute-start = (f32[6,5,2,128]{3,2,1,0:T(2,128)}, f32[6,5,2,128]{3,2,1,0:T(2,128)S(1)}, u32[]{:S(2)}, u32[]{:S(2)}) collective-permute-start(f32[6,5,2,128]{3,2,1,0:T(2,128)} %pack.1), channel_id=1, source_target_pairs={{16,0},{32,16},{48,32},{0,48},{17,1},{33,17},{49,33},{1,49},{18,2}... | collective-permute-start | bytes 92168 | tf_op jit(solution)/shard_map/ppermute | solution.py:453
  12.6 1.4 %collective-permute-start.3 = (f32[6,5,8,128]{3,2,1,0:T(8,128)S(1)}, f32[6,5,8,128]{3,2,1,0:T(8,128)S(1)}, u32[]{:S(2)}, u32[]{:S(2)}) collective-permute-start(f32[6,5,8,128]{3,2,1,0:T(8,128)S(1)} %pad_maximum_fusion.1), channel_id=1, source_target_pairs={{0,64},{64,0},{1,65},{65,1},{2,66},{66,2},{3,67},{67,3},{4,68},{68... | collective-permute-start | bytes 368648 | tf_op jit(solution)/shard_map/ppermute | solution.py:457
  14.1 11.5 %collective-permute-start.6 = (f32[12,5,8,128]{3,2,1,0:T(8,128)S(1)}, f32[12,5,8,128]{3,2,1,0:T(8,128)S(1)}, u32[]{:S(2)}, u32[]{:S(2)}) collective-permute-start(f32[12,5,8,128]{3,2,1,0:T(8,128)S(1)} %pad_maximum_fusion.own), channel_id=1, source_target_pairs={{3,0},{4,1},{5,2},{6,3},{7,4},{8,5},{9,6},{10,7},{11,8},{12,9},{13... | collective-permute-start | bytes 737288 | tf_op jit(solution)/shard_map/ppermute | solution.py:464
  19.2 13.8 %collective-permute-start.5 = (f32[12,5,8,128]{3,2,1,0:T(8,128)S(1)}, f32[12,5,8,128]{3,2,1,0:T(8,128)S(1)}, u32[]{:S(2)}, u32[]{:S(2)}) collective-permute-start(f32[12,5,8,128]{3,2,1,0:T(8,128)S(1)} %pad_maximum_fusion.own), channel_id=1, source_target_pairs={{2,0},{3,1},{4,2},{5,3},{6,4},{7,5},{8,6},{9,7},{10,8},{11,9},{12,... | collective-permute-start | bytes 737288 | tf_op jit(solution)/shard_map/ppermute | solution.py:464
  21.9 11.1 %collective-permute-start.4 = (f32[12,5,8,128]{3,2,1,0:T(8,128)S(1)}, f32[12,5,8,128]{3,2,1,0:T(8,128)S(1)}, u32[]{:S(2)}, u32[]{:S(2)}) collective-permute-start(f32[12,5,8,128]{3,2,1,0:T(8,128)S(1)} %pad_maximum_fusion.own), channel_id=1, source_target_pairs={{1,0},{2,1},{3,2},{4,3},{5,4},{6,5},{7,6},{8,7},{9,8},{10,9},{11,1... | collective-permute-start | bytes 737288 | tf_op jit(solution)/shard_map/ppermute | solution.py:464
  25.5 8.0 %collective-permute-start.9 = (f32[12,5,8,128]{3,2,1,0:T(8,128)S(1)}, f32[12,5,8,128]{3,2,1,0:T(8,128)S(1)}, u32[]{:S(2)}, u32[]{:S(2)}) collective-permute-start(f32[12,5,8,128]{3,2,1,0:T(8,128)S(1)} %collective-permute-done.6.a3), channel_id=1, source_target_pairs={{0,64},{64,0},{1,65},{65,1},{2,66},{66,2},{3,67},{67,3},{4,68},{68... | collective-permute-start | bytes 737288 | tf_op jit(solution)/shard_map/ppermute | solution.py:457
  33.0 1.5 %collective-permute-start.8 = (f32[12,5,8,128]{3,2,1,0:T(8,128)S(1)}, f32[12,5,8,128]{3,2,1,0:T(8,128)S(1)}, u32[]{:S(2)}, u32[]{:S(2)}) collective-permute-start(f32[12,5,8,128]{3,2,1,0:T(8,128)S(1)} %collective-permute-done.5.a2), channel_id=1, source_target_pairs={{0,64},{64,0},{1,65},{65,1},{2,66},{66,2},{3,67},{67,3},{4,68},{68... | collective-permute-start | bytes 737288 | tf_op jit(solution)/shard_map/ppermute | solution.py:457
  33.0 1.9 %collective-permute-start.7 = (f32[12,5,8,128]{3,2,1,0:T(8,128)S(1)}, f32[12,5,8,128]{3,2,1,0:T(8,128)S(1)}, u32[]{:S(2)}, u32[]{:S(2)}) collective-permute-start(f32[12,5,8,128]{3,2,1,0:T(8,128)S(1)} %collective-permute-done.4.a1), channel_id=1, source_target_pairs={{0,64},{64,0},{1,65},{65,1},{2,66},{66,2},{3,67},{67,3},{4,68},{68... | collective-permute-start | bytes 737288 | tf_op jit(solution)/shard_map/ppermute | solution.py:457

commit v8 on v6

--- a/solution.py
+++ b/solution.py
@@ -25,6 +25,9 @@
 ]
 FORWARD = [d for d in OFFSETS if d > (0, 0, 0)]
 GROUPS, PER = 5, 7
+
+
+FIRSTS = {min(n for n, d in enumerate(FORWARD) if d[2] == dz) for dz in range(-2, 3)}
 
 
 def lane_iota():
@@ -66,6 +69,8 @@
 
 
 def wrap(x):
+    if isinstance(x, int):
+        return x % NX
     return jnp.where(x >= NX, x - NX, jnp.where(x < 0, x + NX, x))
 
 
@@ -148,6 +153,7 @@
 
 def region_kernel(
     own, a1, a2, a3, b1, b2, b3, kept_out, info_out, chan, near, coef, moved, basis,
+    raw, now, past,
 ):
     gx = lax.axis_index("gx")
     gy = lax.axis_index("gy")
@@ -185,7 +191,7 @@
                 chan[x, group * PER + member] = acc
         return carry
 
-    lax.fori_loop(0, NX, gather, 0)
+    unrolled(NX, 2, gather, 0)
 
     def spread(x, carry):
         for c in range(4):
@@ -197,11 +203,12 @@
     unrolled(NX, 3, spread, 0)
 
     def pairs(x, carry):
-        home = {dz: [roll_lanes(chan[x, 3 + c], -dz) for c in range(4)] for dz in range(-2, 3)}
-        for number, d in enumerate(FORWARD):
+        for number, d in sorted(enumerate(FORWARD), key=lambda t: t[1][2]):
+            if number in FIRSTS:
+                home = [roll_lanes(chan[x, 3 + c], -d[2]) for c in range(4)]
             other = wrap(x + d[0])
             place = (d[1] + 2) * 4
-            polar, *jit = home[d[2]]
+            polar, *jit = home
             sep = [((near[other, place + 1 + c] - jit[c]) + float(d[c])) * SPACING for c in range(3)]
             dist_sq = sep[0] * sep[0] + sep[1] * sep[1] + sep[2] * sep[2]
             over = lax.rsqrt(dist_sq)
@@ -251,74 +258,71 @@
     zero = jnp.zeros((8, 128), F32)
     slab = (along >= 18) & (along < 24)
 
-    def start(x, carry):
+    def prepare(x, carry):
         for c in range(3):
-            move(x, c, chan[x, 3] * chan[x, c])
-        return carry
-
-    unrolled(NX, 4, start, 0)
-
-    def begin(x, carry):
-        out = couple(x)
-        polar = chan[x, 3]
-        for c in range(3):
-            basis[0, x * 3 + c] = zero
-            basis[1, x * 3 + c] = polar * out[c]
-        return carry
-
-    unrolled(NX, 3, begin, 0)
-
-    def again(x, carry):
-        for c in range(3):
-            move(x, c, basis[1, x * 3 + c])
-        return carry
-
-    unrolled(NX, 4, again, 0)
+            raw[x * 3 + c] = chan[x, 3] * chan[x, c]
+            now[x * 3 + c] = zero
+            past[x * 3 + c] = zero
+        return carry
+
+    unrolled(NX, 4, prepare, 0)
+
+    def next_vector(x, c, al, be, sc):
+        return (raw[x * 3 + c] - al * now[x * 3 + c] - be * past[x * 3 + c]) * sc
 
     def extend(k, carry):
-        info, before = carry
-
-        def one(x, sums):
+        info, before, al, be, sc = carry
+        sums = [zero] * 4
+
+        def scale(x):
+            for c in range(3):
+                new = next_vector(x, c, al, be, sc)
+                past[x * 3 + c] = now[x * 3 + c]
+                now[x * 3 + c] = new
+                basis[k, x * 3 + c] = new
+                move(x, c, new)
+
+        for x in (10, 11, 0, 1, 2):
+            scale(x)
+        for x in range(NX):
+            if 3 <= x + 3 < 10:
+                scale(x + 3)
             out = couple(x)
             polar = chan[x, 3]
             over = chan[x, 35]
-            sums = list(sums)
             for c in range(3):
-                u = basis[k + 1, x * 3 + c]
+                u = now[x * 3 + c]
                 w = polar * out[c]
-                basis[k + 2, x * 3 + c] = w
+                raw[x * 3 + c] = w
                 sums[0] = sums[0] + out[c] * u
-                sums[1] = sums[1] + out[c] * basis[k, x * 3 + c]
+                sums[1] = sums[1] + out[c] * past[x * 3 + c]
                 sums[2] = sums[2] + out[c] * w
                 sums[3] = sums[3] + (u * over) * u
-            return tuple(sums)
-
-        sums = unrolled(NX, 3, one, (zero,) * 4)
-        now, past, full, norm = [total(jnp.where(slab, s, 0.0)) for s in sums]
+        along_now, along_past, full, norm = [total(jnp.where(slab, t, 0.0)) for t in sums]
+        live = k > 0
+        norm = jnp.where(live, norm, 0.0)
         tiny = 1e-36
-        al = jnp.where(norm > tiny, now / jnp.maximum(norm, tiny), 0.0)
-        be = jnp.where(before > tiny, past / jnp.maximum(before, tiny), 0.0)
-        rest = full - al * now - be * past
+        al = jnp.where(norm > tiny, along_now / jnp.maximum(norm, tiny), 0.0)
+        be = jnp.where(before > tiny, along_past / jnp.maximum(before, tiny), 0.0)
+        rest = full - al * along_now - be * along_past
         rest = jnp.maximum(rest, 1e-10 * full)
         good = (rest > tiny) & (norm > tiny)
         inv = jnp.where(good, jnp.sqrt(rest / jnp.maximum(norm, tiny)), 1.0)
         inv = jnp.minimum(jnp.maximum(inv, 1e-6), 1e3)
-        sc = 1.0 / inv
-
-        def scale(x, carry):
-            for c in range(3):
-                at = x * 3 + c
-                new = (basis[k + 2, at] - al * basis[k + 1, at] - be * basis[k, at]) * sc
-                basis[k + 2, at] = new
-                move(x, c, new)
-            return carry
-
-        unrolled(NX, 4, scale, 0)
-        info = jnp.where(lane == 45 + k, al, info)
-        info = jnp.where(lane == 53 + k, be, info)
-        return jnp.where(lane == 61 + k, inv, info), norm
-
-    info, _ = lax.fori_loop(0, ITERS, extend, (zero, jnp.zeros((1, 1), F32)))
+        info = jnp.where(lane == 44 + k, jnp.where(live, al, info), info)
+        info = jnp.where(lane == 52 + k, jnp.where(live, be, info), info)
+        info = jnp.where(lane == 60 + k, jnp.where(live, inv, info), info)
+        return info, norm, al, be, 1.0 / inv
+
+    none = jnp.zeros((1, 1), F32)
+    info, _, al, be, sc = lax.fori_loop(0, BASIS, extend, (zero, none, none, none, none + 1.0))
+
+    def end(x, carry):
+        for c in range(3):
+            basis[BASIS, x * 3 + c] = next_vector(x, c, al, be, sc)
+        return carry
+
+    unrolled(NX, 4, end, 0)
 
     number = 0
     for low, high in ((0, 3), (3, BASIS)):
@@ -352,7 +356,7 @@
         for c in range(3):
             for k in range(BASIS):
                 kept_out[x, k * 3 + c] = front(basis[k + 1, far * 3 + c])
-            kept_out[x, 27 + c] = front(chan[far, 3] * chan[far, c])
+            kept_out[x, 27 + c] = front(basis[0, far * 3 + c])
         kept_out[x, 30] = front(chan[far, 35])
         return carry
 
@@ -478,6 +482,9 @@
             pltpu.VMEM((NX, 4 * len(OFFSETS)) + vreg, F32),
             pltpu.VMEM((NX, 16) + vreg, F32),
             pltpu.VMEM((BASIS + 1, 3 * NX) + vreg, F32),
+            pltpu.VMEM((3 * NX,) + vreg, F32),
+            pltpu.VMEM((3 * NX,) + vreg, F32),
+            pltpu.VMEM((3 * NX,) + vreg, F32),
         ],
         compiler_params=pltpu.CompilerParams(vmem_limit_bytes=36 * 1024 * 1024),
         name="region",

time: 78.1 us -> 74.2 us (0.950)
  Pallas kernels: 33.4 us -> 29.5 us
    pallas_call x1, Pallas kernels: 28.3 us -> 24.4 us  [per_device(): pl.pallas_call(region_kernel, out_shape=(jax.ShapeDtypeStruct((EDGE, 31)...]
where the time goes in v8:
time: 74.2 us; the launch traced here: 74 us
  Pallas kernels  29.5 us (40%)
  starting transfers between devices  15.7 us (21%)
  waiting for transfers between devices  15.1 us (20%)
  blocking collectives  12.2 us (16%)
  other arithmetic  0.88 us (1%)
    pallas_call x1, Pallas kernels, per_device(): pl.pallas_call(region_kernel, out_shape=(jax.ShapeDtypeStruct((EDGE, 31)...  24.4 us
    all_to_all x1, blocking collectives, per_device(): info = lax.all_to_all(info, GZ, 0, 0, tiled=True)  12.2 us
    ppermute x3, waiting for transfers between devices, fetch(): return lax.ppermute(own, ('gx',) + GZ, pairs)  9.73 us
    ppermute x3, starting transfers between devices, fetch(): return lax.ppermute(own, ('gx',) + GZ, pairs)  9.21 us
    ppermute x3, starting transfers between devices, per_device(): lax.ppermute(packed, 'gy', [((i + k) % 4, i) for i in range(4)])  5.87 us
    ppermute x4, waiting for transfers between devices, swap(): return lax.ppermute(v, 'gx', [(0, 1), (1, 0)])  2.67 us
    ppermute x3, waiting for transfers between devices, per_device(): lax.ppermute(packed, 'gy', [((i + k) % 4, i) for i in range(4)])  2.67 us
    pallas_call x1, Pallas kernels, per_device(): pl.pallas_call(pack_kernel, out_shape=jax.ShapeDtypeStruct((EDGE, GROUPS,...  2.59 us
  transfers between devices with their start and end apart: 10, of which 7 were waited for; matrix products, arithmetic and copies ran while one was open for 0% of the time, Pallas kernels for 0%

profile of v8, /device:TPU:0, one launch (start us, length us, event | category | flops | bytes accessed | tf_op | source)
XLA Modules:
  0.0 74.0 jit_solution(10457948177809974954)
XLA Ops:
  0.6 2.6 %pack.1 = f32[6,5,2,128]{3,2,1,0:T(2,128)} custom-call(f32[6,6,3,6]{3,2,1,0:T(4,128)} %bitcast.5, f32[6,6,6]{2,1,0:T(8,128)} %polar_in.1, f32[6,6,3,6]{3,2,1,0:T(4,128)} %bitcast.6, s32[6,6,6,56]{3,2,1,0:T(8,128)} %neighbors_in.1), custom_call_target="tpu_custom_call" | custom-call | tf_op jit(solution)/shard_map/pack/pallas_call | solution.py:439
  3.2 0.0 copy-start
  3.2 1.7 %collective-permute-start.2 = (f32[6,5,2,128]{3,2,1,0:T(2,128)}, f32[6,5,2,128]{3,2,1,0:T(2,128)S(1)}, u32[]{:S(2)}, u32[]{:S(2)}) collective-permute-start(f32[6,5,2,128]{3,2,1,0:T(2,128)} %pack.1), channel_id=1, source_target_pairs={{48,0},{0,16},{16,32},{32,48},{49,1},{1,17},{17,33},{33,49},{50,2}... | collective-permute-start | bytes 92168 | tf_op jit(solution)/shard_map/ppermute | solution.py:455
  4.9 2.7 %collective-permute-start.1 = (f32[6,5,2,128]{3,2,1,0:T(2,128)}, f32[6,5,2,128]{3,2,1,0:T(2,128)S(1)}, u32[]{:S(2)}, u32[]{:S(2)}) collective-permute-start(f32[6,5,2,128]{3,2,1,0:T(2,128)} %pack.1), channel_id=1, source_target_pairs={{32,0},{48,16},{0,32},{16,48},{33,1},{49,17},{1,33},{17,49},{34,2}... | collective-permute-start | bytes 92168 | tf_op jit(solution)/shard_map/ppermute | solution.py:455
  7.7 1.4 %collective-permute-start = (f32[6,5,2,128]{3,2,1,0:T(2,128)}, f32[6,5,2,128]{3,2,1,0:T(2,128)S(1)}, u32[]{:S(2)}, u32[]{:S(2)}) collective-permute-start(f32[6,5,2,128]{3,2,1,0:T(2,128)} %pack.1), channel_id=1, source_target_pairs={{16,0},{32,16},{48,32},{0,48},{17,1},{33,17},{49,33},{1,49},{18,2}... | collective-permute-start | bytes 92168 | tf_op jit(solution)/shard_map/ppermute | solution.py:455
  9.1 0.0 collective-permute-done.2
  9.1 1.4 %collective-permute-done.1 = f32[6,5,2,128]{3,2,1,0:T(2,128)S(1)} collective-permute-done((f32[6,5,2,128]{3,2,1,0:T(2,128)}, f32[6,5,2,128]{3,2,1,0:T(2,128)S(1)}, u32[]{:S(2)}, u32[]{:S(2)}) %collective-permute-start.1) | collective-permute-done | bytes 30752 | tf_op jit(solution)/shard_map/ppermute | solution.py:455
  10.6 1.2 %collective-permute-done = f32[6,5,2,128]{3,2,1,0:T(2,128)S(1)} collective-permute-done((f32[6,5,2,128]{3,2,1,0:T(2,128)}, f32[6,5,2,128]{3,2,1,0:T(2,128)S(1)}, u32[]{:S(2)}, u32[]{:S(2)}) %collective-permute-start) | collective-permute-done | bytes 30752 | tf_op jit(solution)/shard_map/ppermute | solution.py:455
  11.8 0.8 %pad_maximum_fusion.1 = f32[6,5,8,128]{3,2,1,0:T(8,128)S(1)} fusion(f32[6,5,2,128]{3,2,1,0:T(2,128)S(1)} %collective-permute-done.2, f32[6,5,2,128]{3,2,1,0:T(2,128)S(1)} %collective-permute-done.1, f32[6,5,2,128]{3,2,1,0:T(2,128)S(1)} %collective-permute-done, f32[6,5,2,128]{3,2,1,0:T(2,128)} %pack.1), kind=kLoop, calls=%fused_computation.1 | loop fusion | flops 92160 | bytes 245760 | tf_op jit(solution)/shard_map/concatenate | solution.py:457
  12.6 0.1 collective-permute-start.3
  12.7 1.3 %collective-permute-done.3 = f32[6,5,8,128]{3,2,1,0:T(8,128)S(1)} collective-permute-done((f32[6,5,8,128]{3,2,1,0:T(8,128)S(1)}, f32[6,5,8,128]{3,2,1,0:T(8,128)S(1)}, u32[]{:S(2)}, u32[]{:S(2)}) %collective-permute-start.3) | collective-permute-done | bytes 122912 | tf_op jit(solution)/shard_map/ppermute | solution.py:460
  14.0 0.0 copy-done
  14.0 0.1 pad_maximum_fusion.own
  14.1 5.1 %collective-permute-start.6 = (f32[12,5,8,128]{3,2,1,0:T(8,128)S(1)}, f32[12,5,8,128]{3,2,1,0:T(8,128)S(1)}, u32[]{:S(2)}, u32[]{:S(2)}) collective-permute-start(f32[12,5,8,128]{3,2,1,0:T(8,128)S(1)} %pad_maximum_fusion.own), channel_id=1, source_target_pairs={{3,0},{4,1},{5,2},{6,3},{7,4},{8,5},{9,6},{10,7},{11,8},{12,9},{13... | collective-permute-start | bytes 737288 | tf_op jit(solution)/shard_map/ppermute | solution.py:467
  19.2 2.7 %collective-permute-start.5 = (f32[12,5,8,128]{3,2,1,0:T(8,128)S(1)}, f32[12,5,8,128]{3,2,1,0:T(8,128)S(1)}, u32[]{:S(2)}, u32[]{:S(2)}) collective-permute-start(f32[12,5,8,128]{3,2,1,0:T(8,128)S(1)} %pad_maximum_fusion.own), channel_id=1, source_target_pairs={{2,0},{3,1},{4,2},{5,3},{6,4},{7,5},{8,6},{9,7},{10,8},{11,9},{12,... | collective-permute-start | bytes 737288 | tf_op jit(solution)/shard_map/ppermute | solution.py:467
  21.9 1.3 %collective-permute-start.4 = (f32[12,5,8,128]{3,2,1,0:T(8,128)S(1)}, f32[12,5,8,128]{3,2,1,0:T(8,128)S(1)}, u32[]{:S(2)}, u32[]{:S(2)}) collective-permute-start(f32[12,5,8,128]{3,2,1,0:T(8,128)S(1)} %pad_maximum_fusion.own), channel_id=1, source_target_pairs={{1,0},{2,1},{3,2},{4,3},{5,4},{6,5},{7,6},{8,7},{9,8},{10,9},{11,1... | collective-permute-start | bytes 737288 | tf_op jit(solution)/shard_map/ppermute | solution.py:467
  23.3 2.2 %collective-permute-done.6.a3 = f32[12,5,8,128]{3,2,1,0:T(8,128)S(1)} collective-permute-done((f32[12,5,8,128]{3,2,1,0:T(8,128)S(1)}, f32[12,5,8,128]{3,2,1,0:T(8,128)S(1)}, u32[]{:S(2)}, u32[]{:S(2)}) %collective-permute-start.6) | collective-permute-done | bytes 245792 | tf_op jit(solution)/shard_map/ppermute | solution.py:467
  25.5 0.0 collective-permute-start.9
  25.5 7.5 %collective-permute-done.5.a2 = f32[12,5,8,128]{3,2,1,0:T(8,128)S(1)} collective-permute-done((f32[12,5,8,128]{3,2,1,0:T(8,128)S(1)}, f32[12,5,8,128]{3,2,1,0:T(8,128)S(1)}, u32[]{:S(2)}, u32[]{:S(2)}) %collective-permute-start.5) | collective-permute-done | bytes 245792 | tf_op jit(solution)/shard_map/ppermute | solution.py:467
  33.0 0.0 collective-permute-start.8
  33.0 0.0 collective-permute-done.4.a1
  33.0 0.5 collective-permute-start.7
  33.5 0.0 collective-permute-done.9.b3
  33.5 1.0 %collective-permute-done.8.b2 = f32[12,5,8,128]{3,2,1,0:T(8,128)S(1)} collective-permute-done((f32[12,5,8,128]{3,2,1,0:T(8,128)S(1)}, f32[12,5,8,128]{3,2,1,0:T(8,128)S(1)}, u32[]{:S(2)}, u32[]{:S(2)}) %collective-permute-start.8) | collective-permute-done | bytes 245792 | tf_op jit(solution)/shard_map/ppermute | solution.py:460
  34.5 0.4 collective-permute-done.7.b1
  34.9 24.4 %region.1 = (f32[6,31,8,128]{3,2,1,0:T(8,128)S(1)}, f32[16,8,128]{2,1,0:T(8,128)S(1)}) custom-call(f32[12,5,8,128]{3,2,1,0:T(8,128)S(1)} %pad_maximum_fusion.own, f32[12,5,8,128]{3,2,1,0:T(8,128)S(1)} %collective-permute-done.4.a1, f32[12,5,8,128]{3,2,1,0:T(8,128)S(1)} %collective-permute-done.5.a2, f32[12,5,8,128]{3,2,1,0:T(8,128)S(1)} %collective-permute-done.6.a3, ...), custom_call_target="tpu_custom_call" | custom-call | tf_op jit(solution)/shard_map/region/pallas_call | solution.py:473
  59.3 12.2 %all_to_all.5.info = f32[16,8,128]{2,1,0:T(8,128)S(1)} all-to-all(f32[16,8,128]{2,1,0:T(8,128)S(1)} %get-tuple-element.9), channel_id=1, replica_groups=mesh['gx'=2,'gy'=4,'gz_0'=4,'gz_1'=4] {'gz_0','gz_1'}, dimensions={0} | all-to-all | bytes 131072 | tf_op jit(solution)/shard_map/all_to_all | solution.py:493
  71.5 2.5 %finish.1 = (f32[6,6,3,6]{3,2,1,0:T(4,128)}, f32[6,6,3,6]{3,2,1,0:T(4,128)}, f32[1,8]{1,0:T(1,128)}) custom-call(f32[6,31,8,128]{3,2,1,0:T(8,128)S(1)} %get-tuple-element.8.kept, f32[16,8,128]{2,1,0:T(8,128)S(1)} %all_to_all.5.info), custom_call_target="tpu_custom_call" | custom-call | tf_op jit(solution)/shard_map/finish/pallas_call | solution.py:495
Async XLA Ops:
  3.2 10.8 %copy-start = (f32[6,5,2,128]{3,2,1,0:T(2,128)S(1)}, f32[6,5,2,128]{3,2,1,0:T(2,128)}, u32[]{:S(2)}) copy-start(f32[6,5,2,128]{3,2,1,0:T(2,128)} %pack.1) | copy-start | bytes 92164
  3.2 5.9 %collective-permute-start.2 = (f32[6,5,2,128]{3,2,1,0:T(2,128)}, f32[6,5,2,128]{3,2,1,0:T(2,128)S(1)}, u32[]{:S(2)}, u32[]{:S(2)}) collective-permute-start(f32[6,5,2,128]{3,2,1,0:T(2,128)} %pack.1), channel_id=1, source_target_pairs={{48,0},{0,16},{16,32},{32,48},{49,1},{1,17},{17,33},{33,49},{50,2}... | collective-permute-start | bytes 92168 | tf_op jit(solution)/shard_map/ppermute | solution.py:455
  4.9 5.6 %collective-permute-start.1 = (f32[6,5,2,128]{3,2,1,0:T(2,128)}, f32[6,5,2,128]{3,2,1,0:T(2,128)S(1)}, u32[]{:S(2)}, u32[]{:S(2)}) collective-permute-start(f32[6,5,2,128]{3,2,1,0:T(2,128)} %pack.1), channel_id=1, source_target_pairs={{32,0},{48,16},{0,32},{16,48},{33,1},{49,17},{1,33},{17,49},{34,2}... | collective-permute-start | bytes 92168 | tf_op jit(solution)/shard_map/ppermute | solution.py:455
  7.7 4.1 %collective-permute-start = (f32[6,5,2,128]{3,2,1,0:T(2,128)}, f32[6,5,2,128]{3,2,1,0:T(2,128)S(1)}, u32[]{:S(2)}, u32[]{:S(2)}) collective-permute-start(f32[6,5,2,128]{3,2,1,0:T(2,128)} %pack.1), channel_id=1, source_target_pairs={{16,0},{32,16},{48,32},{0,48},{17,1},{33,17},{49,33},{1,49},{18,2}... | collective-permute-start | bytes 92168 | tf_op jit(solution)/shard_map/ppermute | solution.py:455
  12.6 1.4 %collective-permute-start.3 = (f32[6,5,8,128]{3,2,1,0:T(8,128)S(1)}, f32[6,5,8,128]{3,2,1,0:T(8,128)S(1)}, u32[]{:S(2)}, u32[]{:S(2)}) collective-permute-start(f32[6,5,8,128]{3,2,1,0:T(8,128)S(1)} %pad_maximum_fusion.1), channel_id=1, source_target_pairs={{0,64},{64,0},{1,65},{65,1},{2,66},{66,2},{3,67},{67,3},{4,68},{68... | collective-permute-start | bytes 368648 | tf_op jit(solution)/shard_map/ppermute | solution.py:460
  14.1 11.4 %collective-permute-start.6 = (f32[12,5,8,128]{3,2,1,0:T(8,128)S(1)}, f32[12,5,8,128]{3,2,1,0:T(8,128)S(1)}, u32[]{:S(2)}, u32[]{:S(2)}) collective-permute-start(f32[12,5,8,128]{3,2,1,0:T(8,128)S(1)} %pad_maximum_fusion.own), channel_id=1, source_target_pairs={{3,0},{4,1},{5,2},{6,3},{7,4},{8,5},{9,6},{10,7},{11,8},{12,9},{13... | collective-permute-start | bytes 737288 | tf_op jit(solution)/shard_map/ppermute | solution.py:467
  19.2 13.8 %collective-permute-start.5 = (f32[12,5,8,128]{3,2,1,0:T(8,128)S(1)}, f32[12,5,8,128]{3,2,1,0:T(8,128)S(1)}, u32[]{:S(2)}, u32[]{:S(2)}) collective-permute-start(f32[12,5,8,128]{3,2,1,0:T(8,128)S(1)} %pad_maximum_fusion.own), channel_id=1, source_target_pairs={{2,0},{3,1},{4,2},{5,3},{6,4},{7,5},{8,6},{9,7},{10,8},{11,9},{12,... | collective-permute-start | bytes 737288 | tf_op jit(solution)/shard_map/ppermute | solution.py:467
  21.9 11.1 %collective-permute-start.4 = (f32[12,5,8,128]{3,2,1,0:T(8,128)S(1)}, f32[12,5,8,128]{3,2,1,0:T(8,128)S(1)}, u32[]{:S(2)}, u32[]{:S(2)}) collective-permute-start(f32[12,5,8,128]{3,2,1,0:T(8,128)S(1)} %pad_maximum_fusion.own), channel_id=1, source_target_pairs={{1,0},{2,1},{3,2},{4,3},{5,4},{6,5},{7,6},{8,7},{9,8},{10,9},{11,1... | collective-permute-start | bytes 737288 | tf_op jit(solution)/shard_map/ppermute | solution.py:467
  25.5 8.0 %collective-permute-start.9 = (f32[12,5,8,128]{3,2,1,0:T(8,128)S(1)}, f32[12,5,8,128]{3,2,1,0:T(8,128)S(1)}, u32[]{:S(2)}, u32[]{:S(2)}) collective-permute-start(f32[12,5,8,128]{3,2,1,0:T(8,128)S(1)} %collective-permute-done.6.a3), channel_id=1, source_target_pairs={{0,64},{64,0},{1,65},{65,1},{2,66},{66,2},{3,67},{67,3},{4,68},{68... | collective-permute-start | bytes 737288 | tf_op jit(solution)/shard_map/ppermute | solution.py:460
  33.0 1.5 %collective-permute-start.8 = (f32[12,5,8,128]{3,2,1,0:T(8,128)S(1)}, f32[12,5,8,128]{3,2,1,0:T(8,128)S(1)}, u32[]{:S(2)}, u32[]{:S(2)}) collective-permute-start(f32[12,5,8,128]{3,2,1,0:T(8,128)S(1)} %collective-permute-done.5.a2), channel_id=1, source_target_pairs={{0,64},{64,0},{1,65},{65,1},{2,66},{66,2},{3,67},{67,3},{4,68},{68... | collective-permute-start | bytes 737288 | tf_op jit(solution)/shard_map/ppermute | solution.py:460
  33.0 1.9 %collective-permute-start.7 = (f32[12,5,8,128]{3,2,1,0:T(8,128)S(1)}, f32[12,5,8,128]{3,2,1,0:T(8,128)S(1)}, u32[]{:S(2)}, u32[]{:S(2)}) collective-permute-start(f32[12,5,8,128]{3,2,1,0:T(8,128)S(1)} %collective-permute-done.4.a1), channel_id=1, source_target_pairs={{0,64},{64,0},{1,65},{65,1},{2,66},{66,2},{3,67},{67,3},{4,68},{68... | collective-permute-start | bytes 737288 | tf_op jit(solution)/shard_map/ppermute | solution.py:460

commit v9 on v8

--- a/solution.py
+++ b/solution.py
@@ -363,41 +363,48 @@
     unrolled(EDGE, 2, keep, 0)
 
 
-def finish_kernel(kept, info, dip_out, res_out, len_out, table):
+def finish_kernel(kept, info, dip_out, res_out, len_out):
     gz = lax.axis_index("gz_0") * 4 + lax.axis_index("gz_1")
-    wide = jnp.concatenate([info[e, 0:1, :] for e in range(16)] + [jnp.zeros((112, 128), F32)], axis=0)
-    table[...] = wide.T
+    table = jnp.concatenate([info[e, 0:1, :] for e in range(16)], axis=0)
+    wide = (2, 8, 128)
+
+    def column(n):
+        return jnp.broadcast_to(table[:, n : n + 1], (16, 128)).reshape(wide)
+
     rows = {}
     number = 0
     for low, high in ((0, 3), (3, BASIS)):
         for i in range(low, high):
             for j in range(i, BASIS):
-                rows[i, j] = rows[j, i] = table[number : number + 1, :]
+                rows[i, j] = rows[j, i] = column(number)
                 number += 1
-    al = [table[45 + k : 46 + k, :] for k in range(ITERS)]
-    be = [table[53 + k : 54 + k, :] for k in range(ITERS)]
-    inv = [table[61 + k : 62 + k, :] for k in range(ITERS)]
-    lane = lax.broadcasted_iota(jnp.int32, (1, 128), 1)
-    zero = jnp.zeros((1, 128), F32)
-    one = jnp.where(lane < 16, 1.0, 0.0)
+    al = [column(45 + k) for k in range(ITERS)]
+    be = [column(53 + k) for k in range(ITERS)]
+    inv = [column(61 + k) for k in range(ITERS)]
+    zero = jnp.zeros(wide, F32)
+    slab = lax.broadcasted_iota(jnp.int32, wide, 0) * 8 + lax.broadcasted_iota(jnp.int32, wide, 1)
+    lane = lax.broadcasted_iota(jnp.int32, (8, 128), 1)
 
     def summed(v):
-        return jnp.sum(v, axis=1, keepdims=True)
+        t = v[0] + v[1]
+        for by in (4, 2, 1):
+            t = t + pltpu.roll(t, by, 0)
+        return t
 
     def form(left, right, size_left, size_right):
         acc = zero
         for i in range(size_left):
-            inner = zero
-            for j in range(size_right):
+            inner = rows[i, 0] * right[0]
+            for j in range(1, size_right):
                 inner = inner + rows[i, j] * right[j]
             acc = acc + left[i] * inner
         return summed(acc)
 
-    search = [one] + [zero] * ITERS
-    resid = [one] + [zero] * ITERS
+    search = [zero + 1.0] + [zero] * ITERS
+    resid = [zero + 1.0] + [zero] * ITERS
     moves = [zero] * BASIS
     gamma = summed(rows[0, 0])
-    lengths = zero
+    lengths = jnp.zeros((8, 128), F32)
     for k in range(ITERS):
         image = list(search)
         for j in range(k + 1):
@@ -407,15 +414,15 @@
                 image[j - 1] = image[j - 1] - be[j] * search[j]
         step = gamma / form(search, image, k + 1, k + 2)
         lengths = jnp.where(lane == k, step, lengths)
-        moves = [moves[j] + step * search[j] for j in range(BASIS)]
-        resid = [resid[j] - step * image[j] for j in range(BASIS)]
+        moves = [moves[j] + step[None] * search[j] if j <= k else moves[j] for j in range(BASIS)]
+        resid = [resid[j] - step[None] * image[j] if j <= k + 1 else resid[j] for j in range(BASIS)]
         if k + 1 < ITERS:
             after = form(resid, resid, k + 2, k + 2)
             ratio = after / gamma
-            search = [resid[j] + ratio * search[j] for j in range(BASIS)]
+            search = [resid[j] + ratio[None] * search[j] if j <= k + 1 else zero for j in range(BASIS)]
             gamma = after
-    len_out[...] = lengths[:, :ITERS]
-    here = lane == gz
+    len_out[...] = lengths[0:1, :ITERS]
+    here = slab == gz
     moves = [summed(jnp.where(here, v, 0.0)) for v in moves]
     resid = [summed(jnp.where(here, v, 0.0)) for v in resid]
     for x in range(EDGE):
@@ -447,9 +454,9 @@
             pltpu.VMEM((EDGE, EDGE, EDGE, 56), jnp.int32),
             pltpu.SemaphoreType.DMA((4,)),
         ],
-        compiler_params=pltpu.CompilerParams(vmem_limit_bytes=60 * 1024 * 1024),
+        compiler_params=pltpu.CompilerParams(vmem_limit_bytes=8 * 1024 * 1024),
         name="pack",
-    )(permanent_field.transpose(0, 1, 3, 2), polar, jitter.transpose(0, 1, 3, 2), neighbors)
+    )(*(pltpu.with_memory_space_constraint(v, pltpu.HBM) for v in (permanent_field.transpose(0, 1, 3, 2), polar, jitter.transpose(0, 1, 3, 2), neighbors)))
 
     around = [packed] + [
         lax.ppermute(packed, "gy", [((i + k) % 4, i) for i in range(4)]) for k in (1, 2, 3)
@@ -499,7 +506,6 @@
             jax.ShapeDtypeStruct((EDGE, EDGE, 3, EDGE), F32),
             jax.ShapeDtypeStruct((1, ITERS), F32),
         ),
-        scratch_shapes=[pltpu.VMEM((128, 128), F32)],
         compiler_params=pltpu.CompilerParams(vmem_limit_bytes=8 * 1024 * 1024),
         name="finish",
     )(kept, info)

time: 74.2 us -> 71.6 us (0.965)
  Pallas kernels: 29.5 us -> 28 us
  other arithmetic: 0.88 us -> 0.12 us
    pallas_call x1, Pallas kernels: 2.5 us -> 1.55 us  [per_device(): pl.pallas_call(finish_kernel, out_shape=(jax.ShapeDtypeStruct((EDGE, EDGE...]
    concatenate x1, other arithmetic: 0.81 us -> 0.06 us  [per_device(): half = jnp.concatenate(around, axis=2)]
where the time goes in v9:
time: 71.6 us; the launch traced here: 71.5 us
  Pallas kernels  28 us (39%)
  starting transfers between devices  15.7 us (22%)
  waiting for transfers between devices  14.9 us (21%)
  blocking collectives  12.2 us (17%)
    pallas_call x1, Pallas kernels, per_device(): pl.pallas_call(region_kernel, out_shape=(jax.ShapeDtypeStruct((EDGE, 31)...  24.4 us
    all_to_all x1, blocking collectives, per_device(): info = lax.all_to_all(info, GZ, 0, 0, tiled=True)  12.2 us
    ppermute x3, waiting for transfers between devices, fetch(): return lax.ppermute(own, ('gx',) + GZ, pairs)  9.73 us
    ppermute x3, starting transfers between devices, fetch(): return lax.ppermute(own, ('gx',) + GZ, pairs)  9.21 us
    ppermute x3, starting transfers between devices, per_device(): lax.ppermute(packed, 'gy', [((i + k) % 4, i) for i in range(4)])  5.87 us
    ppermute x4, waiting for transfers between devices, swap(): return lax.ppermute(v, 'gx', [(0, 1), (1, 0)])  2.67 us
    ppermute x3, waiting for transfers between devices, per_device(): lax.ppermute(packed, 'gy', [((i + k) % 4, i) for i in range(4)])  2.46 us
    pallas_call x1, Pallas kernels, per_device(): pl.pallas_call(pack_kernel, out_shape=jax.ShapeDtypeStruct((EDGE, GROUPS,...  1.98 us
  transfers between devices with their start and end apart: 10, of which 7 were waited for; matrix products, arithmetic and copies ran while one was open for 0% of the time, Pallas kernels for 0%

profile of v9, /device:TPU:0, one launch (start us, length us, event | category | flops | bytes accessed | tf_op | source)
XLA Modules:
  0.0 71.5 jit_solution(2291163738836715203)
XLA Ops:
  0.6 2.0 %pack.1 = f32[6,5,2,128]{3,2,1,0:T(2,128)S(1)} custom-call(f32[6,6,3,6]{3,2,1,0:T(4,128)} %bitcast.5, f32[6,6,6]{2,1,0:T(8,128)} %polar_in.1, f32[6,6,3,6]{3,2,1,0:T(4,128)} %bitcast.6, s32[6,6,6,56]{3,2,1,0:T(8,128)} %neighbors_in.1), custom_call_target="tpu_custom_call" | custom-call | tf_op jit(solution)/shard_map/pack/pallas_call | solution.py:446
  2.6 1.7 %collective-permute-start.2 = (f32[6,5,2,128]{3,2,1,0:T(2,128)S(1)}, f32[6,5,2,128]{3,2,1,0:T(2,128)S(1)}, u32[]{:S(2)}, u32[]{:S(2)}) collective-permute-start(f32[6,5,2,128]{3,2,1,0:T(2,128)S(1)} %pack.1), channel_id=1, source_target_pairs={{48,0},{0,16},{16,32},{32,48},{49,1},{1,17},{17,33},{33,49},{50,2}... | collective-permute-start | bytes 92168 | tf_op jit(solution)/shard_map/ppermute | solution.py:462
  4.3 2.7 %collective-permute-start.1 = (f32[6,5,2,128]{3,2,1,0:T(2,128)S(1)}, f32[6,5,2,128]{3,2,1,0:T(2,128)S(1)}, u32[]{:S(2)}, u32[]{:S(2)}) collective-permute-start(f32[6,5,2,128]{3,2,1,0:T(2,128)S(1)} %pack.1), channel_id=1, source_target_pairs={{32,0},{48,16},{0,32},{16,48},{33,1},{49,17},{1,33},{17,49},{34,2}... | collective-permute-start | bytes 92168 | tf_op jit(solution)/shard_map/ppermute | solution.py:462
  7.1 1.4 %collective-permute-start = (f32[6,5,2,128]{3,2,1,0:T(2,128)S(1)}, f32[6,5,2,128]{3,2,1,0:T(2,128)S(1)}, u32[]{:S(2)}, u32[]{:S(2)}) collective-permute-start(f32[6,5,2,128]{3,2,1,0:T(2,128)S(1)} %pack.1), channel_id=1, source_target_pairs={{16,0},{32,16},{48,32},{0,48},{17,1},{33,17},{49,33},{1,49},{18,2}... | collective-permute-start | bytes 92168 | tf_op jit(solution)/shard_map/ppermute | solution.py:462
  8.5 0.0 collective-permute-done.2
  8.5 1.2 %collective-permute-done.1 = f32[6,5,2,128]{3,2,1,0:T(2,128)S(1)} collective-permute-done((f32[6,5,2,128]{3,2,1,0:T(2,128)S(1)}, f32[6,5,2,128]{3,2,1,0:T(2,128)S(1)}, u32[]{:S(2)}, u32[]{:S(2)}) %collective-permute-start.1) | collective-permute-done | bytes 30752 | tf_op jit(solution)/shard_map/ppermute | solution.py:462
  9.7 1.2 %collective-permute-done = f32[6,5,2,128]{3,2,1,0:T(2,128)S(1)} collective-permute-done((f32[6,5,2,128]{3,2,1,0:T(2,128)S(1)}, f32[6,5,2,128]{3,2,1,0:T(2,128)S(1)}, u32[]{:S(2)}, u32[]{:S(2)}) %collective-permute-start) | collective-permute-done | bytes 30752 | tf_op jit(solution)/shard_map/ppermute | solution.py:462
  11.0 0.1 pad_maximum_fusion.1
  11.0 0.1 collective-permute-start.3
  11.1 1.3 %collective-permute-done.3 = f32[6,5,8,128]{3,2,1,0:T(8,128)S(1)} collective-permute-done((f32[6,5,8,128]{3,2,1,0:T(8,128)S(1)}, f32[6,5,8,128]{3,2,1,0:T(8,128)S(1)}, u32[]{:S(2)}, u32[]{:S(2)}) %collective-permute-start.3) | collective-permute-done | bytes 122912 | tf_op jit(solution)/shard_map/ppermute | solution.py:467
  12.4 0.1 pad_maximum_fusion.own
  12.5 5.1 %collective-permute-start.6 = (f32[12,5,8,128]{3,2,1,0:T(8,128)S(1)}, f32[12,5,8,128]{3,2,1,0:T(8,128)S(1)}, u32[]{:S(2)}, u32[]{:S(2)}) collective-permute-start(f32[12,5,8,128]{3,2,1,0:T(8,128)S(1)} %pad_maximum_fusion.own), channel_id=1, source_target_pairs={{3,0},{4,1},{5,2},{6,3},{7,4},{8,5},{9,6},{10,7},{11,8},{12,9},{13... | collective-permute-start | bytes 737288 | tf_op jit(solution)/shard_map/ppermute | solution.py:474
  17.6 2.7 %collective-permute-start.5 = (f32[12,5,8,128]{3,2,1,0:T(8,128)S(1)}, f32[12,5,8,128]{3,2,1,0:T(8,128)S(1)}, u32[]{:S(2)}, u32[]{:S(2)}) collective-permute-start(f32[12,5,8,128]{3,2,1,0:T(8,128)S(1)} %pad_maximum_fusion.own), channel_id=1, source_target_pairs={{2,0},{3,1},{4,2},{5,3},{6,4},{7,5},{8,6},{9,7},{10,8},{11,9},{12,... | collective-permute-start | bytes 737288 | tf_op jit(solution)/shard_map/ppermute | solution.py:474
  20.4 1.3 %collective-permute-start.4 = (f32[12,5,8,128]{3,2,1,0:T(8,128)S(1)}, f32[12,5,8,128]{3,2,1,0:T(8,128)S(1)}, u32[]{:S(2)}, u32[]{:S(2)}) collective-permute-start(f32[12,5,8,128]{3,2,1,0:T(8,128)S(1)} %pad_maximum_fusion.own), channel_id=1, source_target_pairs={{1,0},{2,1},{3,2},{4,3},{5,4},{6,5},{7,6},{8,7},{9,8},{10,9},{11,1... | collective-permute-start | bytes 737288 | tf_op jit(solution)/shard_map/ppermute | solution.py:474
  21.7 2.2 %collective-permute-done.6.a3 = f32[12,5,8,128]{3,2,1,0:T(8,128)S(1)} collective-permute-done((f32[12,5,8,128]{3,2,1,0:T(8,128)S(1)}, f32[12,5,8,128]{3,2,1,0:T(8,128)S(1)}, u32[]{:S(2)}, u32[]{:S(2)}) %collective-permute-start.6) | collective-permute-done | bytes 245792 | tf_op jit(solution)/shard_map/ppermute | solution.py:474
  23.9 0.0 collective-permute-start.9
  23.9 7.5 %collective-permute-done.5.a2 = f32[12,5,8,128]{3,2,1,0:T(8,128)S(1)} collective-permute-done((f32[12,5,8,128]{3,2,1,0:T(8,128)S(1)}, f32[12,5,8,128]{3,2,1,0:T(8,128)S(1)}, u32[]{:S(2)}, u32[]{:S(2)}) %collective-permute-start.5) | collective-permute-done | bytes 245792 | tf_op jit(solution)/shard_map/ppermute | solution.py:474
  31.4 0.0 collective-permute-start.8
  31.4 0.0 collective-permute-done.4.a1
  31.4 0.5 collective-permute-start.7
  32.0 0.0 collective-permute-done.9.b3
  32.0 1.0 %collective-permute-done.8.b2 = f32[12,5,8,128]{3,2,1,0:T(8,128)S(1)} collective-permute-done((f32[12,5,8,128]{3,2,1,0:T(8,128)S(1)}, f32[12,5,8,128]{3,2,1,0:T(8,128)S(1)}, u32[]{:S(2)}, u32[]{:S(2)}) %collective-permute-start.8) | collective-permute-done | bytes 245792 | tf_op jit(solution)/shard_map/ppermute | solution.py:467
  32.9 0.4 collective-permute-done.7.b1
  33.3 24.4 %region.1 = (f32[6,31,8,128]{3,2,1,0:T(8,128)S(1)}, f32[16,8,128]{2,1,0:T(8,128)S(1)}) custom-call(f32[12,5,8,128]{3,2,1,0:T(8,128)S(1)} %pad_maximum_fusion.own, f32[12,5,8,128]{3,2,1,0:T(8,128)S(1)} %collective-permute-done.4.a1, f32[12,5,8,128]{3,2,1,0:T(8,128)S(1)} %collective-permute-done.5.a2, f32[12,5,8,128]{3,2,1,0:T(8,128)S(1)} %collective-permute-done.6.a3, ...), custom_call_target="tpu_custom_call" | custom-call | tf_op jit(solution)/shard_map/region/pallas_call | solution.py:480
  57.7 12.2 %all_to_all.5.info = f32[16,8,128]{2,1,0:T(8,128)S(1)} all-to-all(f32[16,8,128]{2,1,0:T(8,128)S(1)} %get-tuple-element.9), channel_id=1, replica_groups=mesh['gx'=2,'gy'=4,'gz_0'=4,'gz_1'=4] {'gz_0','gz_1'}, dimensions={0} | all-to-all | bytes 131072 | tf_op jit(solution)/shard_map/all_to_all | solution.py:500
  69.9 1.5 %finish.1 = (f32[6,6,3,6]{3,2,1,0:T(4,128)}, f32[6,6,3,6]{3,2,1,0:T(4,128)}, f32[1,8]{1,0:T(1,128)}) custom-call(f32[6,31,8,128]{3,2,1,0:T(8,128)S(1)} %get-tuple-element.8.kept, f32[16,8,128]{2,1,0:T(8,128)S(1)} %all_to_all.5.info), custom_call_target="tpu_custom_call" | custom-call | tf_op jit(solution)/shard_map/finish/pallas_call | solution.py:502
Async XLA Ops:
  2.6 5.9 %collective-permute-start.2 = (f32[6,5,2,128]{3,2,1,0:T(2,128)S(1)}, f32[6,5,2,128]{3,2,1,0:T(2,128)S(1)}, u32[]{:S(2)}, u32[]{:S(2)}) collective-permute-start(f32[6,5,2,128]{3,2,1,0:T(2,128)S(1)} %pack.1), channel_id=1, source_target_pairs={{48,0},{0,16},{16,32},{32,48},{49,1},{1,17},{17,33},{33,49},{50,2}... | collective-permute-start | bytes 92168 | tf_op jit(solution)/shard_map/ppermute | solution.py:462
  4.3 5.4 %collective-permute-start.1 = (f32[6,5,2,128]{3,2,1,0:T(2,128)S(1)}, f32[6,5,2,128]{3,2,1,0:T(2,128)S(1)}, u32[]{:S(2)}, u32[]{:S(2)}) collective-permute-start(f32[6,5,2,128]{3,2,1,0:T(2,128)S(1)} %pack.1), channel_id=1, source_target_pairs={{32,0},{48,16},{0,32},{16,48},{33,1},{49,17},{1,33},{17,49},{34,2}... | collective-permute-start | bytes 92168 | tf_op jit(solution)/shard_map/ppermute | solution.py:462
  7.1 3.9 %collective-permute-start = (f32[6,5,2,128]{3,2,1,0:T(2,128)S(1)}, f32[6,5,2,128]{3,2,1,0:T(2,128)S(1)}, u32[]{:S(2)}, u32[]{:S(2)}) collective-permute-start(f32[6,5,2,128]{3,2,1,0:T(2,128)S(1)} %pack.1), channel_id=1, source_target_pairs={{16,0},{32,16},{48,32},{0,48},{17,1},{33,17},{49,33},{1,49},{18,2}... | collective-permute-start | bytes 92168 | tf_op jit(solution)/shard_map/ppermute | solution.py:462
  11.0 1.4 %collective-permute-start.3 = (f32[6,5,8,128]{3,2,1,0:T(8,128)S(1)}, f32[6,5,8,128]{3,2,1,0:T(8,128)S(1)}, u32[]{:S(2)}, u32[]{:S(2)}) collective-permute-start(f32[6,5,8,128]{3,2,1,0:T(8,128)S(1)} %pad_maximum_fusion.1), channel_id=1, source_target_pairs={{0,64},{64,0},{1,65},{65,1},{2,66},{66,2},{3,67},{67,3},{4,68},{68... | collective-permute-start | bytes 368648 | tf_op jit(solution)/shard_map/ppermute | solution.py:467
  12.5 11.4 %collective-permute-start.6 = (f32[12,5,8,128]{3,2,1,0:T(8,128)S(1)}, f32[12,5,8,128]{3,2,1,0:T(8,128)S(1)}, u32[]{:S(2)}, u32[]{:S(2)}) collective-permute-start(f32[12,5,8,128]{3,2,1,0:T(8,128)S(1)} %pad_maximum_fusion.own), channel_id=1, source_target_pairs={{3,0},{4,1},{5,2},{6,3},{7,4},{8,5},{9,6},{10,7},{11,8},{12,9},{13... | collective-permute-start | bytes 737288 | tf_op jit(solution)/shard_map/ppermute | solution.py:474
  17.6 13.8 %collective-permute-start.5 = (f32[12,5,8,128]{3,2,1,0:T(8,128)S(1)}, f32[12,5,8,128]{3,2,1,0:T(8,128)S(1)}, u32[]{:S(2)}, u32[]{:S(2)}) collective-permute-start(f32[12,5,8,128]{3,2,1,0:T(8,128)S(1)} %pad_maximum_fusion.own), channel_id=1, source_target_pairs={{2,0},{3,1},{4,2},{5,3},{6,4},{7,5},{8,6},{9,7},{10,8},{11,9},{12,... | collective-permute-start | bytes 737288 | tf_op jit(solution)/shard_map/ppermute | solution.py:474
  20.4 11.1 %collective-permute-start.4 = (f32[12,5,8,128]{3,2,1,0:T(8,128)S(1)}, f32[12,5,8,128]{3,2,1,0:T(8,128)S(1)}, u32[]{:S(2)}, u32[]{:S(2)}) collective-permute-start(f32[12,5,8,128]{3,2,1,0:T(8,128)S(1)} %pad_maximum_fusion.own), channel_id=1, source_target_pairs={{1,0},{2,1},{3,2},{4,3},{5,4},{6,5},{7,6},{8,7},{9,8},{10,9},{11,1... | collective-permute-start | bytes 737288 | tf_op jit(solution)/shard_map/ppermute | solution.py:474
  23.9 8.0 %collective-permute-start.9 = (f32[12,5,8,128]{3,2,1,0:T(8,128)S(1)}, f32[12,5,8,128]{3,2,1,0:T(8,128)S(1)}, u32[]{:S(2)}, u32[]{:S(2)}) collective-permute-start(f32[12,5,8,128]{3,2,1,0:T(8,128)S(1)} %collective-permute-done.6.a3), channel_id=1, source_target_pairs={{0,64},{64,0},{1,65},{65,1},{2,66},{66,2},{3,67},{67,3},{4,68},{68... | collective-permute-start | bytes 737288 | tf_op jit(solution)/shard_map/ppermute | solution.py:467
  31.4 1.5 %collective-permute-start.8 = (f32[12,5,8,128]{3,2,1,0:T(8,128)S(1)}, f32[12,5,8,128]{3,2,1,0:T(8,128)S(1)}, u32[]{:S(2)}, u32[]{:S(2)}) collective-permute-start(f32[12,5,8,128]{3,2,1,0:T(8,128)S(1)} %collective-permute-done.5.a2), channel_id=1, source_target_pairs={{0,64},{64,0},{1,65},{65,1},{2,66},{66,2},{3,67},{67,3},{4,68},{68... | collective-permute-start | bytes 737288 | tf_op jit(solution)/shard_map/ppermute | solution.py:467
  31.4 1.9 %collective-permute-start.7 = (f32[12,5,8,128]{3,2,1,0:T(8,128)S(1)}, f32[12,5,8,128]{3,2,1,0:T(8,128)S(1)}, u32[]{:S(2)}, u32[]{:S(2)}) collective-permute-start(f32[12,5,8,128]{3,2,1,0:T(8,128)S(1)} %collective-permute-done.4.a1), channel_id=1, source_target_pairs={{0,64},{64,0},{1,65},{65,1},{2,66},{66,2},{3,67},{67,3},{4,68},{68... | collective-permute-start | bytes 737288 | tf_op jit(solution)/shard_map/ppermute | solution.py:467

commit v10 on v9

--- a/solution.py
+++ b/solution.py
@@ -345,7 +345,7 @@
             number += 1
 
     for e in range(16):
-        info_out[e] = info
+        info_out[e] = info[0:1, :]
 
     def keep(x, carry):
         far = x + EDGE * gx
@@ -365,7 +365,7 @@
 
 def finish_kernel(kept, info, dip_out, res_out, len_out):
     gz = lax.axis_index("gz_0") * 4 + lax.axis_index("gz_1")
-    table = jnp.concatenate([info[e, 0:1, :] for e in range(16)], axis=0)
+    table = jnp.concatenate([info[e] for e in range(16)], axis=0)
     wide = (2, 8, 128)
 
     def column(n):
@@ -458,15 +458,22 @@
         name="pack",
     )(*(pltpu.with_memory_space_constraint(v, pltpu.HBM) for v in (permanent_field.transpose(0, 1, 3, 2), polar, jitter.transpose(0, 1, 3, 2), neighbors)))
 
-    around = [packed] + [
-        lax.ppermute(packed, "gy", [((i + k) % 4, i) for i in range(4)]) for k in (1, 2, 3)
-    ]
-    half = jnp.concatenate(around, axis=2)
-
     def swap(v):
         return lax.ppermute(v, "gx", [(0, 1), (1, 0)])
 
-    own = jnp.concatenate([half, swap(half)], axis=0)
+    both = jnp.concatenate([packed, swap(packed)], axis=0)
+    beside = lax.ppermute(
+        both,
+        ("gx", "gy"),
+        [((i + 1) % 4, i) for i in range(4)] + [(4 + (i - 1) % 4, 4 + i) for i in range(4)],
+    )
+    across = lax.ppermute(both, "gy", [((i + 2) % 4, i) for i in range(4)])
+    other = swap(beside)
+    other = jnp.concatenate([other[EDGE:], other[:EDGE]], axis=0)
+    low = lax.axis_index("gx") == 0
+    own = jnp.concatenate(
+        [both, jnp.where(low, beside, other), across, jnp.where(low, other, beside)], axis=2
+    )
 
     def fetch(k):
         pairs = [((i + k) % 16, i) for i in range(16)]
@@ -481,7 +488,7 @@
         region_kernel,
         out_shape=(
             jax.ShapeDtypeStruct((EDGE, 31) + vreg, F32),
-            jax.ShapeDtypeStruct((16,) + vreg, F32),
+            jax.ShapeDtypeStruct((16, 1, 128), F32),
         ),
         scratch_shapes=[
             pltpu.VMEM((NX, 36) + vreg, F32),

time: 71.6 us -> 74.5 us (1.041)
  waiting for transfers between devices: 14.9 us -> 17.1 us
    ppermute x3 -> x2, waiting for transfers between devices: 2.46 us -> 5.39 us  [the longest x1 3.53 us: per_device(): across = lax.ppermute(both, 'gy', [((i + 2) % 4, i) for i in range(4)])]
    ppermute x3 -> x2, starting transfers between devices: 5.87 us -> 5.59 us  [the longest x1 2.97 us: per_device(): lax.ppermute(both, ('gx', 'gy'), [((i + 1) % 4, i) for i in range(4)] + [...]
    ppermute x4 -> x5, waiting for transfers between devices: 2.67 us -> 2.54 us  [swap(): return lax.ppermute(v, 'gx', [(0, 1), (1, 0)])]
where the time goes in v10:
time: 74.5 us; the launch traced here: 73.7 us
  Pallas kernels  28 us (38%)
  waiting for transfers between devices  17.1 us (23%)
  starting transfers between devices  15.4 us (21%)
  blocking collectives  12.3 us (17%)
    pallas_call x1, Pallas kernels, per_device(): pl.pallas_call(region_kernel, out_shape=(jax.ShapeDtypeStruct((EDGE, 31)...  24.4 us
    all_to_all x1, blocking collectives, per_device(): info = lax.all_to_all(info, GZ, 0, 0, tiled=True)  12.3 us
    ppermute x3, starting transfers between devices, fetch(): return lax.ppermute(own, ('gx',) + GZ, pairs)  9.21 us
    ppermute x3, waiting for transfers between devices, fetch(): return lax.ppermute(own, ('gx',) + GZ, pairs)  9.16 us
    ppermute x1, waiting for transfers between devices, per_device(): across = lax.ppermute(both, 'gy', [((i + 2) % 4, i) for i in range(4)])  3.53 us
    ppermute x1, starting transfers between devices, per_device(): lax.ppermute(both, ('gx', 'gy'), [((i + 1) % 4, i) for i in range(4)] + [...  2.97 us
    ppermute x1, starting transfers between devices, per_device(): across = lax.ppermute(both, 'gy', [((i + 2) % 4, i) for i in range(4)])  2.62 us
    ppermute x5, waiting for transfers between devices, swap(): return lax.ppermute(v, 'gx', [(0, 1), (1, 0)])  2.54 us
  transfers between devices with their start and end apart: 10, of which 7 were waited for; matrix products, arithmetic and copies ran while one was open for 0% of the time, Pallas kernels for 0%

profile of v10, /device:TPU:0, one launch (start us, length us, event | category | flops | bytes accessed | tf_op | source)
XLA Modules:
  0.0 73.7 jit_solution(2944818194850497098)
XLA Ops:
  0.6 2.0 %pack.1 = f32[6,5,2,128]{3,2,1,0:T(2,128)S(1)} custom-call(f32[6,6,3,6]{3,2,1,0:T(4,128)} %bitcast.5, f32[6,6,6]{2,1,0:T(8,128)} %polar_in.1, f32[6,6,3,6]{3,2,1,0:T(4,128)} %bitcast.6, s32[6,6,6,56]{3,2,1,0:T(8,128)} %neighbors_in.1), custom_call_target="tpu_custom_call" | custom-call | tf_op jit(solution)/shard_map/pack/pallas_call | solution.py:446
  2.6 0.1 collective-permute-start
  2.7 1.2 %collective-permute-done = f32[6,5,2,128]{3,2,1,0:T(2,128)S(1)} collective-permute-done((f32[6,5,2,128]{3,2,1,0:T(2,128)S(1)}, f32[6,5,2,128]{3,2,1,0:T(2,128)S(1)}, u32[]{:S(2)}, u32[]{:S(2)}) %collective-permute-start) | collective-permute-done | bytes 30752 | tf_op jit(solution)/shard_map/ppermute | solution.py:462
  3.9 3.0 %collective-permute-start.1 = (f32[12,5,2,128]{3,2,1,0:T(2,128)S(1)}, f32[12,5,2,128]{3,2,1,0:T(2,128)S(1)}, u32[]{:S(2)}, u32[]{:S(2)}) collective-permute-start(f32[12,5,2,128]{3,2,1,0:T(2,128)S(1)} %pad_maximum_fusion.1), channel_id=1, source_target_pairs={{16,0},{32,16},{48,32},{0,48},{112,64},{64,80},{80,96},{96,112},{1... | collective-permute-start | bytes 184328 | tf_op jit(solution)/shard_map/ppermute | solution.py:465
  6.9 1.9 %collective-permute-done.1 = f32[12,5,2,128]{3,2,1,0:T(2,128)S(1)} collective-permute-done((f32[12,5,2,128]{3,2,1,0:T(2,128)S(1)}, f32[12,5,2,128]{3,2,1,0:T(2,128)S(1)}, u32[]{:S(2)}, u32[]{:S(2)}) %collective-permute-start.1) | collective-permute-done | bytes 61472 | tf_op jit(solution)/shard_map/ppermute | solution.py:465
  8.8 0.0 collective-permute-start.2
  8.8 2.6 %collective-permute-start.3 = (f32[12,5,2,128]{3,2,1,0:T(2,128)S(1)}, f32[12,5,2,128]{3,2,1,0:T(2,128)S(1)}, u32[]{:S(2)}, u32[]{:S(2)}) collective-permute-start(f32[12,5,2,128]{3,2,1,0:T(2,128)S(1)} %pad_maximum_fusion.1), channel_id=1, source_target_pairs={{32,0},{48,16},{0,32},{16,48},{33,1},{49,17},{1,33},{17,49},{34,2}... | collective-permute-start | bytes 184328 | tf_op jit(solution)/shard_map/ppermute | solution.py:470
  11.4 0.0 collective-permute-done.2
  11.4 0.1 broadcast_select_fusion.1
  11.5 3.5 %collective-permute-done.3 = f32[12,5,2,128]{3,2,1,0:T(2,128)S(1)} collective-permute-done((f32[12,5,2,128]{3,2,1,0:T(2,128)S(1)}, f32[12,5,2,128]{3,2,1,0:T(2,128)S(1)}, u32[]{:S(2)}, u32[]{:S(2)}) %collective-permute-start.3) | collective-permute-done | bytes 61472 | tf_op jit(solution)/shard_map/ppermute | solution.py:470
  15.0 0.1 pad_maximum_fusion.own
  15.1 5.1 %collective-permute-start.6 = (f32[12,5,8,128]{3,2,1,0:T(8,128)S(1)}, f32[12,5,8,128]{3,2,1,0:T(8,128)S(1)}, u32[]{:S(2)}, u32[]{:S(2)}) collective-permute-start(f32[12,5,8,128]{3,2,1,0:T(8,128)S(1)} %pad_maximum_fusion.own), channel_id=1, source_target_pairs={{3,0},{4,1},{5,2},{6,3},{7,4},{8,5},{9,6},{10,7},{11,8},{12,9},{13... | collective-permute-start | bytes 737288 | tf_op jit(solution)/shard_map/ppermute | solution.py:481
  20.2 2.7 %collective-permute-start.5 = (f32[12,5,8,128]{3,2,1,0:T(8,128)S(1)}, f32[12,5,8,128]{3,2,1,0:T(8,128)S(1)}, u32[]{:S(2)}, u32[]{:S(2)}) collective-permute-start(f32[12,5,8,128]{3,2,1,0:T(8,128)S(1)} %pad_maximum_fusion.own), channel_id=1, source_target_pairs={{2,0},{3,1},{4,2},{5,3},{6,4},{7,5},{8,6},{9,7},{10,8},{11,9},{12,... | collective-permute-start | bytes 737288 | tf_op jit(solution)/shard_map/ppermute | solution.py:481
  23.0 1.3 %collective-permute-start.4 = (f32[12,5,8,128]{3,2,1,0:T(8,128)S(1)}, f32[12,5,8,128]{3,2,1,0:T(8,128)S(1)}, u32[]{:S(2)}, u32[]{:S(2)}) collective-permute-start(f32[12,5,8,128]{3,2,1,0:T(8,128)S(1)} %pad_maximum_fusion.own), channel_id=1, source_target_pairs={{1,0},{2,1},{3,2},{4,3},{5,4},{6,5},{7,6},{8,7},{9,8},{10,9},{11,1... | collective-permute-start | bytes 737288 | tf_op jit(solution)/shard_map/ppermute | solution.py:481
  24.3 2.2 %collective-permute-done.6.a3 = f32[12,5,8,128]{3,2,1,0:T(8,128)S(1)} collective-permute-done((f32[12,5,8,128]{3,2,1,0:T(8,128)S(1)}, f32[12,5,8,128]{3,2,1,0:T(8,128)S(1)}, u32[]{:S(2)}, u32[]{:S(2)}) %collective-permute-start.6) | collective-permute-done | bytes 245792 | tf_op jit(solution)/shard_map/ppermute | solution.py:481
  26.6 0.0 collective-permute-start.9
  26.6 6.9 %collective-permute-done.5.a2 = f32[12,5,8,128]{3,2,1,0:T(8,128)S(1)} collective-permute-done((f32[12,5,8,128]{3,2,1,0:T(8,128)S(1)}, f32[12,5,8,128]{3,2,1,0:T(8,128)S(1)}, u32[]{:S(2)}, u32[]{:S(2)}) %collective-permute-start.5) | collective-permute-done | bytes 245792 | tf_op jit(solution)/shard_map/ppermute | solution.py:481
  33.5 0.0 collective-permute-start.8
  33.5 0.0 collective-permute-done.4.a1
  33.5 0.5 collective-permute-start.7
  34.0 0.0 collective-permute-done.9.b3
  34.0 1.0 %collective-permute-done.8.b2 = f32[12,5,8,128]{3,2,1,0:T(8,128)S(1)} collective-permute-done((f32[12,5,8,128]{3,2,1,0:T(8,128)S(1)}, f32[12,5,8,128]{3,2,1,0:T(8,128)S(1)}, u32[]{:S(2)}, u32[]{:S(2)}) %collective-permute-start.8) | collective-permute-done | bytes 245792 | tf_op jit(solution)/shard_map/ppermute | solution.py:462
  35.0 0.4 collective-permute-done.7.b1
  35.4 24.4 %region.1 = (f32[6,31,8,128]{3,2,1,0:T(8,128)S(1)}, f32[16,1,128]{2,1,0:T(1,128)S(1)}) custom-call(f32[12,5,8,128]{3,2,1,0:T(8,128)S(1)} %pad_maximum_fusion.own, f32[12,5,8,128]{3,2,1,0:T(8,128)S(1)} %collective-permute-done.4.a1, f32[12,5,8,128]{3,2,1,0:T(8,128)S(1)} %collective-permute-done.5.a2, f32[12,5,8,128]{3,2,1,0:T(8,128)S(1)} %collective-permute-done.6.a3, ...), custom_call_target="tpu_custom_call" | custom-call | tf_op jit(solution)/shard_map/region/pallas_call | solution.py:487
  59.8 12.3 %all_to_all.5.info = f32[16,1,128]{2,1,0:T(1,128)S(1)} all-to-all(f32[16,1,128]{2,1,0:T(1,128)S(1)} %get-tuple-element.9), channel_id=1, replica_groups=mesh['gx'=2,'gy'=4,'gz_0'=4,'gz_1'=4] {'gz_0','gz_1'}, dimensions={0} | all-to-all | bytes 16384 | tf_op jit(solution)/shard_map/all_to_all | solution.py:507
  72.1 1.5 %finish.1 = (f32[6,6,3,6]{3,2,1,0:T(4,128)}, f32[6,6,3,6]{3,2,1,0:T(4,128)}, f32[1,8]{1,0:T(1,128)}) custom-call(f32[6,31,8,128]{3,2,1,0:T(8,128)S(1)} %get-tuple-element.8.kept, f32[16,1,128]{2,1,0:T(1,128)S(1)} %all_to_all.5.info), custom_call_target="tpu_custom_call" | custom-call | tf_op jit(solution)/shard_map/finish/pallas_call | solution.py:509
  (2 shorter events, 0.0 us)
Async XLA Ops:
  2.6 1.3 %collective-permute-start = (f32[6,5,2,128]{3,2,1,0:T(2,128)S(1)}, f32[6,5,2,128]{3,2,1,0:T(2,128)S(1)}, u32[]{:S(2)}, u32[]{:S(2)}) collective-permute-start(f32[6,5,2,128]{3,2,1,0:T(2,128)S(1)} %pack.1), channel_id=1, source_target_pairs={{0,64},{64,0},{1,65},{65,1},{2,66},{66,2},{3,67},{67,3},{4,68},{68... | collective-permute-start | bytes 92168 | tf_op jit(solution)/shard_map/ppermute | solution.py:462
  3.9 4.8 %collective-permute-start.1 = (f32[12,5,2,128]{3,2,1,0:T(2,128)S(1)}, f32[12,5,2,128]{3,2,1,0:T(2,128)S(1)}, u32[]{:S(2)}, u32[]{:S(2)}) collective-permute-start(f32[12,5,2,128]{3,2,1,0:T(2,128)S(1)} %pad_maximum_fusion.1), channel_id=1, source_target_pairs={{16,0},{32,16},{48,32},{0,48},{112,64},{64,80},{80,96},{96,112},{1... | collective-permute-start | bytes 184328 | tf_op jit(solution)/shard_map/ppermute | solution.py:465
  8.8 2.6 %collective-permute-start.2 = (f32[12,5,2,128]{3,2,1,0:T(2,128)S(1)}, f32[12,5,2,128]{3,2,1,0:T(2,128)S(1)}, u32[]{:S(2)}, u32[]{:S(2)}) collective-permute-start(f32[12,5,2,128]{3,2,1,0:T(2,128)S(1)} %collective-permute-done.1), channel_id=1, source_target_pairs={{0,64},{64,0},{1,65},{65,1},{2,66},{66,2},{3,67},{67,3},{4,68},{68... | collective-permute-start | bytes 184328 | tf_op jit(solution)/shard_map/ppermute | solution.py:462
  8.8 6.2 %collective-permute-start.3 = (f32[12,5,2,128]{3,2,1,0:T(2,128)S(1)}, f32[12,5,2,128]{3,2,1,0:T(2,128)S(1)}, u32[]{:S(2)}, u32[]{:S(2)}) collective-permute-start(f32[12,5,2,128]{3,2,1,0:T(2,128)S(1)} %pad_maximum_fusion.1), channel_id=1, source_target_pairs={{32,0},{48,16},{0,32},{16,48},{33,1},{49,17},{1,33},{17,49},{34,2}... | collective-permute-start | bytes 184328 | tf_op jit(solution)/shard_map/ppermute | solution.py:470
  15.1 11.4 %collective-permute-start.6 = (f32[12,5,8,128]{3,2,1,0:T(8,128)S(1)}, f32[12,5,8,128]{3,2,1,0:T(8,128)S(1)}, u32[]{:S(2)}, u32[]{:S(2)}) collective-permute-start(f32[12,5,8,128]{3,2,1,0:T(8,128)S(1)} %pad_maximum_fusion.own), channel_id=1, source_target_pairs={{3,0},{4,1},{5,2},{6,3},{7,4},{8,5},{9,6},{10,7},{11,8},{12,9},{13... | collective-permute-start | bytes 737288 | tf_op jit(solution)/shard_map/ppermute | solution.py:481
  20.2 13.3 %collective-permute-start.5 = (f32[12,5,8,128]{3,2,1,0:T(8,128)S(1)}, f32[12,5,8,128]{3,2,1,0:T(8,128)S(1)}, u32[]{:S(2)}, u32[]{:S(2)}) collective-permute-start(f32[12,5,8,128]{3,2,1,0:T(8,128)S(1)} %pad_maximum_fusion.own), channel_id=1, source_target_pairs={{2,0},{3,1},{4,2},{5,3},{6,4},{7,5},{8,6},{9,7},{10,8},{11,9},{12,... | collective-permute-start | bytes 737288 | tf_op jit(solution)/shard_map/ppermute | solution.py:481
  23.0 10.5 %collective-permute-start.4 = (f32[12,5,8,128]{3,2,1,0:T(8,128)S(1)}, f32[12,5,8,128]{3,2,1,0:T(8,128)S(1)}, u32[]{:S(2)}, u32[]{:S(2)}) collective-permute-start(f32[12,5,8,128]{3,2,1,0:T(8,128)S(1)} %pad_maximum_fusion.own), channel_id=1, source_target_pairs={{1,0},{2,1},{3,2},{4,3},{5,4},{6,5},{7,6},{8,7},{9,8},{10,9},{11,1... | collective-permute-start | bytes 737288 | tf_op jit(solution)/shard_map/ppermute | solution.py:481
  26.6 7.4 %collective-permute-start.9 = (f32[12,5,8,128]{3,2,1,0:T(8,128)S(1)}, f32[12,5,8,128]{3,2,1,0:T(8,128)S(1)}, u32[]{:S(2)}, u32[]{:S(2)}) collective-permute-start(f32[12,5,8,128]{3,2,1,0:T(8,128)S(1)} %collective-permute-done.6.a3), channel_id=1, source_target_pairs={{0,64},{64,0},{1,65},{65,1},{2,66},{66,2},{3,67},{67,3},{4,68},{68... | collective-permute-start | bytes 737288 | tf_op jit(solution)/shard_map/ppermute | solution.py:462
  33.5 1.5 %collective-permute-start.8 = (f32[12,5,8,128]{3,2,1,0:T(8,128)S(1)}, f32[12,5,8,128]{3,2,1,0:T(8,128)S(1)}, u32[]{:S(2)}, u32[]{:S(2)}) collective-permute-start(f32[12,5,8,128]{3,2,1,0:T(8,128)S(1)} %collective-permute-done.5.a2), channel_id=1, source_target_pairs={{0,64},{64,0},{1,65},{65,1},{2,66},{66,2},{3,67},{67,3},{4,68},{68... | collective-permute-start | bytes 737288 | tf_op jit(solution)/shard_map/ppermute | solution.py:462
  33.5 1.9 %collective-permute-start.7 = (f32[12,5,8,128]{3,2,1,0:T(8,128)S(1)}, f32[12,5,8,128]{3,2,1,0:T(8,128)S(1)}, u32[]{:S(2)}, u32[]{:S(2)}) collective-permute-start(f32[12,5,8,128]{3,2,1,0:T(8,128)S(1)} %collective-permute-done.4.a1), channel_id=1, source_target_pairs={{0,64},{64,0},{1,65},{65,1},{2,66},{66,2},{3,67},{67,3},{4,68},{68... | collective-permute-start | bytes 737288 | tf_op jit(solution)/shard_map/ppermute | solution.py:462

commit v11 on v9

--- a/solution.py
+++ b/solution.py
@@ -10,6 +10,7 @@
 BASIS = ITERS + 1
 THOLE = 0.39
 SPACING = 3.5
+LOG2E = 1.4426950408889634
 EDGE = 6
 NX = 12
 WIDE = 42
@@ -25,9 +26,6 @@
 ]
 FORWARD = [d for d in OFFSETS if d > (0, 0, 0)]
 GROUPS, PER = 5, 7
-
-
-FIRSTS = {min(n for n, d in enumerate(FORWARD) if d[2] == dz) for dz in range(-2, 3)}
 
 
 def lane_iota():
@@ -152,7 +150,7 @@
 
 
 def region_kernel(
-    own, a1, a2, a3, b1, b2, b3, kept_out, info_out, chan, near, coef, moved, basis,
+    own, a1, a2, a3, b1, b2, b3, kept_out, info_out, chan, near, home, coef, moved, basis,
     raw, now, past,
 ):
     gx = lax.axis_index("gx")
@@ -185,6 +183,8 @@
                     )
             for member in range(PER):
                 acc = pltpu.roll(outs[member], 2 * gy, 0)
+                if 4 <= group * PER + member < 7:
+                    acc = acc * SPACING
                 if group * PER + member == 3:
                     acc = jnp.where(lane >= 3 * WIDE, 1.0, acc)
                     chan[x, 35] = 1.0 / acc
@@ -196,37 +196,42 @@
     def spread(x, carry):
         for c in range(4):
             v = chan[x, 3 + c]
-            for dy in range(-2, 3):
-                near[x, (dy + 2) * 4 + c] = shifted(v, dy, 0, first, last)
+            for step in range(-2, 3):
+                near[x, (step + 2) * 4 + c] = shifted(v, step, 0, first, last)
+                home[x, (step + 2) * 4 + c] = roll_lanes(v, -step)
         return carry
 
     unrolled(NX, 3, spread, 0)
 
     def pairs(x, carry):
         for number, d in sorted(enumerate(FORWARD), key=lambda t: t[1][2]):
-            if number in FIRSTS:
-                home = [roll_lanes(chan[x, 3 + c], -d[2]) for c in range(4)]
             other = wrap(x + d[0])
             place = (d[1] + 2) * 4
-            polar, *jit = home
-            sep = [((near[other, place + 1 + c] - jit[c]) + float(d[c])) * SPACING for c in range(3)]
+            polar, *jit = [home[x, (d[2] + 2) * 4 + c] for c in range(4)]
+            sep = [near[other, place + 1 + c] - jit[c] for c in range(3)]
+            sep = [t + d[c] * SPACING if d[c] else t for c, t in enumerate(sep)]
             dist_sq = sep[0] * sep[0] + sep[1] * sep[1] + sep[2] * sep[2]
             over = lax.rsqrt(dist_sq)
             cube = dist_sq * dist_sq * over
             over_sq = over * over
             over_cube = over_sq * over
-            damping = THOLE * cube * lax.rsqrt(polar * near[other, place])
-            falloff = jnp.exp(-damping)
-            iso = (1.0 - falloff) * over_cube
-            radial = 3.0 * (1.0 - (1.0 + damping) * falloff) * over_cube * over_sq
-            root = jnp.sqrt(radial)
-            here = roll_lanes(chan[x, 7 + number], -d[2]) > 0.5
-            values = [jnp.where(here, s * root, 0.0) for s in sep] + [jnp.where(here, iso, 0.0)]
+            damping = cube * (THOLE * lax.rsqrt(polar * near[other, place]))
+            falloff = jnp.exp2(damping * -LOG2E)
+            flag = roll_lanes(chan[x, 7 + number], -d[2])
+            iso = (over_cube - falloff * over_cube) * flag
+            radial = (3.0 - (3.0 + 3.0 * damping) * falloff) * (over_cube * over_sq)
+            root = radial * lax.rsqrt(radial) * flag
             ahead = OFFSETS.index(d) * 4
             behind = OFFSETS.index((-d[0], -d[1], -d[2])) * 4
-            for c in range(4):
-                coef[x, ahead + c] = values[c]
-                coef[other, behind + c] = shifted(values[c], -d[1], d[2], first, last)
+            for c in range(3):
+                coef[x, ahead + c] = sep[c] * root
+            coef[x, ahead + 3] = iso
+            root = shifted(root, -d[1], d[2], first, last)
+            coef[other, behind + 3] = shifted(iso, -d[1], d[2], first, last)
+            for c in range(3):
+                back = near[x, (2 - d[1]) * 4 + 1 + c] - home[other, (2 - d[2]) * 4 + 1 + c]
+                back = back - d[c] * SPACING if d[c] else back
+                coef[other, behind + c] = back * root
         return carry
 
     lax.fori_loop(0, NX, pairs, 0)
@@ -302,17 +307,20 @@
         live = k > 0
         norm = jnp.where(live, norm, 0.0)
         tiny = 1e-36
-        al = jnp.where(norm > tiny, along_now / jnp.maximum(norm, tiny), 0.0)
-        be = jnp.where(before > tiny, along_past / jnp.maximum(before, tiny), 0.0)
+        over = jnp.where(norm > tiny, 1.0 / jnp.maximum(norm, tiny), 0.0)
+        over_past = jnp.where(before > tiny, 1.0 / jnp.maximum(before, tiny), 0.0)
+        al = along_now * over
+        be = along_past * over_past
         rest = full - al * along_now - be * along_past
         rest = jnp.maximum(rest, 1e-10 * full)
         good = (rest > tiny) & (norm > tiny)
-        inv = jnp.where(good, jnp.sqrt(rest / jnp.maximum(norm, tiny)), 1.0)
-        inv = jnp.minimum(jnp.maximum(inv, 1e-6), 1e3)
+        sc = jnp.where(good, lax.rsqrt(jnp.maximum(rest * over, 1e-12)), 1.0)
+        sc = jnp.maximum(sc, 1e-3)
+        inv = 1.0 / sc
         info = jnp.where(lane == 44 + k, jnp.where(live, al, info), info)
         info = jnp.where(lane == 52 + k, jnp.where(live, be, info), info)
         info = jnp.where(lane == 60 + k, jnp.where(live, inv, info), info)
-        return info, norm, al, be, 1.0 / inv
+        return info, norm, al, be, sc
 
     none = jnp.zeros((1, 1), F32)
     info, _, al, be, sc = lax.fori_loop(0, BASIS, extend, (zero, none, none, none, none + 1.0))
@@ -486,6 +494,7 @@
         scratch_shapes=[
             pltpu.VMEM((NX, 36) + vreg, F32),
             pltpu.VMEM((NX, 20) + vreg, F32),
+            pltpu.VMEM((NX, 20) + vreg, F32),
             pltpu.VMEM((NX, 4 * len(OFFSETS)) + vreg, F32),
             pltpu.VMEM((NX, 16) + vreg, F32),
             pltpu.VMEM((BASIS + 1, 3 * NX) + vreg, F32),

time: 71.6 us -> 70.2 us (0.980)
  Pallas kernels: 28 us -> 26.5 us
    pallas_call x1, Pallas kernels: 24.4 us -> 23 us  [per_device(): pl.pallas_call(region_kernel, out_shape=(jax.ShapeDtypeStruct((EDGE, 31)...]
where the time goes in v11:
time: 70.2 us; the launch traced here: 70 us
  Pallas kernels  26.5 us (38%)
  starting transfers between devices  15.7 us (22%)
  waiting for transfers between devices  14.9 us (21%)
  blocking collectives  12.2 us (17%)
    pallas_call x1, Pallas kernels, per_device(): pl.pallas_call(region_kernel, out_shape=(jax.ShapeDtypeStruct((EDGE, 31)...  23 us
    all_to_all x1, blocking collectives, per_device(): info = lax.all_to_all(info, GZ, 0, 0, tiled=True)  12.2 us
    ppermute x3, waiting for transfers between devices, fetch(): return lax.ppermute(own, ('gx',) + GZ, pairs)  9.73 us
    ppermute x3, starting transfers between devices, fetch(): return lax.ppermute(own, ('gx',) + GZ, pairs)  9.21 us
    ppermute x3, starting transfers between devices, per_device(): lax.ppermute(packed, 'gy', [((i + k) % 4, i) for i in range(4)])  5.87 us
    ppermute x4, waiting for transfers between devices, swap(): return lax.ppermute(v, 'gx', [(0, 1), (1, 0)])  2.67 us
    ppermute x3, waiting for transfers between devices, per_device(): lax.ppermute(packed, 'gy', [((i + k) % 4, i) for i in range(4)])  2.46 us
    pallas_call x1, Pallas kernels, per_device(): pl.pallas_call(pack_kernel, out_shape=jax.ShapeDtypeStruct((EDGE, GROUPS,...  1.98 us
  transfers between devices with their start and end apart: 10, of which 7 were waited for; matrix products, arithmetic and copies ran while one was open for 0% of the time, Pallas kernels for 0%

profile of v11, /device:TPU:0, one launch (start us, length us, event | category | flops | bytes accessed | tf_op | source)
XLA Modules:
  0.0 70.0 jit_solution(17489247550817707069)
XLA Ops:
  0.6 2.0 %pack.1 = f32[6,5,2,128]{3,2,1,0:T(2,128)S(1)} custom-call(f32[6,6,3,6]{3,2,1,0:T(4,128)} %bitcast.5, f32[6,6,6]{2,1,0:T(8,128)} %polar_in.1, f32[6,6,3,6]{3,2,1,0:T(4,128)} %bitcast.6, s32[6,6,6,56]{3,2,1,0:T(8,128)} %neighbors_in.1), custom_call_target="tpu_custom_call" | custom-call | tf_op jit(solution)/shard_map/pack/pallas_call | solution.py:454
  2.6 1.7 %collective-permute-start.2 = (f32[6,5,2,128]{3,2,1,0:T(2,128)S(1)}, f32[6,5,2,128]{3,2,1,0:T(2,128)S(1)}, u32[]{:S(2)}, u32[]{:S(2)}) collective-permute-start(f32[6,5,2,128]{3,2,1,0:T(2,128)S(1)} %pack.1), channel_id=1, source_target_pairs={{48,0},{0,16},{16,32},{32,48},{49,1},{1,17},{17,33},{33,49},{50,2}... | collective-permute-start | bytes 92168 | tf_op jit(solution)/shard_map/ppermute | solution.py:470
  4.3 2.7 %collective-permute-start.1 = (f32[6,5,2,128]{3,2,1,0:T(2,128)S(1)}, f32[6,5,2,128]{3,2,1,0:T(2,128)S(1)}, u32[]{:S(2)}, u32[]{:S(2)}) collective-permute-start(f32[6,5,2,128]{3,2,1,0:T(2,128)S(1)} %pack.1), channel_id=1, source_target_pairs={{32,0},{48,16},{0,32},{16,48},{33,1},{49,17},{1,33},{17,49},{34,2}... | collective-permute-start | bytes 92168 | tf_op jit(solution)/shard_map/ppermute | solution.py:470
  7.1 1.4 %collective-permute-start = (f32[6,5,2,128]{3,2,1,0:T(2,128)S(1)}, f32[6,5,2,128]{3,2,1,0:T(2,128)S(1)}, u32[]{:S(2)}, u32[]{:S(2)}) collective-permute-start(f32[6,5,2,128]{3,2,1,0:T(2,128)S(1)} %pack.1), channel_id=1, source_target_pairs={{16,0},{32,16},{48,32},{0,48},{17,1},{33,17},{49,33},{1,49},{18,2}... | collective-permute-start | bytes 92168 | tf_op jit(solution)/shard_map/ppermute | solution.py:470
  8.5 0.0 collective-permute-done.2
  8.5 1.2 %collective-permute-done.1 = f32[6,5,2,128]{3,2,1,0:T(2,128)S(1)} collective-permute-done((f32[6,5,2,128]{3,2,1,0:T(2,128)S(1)}, f32[6,5,2,128]{3,2,1,0:T(2,128)S(1)}, u32[]{:S(2)}, u32[]{:S(2)}) %collective-permute-start.1) | collective-permute-done | bytes 30752 | tf_op jit(solution)/shard_map/ppermute | solution.py:470
  9.7 1.2 %collective-permute-done = f32[6,5,2,128]{3,2,1,0:T(2,128)S(1)} collective-permute-done((f32[6,5,2,128]{3,2,1,0:T(2,128)S(1)}, f32[6,5,2,128]{3,2,1,0:T(2,128)S(1)}, u32[]{:S(2)}, u32[]{:S(2)}) %collective-permute-start) | collective-permute-done | bytes 30752 | tf_op jit(solution)/shard_map/ppermute | solution.py:470
  11.0 0.1 pad_maximum_fusion.1
  11.0 0.1 collective-permute-start.3
  11.1 1.3 %collective-permute-done.3 = f32[6,5,8,128]{3,2,1,0:T(8,128)S(1)} collective-permute-done((f32[6,5,8,128]{3,2,1,0:T(8,128)S(1)}, f32[6,5,8,128]{3,2,1,0:T(8,128)S(1)}, u32[]{:S(2)}, u32[]{:S(2)}) %collective-permute-start.3) | collective-permute-done | bytes 122912 | tf_op jit(solution)/shard_map/ppermute | solution.py:475
  12.4 0.1 pad_maximum_fusion.own
  12.5 5.1 %collective-permute-start.6 = (f32[12,5,8,128]{3,2,1,0:T(8,128)S(1)}, f32[12,5,8,128]{3,2,1,0:T(8,128)S(1)}, u32[]{:S(2)}, u32[]{:S(2)}) collective-permute-start(f32[12,5,8,128]{3,2,1,0:T(8,128)S(1)} %pad_maximum_fusion.own), channel_id=1, source_target_pairs={{3,0},{4,1},{5,2},{6,3},{7,4},{8,5},{9,6},{10,7},{11,8},{12,9},{13... | collective-permute-start | bytes 737288 | tf_op jit(solution)/shard_map/ppermute | solution.py:482
  17.6 2.7 %collective-permute-start.5 = (f32[12,5,8,128]{3,2,1,0:T(8,128)S(1)}, f32[12,5,8,128]{3,2,1,0:T(8,128)S(1)}, u32[]{:S(2)}, u32[]{:S(2)}) collective-permute-start(f32[12,5,8,128]{3,2,1,0:T(8,128)S(1)} %pad_maximum_fusion.own), channel_id=1, source_target_pairs={{2,0},{3,1},{4,2},{5,3},{6,4},{7,5},{8,6},{9,7},{10,8},{11,9},{12,... | collective-permute-start | bytes 737288 | tf_op jit(solution)/shard_map/ppermute | solution.py:482
  20.4 1.3 %collective-permute-start.4 = (f32[12,5,8,128]{3,2,1,0:T(8,128)S(1)}, f32[12,5,8,128]{3,2,1,0:T(8,128)S(1)}, u32[]{:S(2)}, u32[]{:S(2)}) collective-permute-start(f32[12,5,8,128]{3,2,1,0:T(8,128)S(1)} %pad_maximum_fusion.own), channel_id=1, source_target_pairs={{1,0},{2,1},{3,2},{4,3},{5,4},{6,5},{7,6},{8,7},{9,8},{10,9},{11,1... | collective-permute-start | bytes 737288 | tf_op jit(solution)/shard_map/ppermute | solution.py:482
  21.7 2.2 %collective-permute-done.6.a3 = f32[12,5,8,128]{3,2,1,0:T(8,128)S(1)} collective-permute-done((f32[12,5,8,128]{3,2,1,0:T(8,128)S(1)}, f32[12,5,8,128]{3,2,1,0:T(8,128)S(1)}, u32[]{:S(2)}, u32[]{:S(2)}) %collective-permute-start.6) | collective-permute-done | bytes 245792 | tf_op jit(solution)/shard_map/ppermute | solution.py:482
  23.9 0.0 collective-permute-start.9
  23.9 7.5 %collective-permute-done.5.a2 = f32[12,5,8,128]{3,2,1,0:T(8,128)S(1)} collective-permute-done((f32[12,5,8,128]{3,2,1,0:T(8,128)S(1)}, f32[12,5,8,128]{3,2,1,0:T(8,128)S(1)}, u32[]{:S(2)}, u32[]{:S(2)}) %collective-permute-start.5) | collective-permute-done | bytes 245792 | tf_op jit(solution)/shard_map/ppermute | solution.py:482
  31.4 0.0 collective-permute-start.8
  31.4 0.0 collective-permute-done.4.a1
  31.4 0.5 collective-permute-start.7
  32.0 0.0 collective-permute-done.9.b3
  32.0 1.0 %collective-permute-done.8.b2 = f32[12,5,8,128]{3,2,1,0:T(8,128)S(1)} collective-permute-done((f32[12,5,8,128]{3,2,1,0:T(8,128)S(1)}, f32[12,5,8,128]{3,2,1,0:T(8,128)S(1)}, u32[]{:S(2)}, u32[]{:S(2)}) %collective-permute-start.8) | collective-permute-done | bytes 245792 | tf_op jit(solution)/shard_map/ppermute | solution.py:475
  32.9 0.4 collective-permute-done.7.b1
  33.3 23.0 %region.1 = (f32[6,31,8,128]{3,2,1,0:T(8,128)S(1)}, f32[16,8,128]{2,1,0:T(8,128)S(1)}) custom-call(f32[12,5,8,128]{3,2,1,0:T(8,128)S(1)} %pad_maximum_fusion.own, f32[12,5,8,128]{3,2,1,0:T(8,128)S(1)} %collective-permute-done.4.a1, f32[12,5,8,128]{3,2,1,0:T(8,128)S(1)} %collective-permute-done.5.a2, f32[12,5,8,128]{3,2,1,0:T(8,128)S(1)} %collective-permute-done.6.a3, ...), custom_call_target="tpu_custom_call" | custom-call | tf_op jit(solution)/shard_map/region/pallas_call | solution.py:488
  56.3 12.2 %all_to_all.5.info = f32[16,8,128]{2,1,0:T(8,128)S(1)} all-to-all(f32[16,8,128]{2,1,0:T(8,128)S(1)} %get-tuple-element.9), channel_id=1, replica_groups=mesh['gx'=2,'gy'=4,'gz_0'=4,'gz_1'=4] {'gz_0','gz_1'}, dimensions={0} | all-to-all | bytes 131072 | tf_op jit(solution)/shard_map/all_to_all | solution.py:509
  68.4 1.5 %finish.1 = (f32[6,6,3,6]{3,2,1,0:T(4,128)}, f32[6,6,3,6]{3,2,1,0:T(4,128)}, f32[1,8]{1,0:T(1,128)}) custom-call(f32[6,31,8,128]{3,2,1,0:T(8,128)S(1)} %get-tuple-element.8.kept, f32[16,8,128]{2,1,0:T(8,128)S(1)} %all_to_all.5.info), custom_call_target="tpu_custom_call" | custom-call | tf_op jit(solution)/shard_map/finish/pallas_call | solution.py:511
Async XLA Ops:
  2.6 5.9 %collective-permute-start.2 = (f32[6,5,2,128]{3,2,1,0:T(2,128)S(1)}, f32[6,5,2,128]{3,2,1,0:T(2,128)S(1)}, u32[]{:S(2)}, u32[]{:S(2)}) collective-permute-start(f32[6,5,2,128]{3,2,1,0:T(2,128)S(1)} %pack.1), channel_id=1, source_target_pairs={{48,0},{0,16},{16,32},{32,48},{49,1},{1,17},{17,33},{33,49},{50,2}... | collective-permute-start | bytes 92168 | tf_op jit(solution)/shard_map/ppermute | solution.py:470
  4.3 5.4 %collective-permute-start.1 = (f32[6,5,2,128]{3,2,1,0:T(2,128)S(1)}, f32[6,5,2,128]{3,2,1,0:T(2,128)S(1)}, u32[]{:S(2)}, u32[]{:S(2)}) collective-permute-start(f32[6,5,2,128]{3,2,1,0:T(2,128)S(1)} %pack.1), channel_id=1, source_target_pairs={{32,0},{48,16},{0,32},{16,48},{33,1},{49,17},{1,33},{17,49},{34,2}... | collective-permute-start | bytes 92168 | tf_op jit(solution)/shard_map/ppermute | solution.py:470
  7.1 3.9 %collective-permute-start = (f32[6,5,2,128]{3,2,1,0:T(2,128)S(1)}, f32[6,5,2,128]{3,2,1,0:T(2,128)S(1)}, u32[]{:S(2)}, u32[]{:S(2)}) collective-permute-start(f32[6,5,2,128]{3,2,1,0:T(2,128)S(1)} %pack.1), channel_id=1, source_target_pairs={{16,0},{32,16},{48,32},{0,48},{17,1},{33,17},{49,33},{1,49},{18,2}... | collective-permute-start | bytes 92168 | tf_op jit(solution)/shard_map/ppermute | solution.py:470
  11.0 1.4 %collective-permute-start.3 = (f32[6,5,8,128]{3,2,1,0:T(8,128)S(1)}, f32[6,5,8,128]{3,2,1,0:T(8,128)S(1)}, u32[]{:S(2)}, u32[]{:S(2)}) collective-permute-start(f32[6,5,8,128]{3,2,1,0:T(8,128)S(1)} %pad_maximum_fusion.1), channel_id=1, source_target_pairs={{0,64},{64,0},{1,65},{65,1},{2,66},{66,2},{3,67},{67,3},{4,68},{68... | collective-permute-start | bytes 368648 | tf_op jit(solution)/shard_map/ppermute | solution.py:475
  12.5 11.4 %collective-permute-start.6 = (f32[12,5,8,128]{3,2,1,0:T(8,128)S(1)}, f32[12,5,8,128]{3,2,1,0:T(8,128)S(1)}, u32[]{:S(2)}, u32[]{:S(2)}) collective-permute-start(f32[12,5,8,128]{3,2,1,0:T(8,128)S(1)} %pad_maximum_fusion.own), channel_id=1, source_target_pairs={{3,0},{4,1},{5,2},{6,3},{7,4},{8,5},{9,6},{10,7},{11,8},{12,9},{13... | collective-permute-start | bytes 737288 | tf_op jit(solution)/shard_map/ppermute | solution.py:482
  17.6 13.8 %collective-permute-start.5 = (f32[12,5,8,128]{3,2,1,0:T(8,128)S(1)}, f32[12,5,8,128]{3,2,1,0:T(8,128)S(1)}, u32[]{:S(2)}, u32[]{:S(2)}) collective-permute-start(f32[12,5,8,128]{3,2,1,0:T(8,128)S(1)} %pad_maximum_fusion.own), channel_id=1, source_target_pairs={{2,0},{3,1},{4,2},{5,3},{6,4},{7,5},{8,6},{9,7},{10,8},{11,9},{12,... | collective-permute-start | bytes 737288 | tf_op jit(solution)/shard_map/ppermute | solution.py:482
  20.4 11.1 %collective-permute-start.4 = (f32[12,5,8,128]{3,2,1,0:T(8,128)S(1)}, f32[12,5,8,128]{3,2,1,0:T(8,128)S(1)}, u32[]{:S(2)}, u32[]{:S(2)}) collective-permute-start(f32[12,5,8,128]{3,2,1,0:T(8,128)S(1)} %pad_maximum_fusion.own), channel_id=1, source_target_pairs={{1,0},{2,1},{3,2},{4,3},{5,4},{6,5},{7,6},{8,7},{9,8},{10,9},{11,1... | collective-permute-start | bytes 737288 | tf_op jit(solution)/shard_map/ppermute | solution.py:482
  23.9 8.0 %collective-permute-start.9 = (f32[12,5,8,128]{3,2,1,0:T(8,128)S(1)}, f32[12,5,8,128]{3,2,1,0:T(8,128)S(1)}, u32[]{:S(2)}, u32[]{:S(2)}) collective-permute-start(f32[12,5,8,128]{3,2,1,0:T(8,128)S(1)} %collective-permute-done.6.a3), channel_id=1, source_target_pairs={{0,64},{64,0},{1,65},{65,1},{2,66},{66,2},{3,67},{67,3},{4,68},{68... | collective-permute-start | bytes 737288 | tf_op jit(solution)/shard_map/ppermute | solution.py:475
  31.4 1.5 %collective-permute-start.8 = (f32[12,5,8,128]{3,2,1,0:T(8,128)S(1)}, f32[12,5,8,128]{3,2,1,0:T(8,128)S(1)}, u32[]{:S(2)}, u32[]{:S(2)}) collective-permute-start(f32[12,5,8,128]{3,2,1,0:T(8,128)S(1)} %collective-permute-done.5.a2), channel_id=1, source_target_pairs={{0,64},{64,0},{1,65},{65,1},{2,66},{66,2},{3,67},{67,3},{4,68},{68... | collective-permute-start | bytes 737288 | tf_op jit(solution)/shard_map/ppermute | solution.py:475
  31.4 1.9 %collective-permute-start.7 = (f32[12,5,8,128]{3,2,1,0:T(8,128)S(1)}, f32[12,5,8,128]{3,2,1,0:T(8,128)S(1)}, u32[]{:S(2)}, u32[]{:S(2)}) collective-permute-start(f32[12,5,8,128]{3,2,1,0:T(8,128)S(1)} %collective-permute-done.4.a1), channel_id=1, source_target_pairs={{0,64},{64,0},{1,65},{65,1},{2,66},{66,2},{3,67},{67,3},{4,68},{68... | collective-permute-start | bytes 737288 | tf_op jit(solution)/shard_map/ppermute | solution.py:475

commit v12 on v11

--- a/solution.py
+++ b/solution.py
@@ -146,7 +146,7 @@
                 out[x, group, s : s + 1, :] = flag
         return carry
 
-    unrolled(EDGE, 2, one, 0)
+    unrolled(EDGE, 6, one, 0)
 
 
 def region_kernel(
@@ -201,7 +201,7 @@
                 home[x, (step + 2) * 4 + c] = roll_lanes(v, -step)
         return carry
 
-    unrolled(NX, 3, spread, 0)
+    unrolled(NX, 6, spread, 0)
 
     def pairs(x, carry):
         for number, d in sorted(enumerate(FORWARD), key=lambda t: t[1][2]):

time: 70.2 us -> 69.6 us (level)
  no operation moved by 1% of the time
where the time goes in v12:
time: 69.6 us; the launch traced here: 69.5 us
  Pallas kernels  26 us (37%)
  starting transfers between devices  15.7 us (23%)
  waiting for transfers between devices  14.9 us (21%)
  blocking collectives  12.2 us (18%)
    pallas_call x1, Pallas kernels, per_device(): pl.pallas_call(region_kernel, out_shape=(jax.ShapeDtypeStruct((EDGE, 31)...  22.8 us
    all_to_all x1, blocking collectives, per_device(): info = lax.all_to_all(info, GZ, 0, 0, tiled=True)  12.2 us
    ppermute x3, waiting for transfers between devices, fetch(): return lax.ppermute(own, ('gx',) + GZ, pairs)  9.73 us
    ppermute x3, starting transfers between devices, fetch(): return lax.ppermute(own, ('gx',) + GZ, pairs)  9.21 us
    ppermute x3, starting transfers between devices, per_device(): lax.ppermute(packed, 'gy', [((i + k) % 4, i) for i in range(4)])  5.87 us
    ppermute x4, waiting for transfers between devices, swap(): return lax.ppermute(v, 'gx', [(0, 1), (1, 0)])  2.67 us
    ppermute x3, waiting for transfers between devices, per_device(): lax.ppermute(packed, 'gy', [((i + k) % 4, i) for i in range(4)])  2.46 us
    pallas_call x1, Pallas kernels, per_device(): pl.pallas_call(pack_kernel, out_shape=jax.ShapeDtypeStruct((EDGE, GROUPS,...  1.6 us
  transfers between devices with their start and end apart: 10, of which 7 were waited for; matrix products, arithmetic and copies ran while one was open for 0% of the time, Pallas kernels for 0%

profile of v12, /device:TPU:0, one launch (start us, length us, event | category | flops | bytes accessed | tf_op | source)
XLA Modules:
  0.0 69.5 jit_solution(16907407224533707951)
XLA Ops:
  0.6 1.6 %pack.1 = f32[6,5,2,128]{3,2,1,0:T(2,128)S(1)} custom-call(f32[6,6,3,6]{3,2,1,0:T(4,128)} %bitcast.5, f32[6,6,6]{2,1,0:T(8,128)} %polar_in.1, f32[6,6,3,6]{3,2,1,0:T(4,128)} %bitcast.6, s32[6,6,6,56]{3,2,1,0:T(8,128)} %neighbors_in.1), custom_call_target="tpu_custom_call" | custom-call | tf_op jit(solution)/shard_map/pack/pallas_call | solution.py:454
  2.2 1.7 %collective-permute-start.2 = (f32[6,5,2,128]{3,2,1,0:T(2,128)S(1)}, f32[6,5,2,128]{3,2,1,0:T(2,128)S(1)}, u32[]{:S(2)}, u32[]{:S(2)}) collective-permute-start(f32[6,5,2,128]{3,2,1,0:T(2,128)S(1)} %pack.1), channel_id=1, source_target_pairs={{48,0},{0,16},{16,32},{32,48},{49,1},{1,17},{17,33},{33,49},{50,2}... | collective-permute-start | bytes 92168 | tf_op jit(solution)/shard_map/ppermute | solution.py:470
  3.9 2.7 %collective-permute-start.1 = (f32[6,5,2,128]{3,2,1,0:T(2,128)S(1)}, f32[6,5,2,128]{3,2,1,0:T(2,128)S(1)}, u32[]{:S(2)}, u32[]{:S(2)}) collective-permute-start(f32[6,5,2,128]{3,2,1,0:T(2,128)S(1)} %pack.1), channel_id=1, source_target_pairs={{32,0},{48,16},{0,32},{16,48},{33,1},{49,17},{1,33},{17,49},{34,2}... | collective-permute-start | bytes 92168 | tf_op jit(solution)/shard_map/ppermute | solution.py:470
  6.7 1.4 %collective-permute-start = (f32[6,5,2,128]{3,2,1,0:T(2,128)S(1)}, f32[6,5,2,128]{3,2,1,0:T(2,128)S(1)}, u32[]{:S(2)}, u32[]{:S(2)}) collective-permute-start(f32[6,5,2,128]{3,2,1,0:T(2,128)S(1)} %pack.1), channel_id=1, source_target_pairs={{16,0},{32,16},{48,32},{0,48},{17,1},{33,17},{49,33},{1,49},{18,2}... | collective-permute-start | bytes 92168 | tf_op jit(solution)/shard_map/ppermute | solution.py:470
  8.1 0.0 collective-permute-done.2
  8.1 1.2 %collective-permute-done.1 = f32[6,5,2,128]{3,2,1,0:T(2,128)S(1)} collective-permute-done((f32[6,5,2,128]{3,2,1,0:T(2,128)S(1)}, f32[6,5,2,128]{3,2,1,0:T(2,128)S(1)}, u32[]{:S(2)}, u32[]{:S(2)}) %collective-permute-start.1) | collective-permute-done | bytes 30752 | tf_op jit(solution)/shard_map/ppermute | solution.py:470
  9.3 1.2 %collective-permute-done = f32[6,5,2,128]{3,2,1,0:T(2,128)S(1)} collective-permute-done((f32[6,5,2,128]{3,2,1,0:T(2,128)S(1)}, f32[6,5,2,128]{3,2,1,0:T(2,128)S(1)}, u32[]{:S(2)}, u32[]{:S(2)}) %collective-permute-start) | collective-permute-done | bytes 30752 | tf_op jit(solution)/shard_map/ppermute | solution.py:470
  10.6 0.1 pad_maximum_fusion.1
  10.6 0.1 collective-permute-start.3
  10.7 1.3 %collective-permute-done.3 = f32[6,5,8,128]{3,2,1,0:T(8,128)S(1)} collective-permute-done((f32[6,5,8,128]{3,2,1,0:T(8,128)S(1)}, f32[6,5,8,128]{3,2,1,0:T(8,128)S(1)}, u32[]{:S(2)}, u32[]{:S(2)}) %collective-permute-start.3) | collective-permute-done | bytes 122912 | tf_op jit(solution)/shard_map/ppermute | solution.py:475
  12.0 0.1 pad_maximum_fusion.own
  12.1 5.1 %collective-permute-start.6 = (f32[12,5,8,128]{3,2,1,0:T(8,128)S(1)}, f32[12,5,8,128]{3,2,1,0:T(8,128)S(1)}, u32[]{:S(2)}, u32[]{:S(2)}) collective-permute-start(f32[12,5,8,128]{3,2,1,0:T(8,128)S(1)} %pad_maximum_fusion.own), channel_id=1, source_target_pairs={{3,0},{4,1},{5,2},{6,3},{7,4},{8,5},{9,6},{10,7},{11,8},{12,9},{13... | collective-permute-start | bytes 737288 | tf_op jit(solution)/shard_map/ppermute | solution.py:482
  17.2 2.7 %collective-permute-start.5 = (f32[12,5,8,128]{3,2,1,0:T(8,128)S(1)}, f32[12,5,8,128]{3,2,1,0:T(8,128)S(1)}, u32[]{:S(2)}, u32[]{:S(2)}) collective-permute-start(f32[12,5,8,128]{3,2,1,0:T(8,128)S(1)} %pad_maximum_fusion.own), channel_id=1, source_target_pairs={{2,0},{3,1},{4,2},{5,3},{6,4},{7,5},{8,6},{9,7},{10,8},{11,9},{12,... | collective-permute-start | bytes 737288 | tf_op jit(solution)/shard_map/ppermute | solution.py:482
  20.0 1.3 %collective-permute-start.4 = (f32[12,5,8,128]{3,2,1,0:T(8,128)S(1)}, f32[12,5,8,128]{3,2,1,0:T(8,128)S(1)}, u32[]{:S(2)}, u32[]{:S(2)}) collective-permute-start(f32[12,5,8,128]{3,2,1,0:T(8,128)S(1)} %pad_maximum_fusion.own), channel_id=1, source_target_pairs={{1,0},{2,1},{3,2},{4,3},{5,4},{6,5},{7,6},{8,7},{9,8},{10,9},{11,1... | collective-permute-start | bytes 737288 | tf_op jit(solution)/shard_map/ppermute | solution.py:482
  21.3 2.2 %collective-permute-done.6.a3 = f32[12,5,8,128]{3,2,1,0:T(8,128)S(1)} collective-permute-done((f32[12,5,8,128]{3,2,1,0:T(8,128)S(1)}, f32[12,5,8,128]{3,2,1,0:T(8,128)S(1)}, u32[]{:S(2)}, u32[]{:S(2)}) %collective-permute-start.6) | collective-permute-done | bytes 245792 | tf_op jit(solution)/shard_map/ppermute | solution.py:482
  23.6 0.0 collective-permute-start.9
  23.6 7.5 %collective-permute-done.5.a2 = f32[12,5,8,128]{3,2,1,0:T(8,128)S(1)} collective-permute-done((f32[12,5,8,128]{3,2,1,0:T(8,128)S(1)}, f32[12,5,8,128]{3,2,1,0:T(8,128)S(1)}, u32[]{:S(2)}, u32[]{:S(2)}) %collective-permute-start.5) | collective-permute-done | bytes 245792 | tf_op jit(solution)/shard_map/ppermute | solution.py:482
  31.1 0.0 collective-permute-start.8
  31.1 0.0 collective-permute-done.4.a1
  31.1 0.5 collective-permute-start.7
  31.6 0.0 collective-permute-done.9.b3
  31.6 1.0 %collective-permute-done.8.b2 = f32[12,5,8,128]{3,2,1,0:T(8,128)S(1)} collective-permute-done((f32[12,5,8,128]{3,2,1,0:T(8,128)S(1)}, f32[12,5,8,128]{3,2,1,0:T(8,128)S(1)}, u32[]{:S(2)}, u32[]{:S(2)}) %collective-permute-start.8) | collective-permute-done | bytes 245792 | tf_op jit(solution)/shard_map/ppermute | solution.py:475
  32.6 0.4 collective-permute-done.7.b1
  32.9 22.8 %region.1 = (f32[6,31,8,128]{3,2,1,0:T(8,128)S(1)}, f32[16,8,128]{2,1,0:T(8,128)S(1)}) custom-call(f32[12,5,8,128]{3,2,1,0:T(8,128)S(1)} %pad_maximum_fusion.own, f32[12,5,8,128]{3,2,1,0:T(8,128)S(1)} %collective-permute-done.4.a1, f32[12,5,8,128]{3,2,1,0:T(8,128)S(1)} %collective-permute-done.5.a2, f32[12,5,8,128]{3,2,1,0:T(8,128)S(1)} %collective-permute-done.6.a3, ...), custom_call_target="tpu_custom_call" | custom-call | tf_op jit(solution)/shard_map/region/pallas_call | solution.py:488
  55.8 12.2 %all_to_all.5.info = f32[16,8,128]{2,1,0:T(8,128)S(1)} all-to-all(f32[16,8,128]{2,1,0:T(8,128)S(1)} %get-tuple-element.9), channel_id=1, replica_groups=mesh['gx'=2,'gy'=4,'gz_0'=4,'gz_1'=4] {'gz_0','gz_1'}, dimensions={0} | all-to-all | bytes 131072 | tf_op jit(solution)/shard_map/all_to_all | solution.py:509
  67.9 1.5 %finish.1 = (f32[6,6,3,6]{3,2,1,0:T(4,128)}, f32[6,6,3,6]{3,2,1,0:T(4,128)}, f32[1,8]{1,0:T(1,128)}) custom-call(f32[6,31,8,128]{3,2,1,0:T(8,128)S(1)} %get-tuple-element.8.kept, f32[16,8,128]{2,1,0:T(8,128)S(1)} %all_to_all.5.info), custom_call_target="tpu_custom_call" | custom-call | tf_op jit(solution)/shard_map/finish/pallas_call | solution.py:511
Async XLA Ops:
  2.2 5.9 %collective-permute-start.2 = (f32[6,5,2,128]{3,2,1,0:T(2,128)S(1)}, f32[6,5,2,128]{3,2,1,0:T(2,128)S(1)}, u32[]{:S(2)}, u32[]{:S(2)}) collective-permute-start(f32[6,5,2,128]{3,2,1,0:T(2,128)S(1)} %pack.1), channel_id=1, source_target_pairs={{48,0},{0,16},{16,32},{32,48},{49,1},{1,17},{17,33},{33,49},{50,2}... | collective-permute-start | bytes 92168 | tf_op jit(solution)/shard_map/ppermute | solution.py:470
  3.9 5.4 %collective-permute-start.1 = (f32[6,5,2,128]{3,2,1,0:T(2,128)S(1)}, f32[6,5,2,128]{3,2,1,0:T(2,128)S(1)}, u32[]{:S(2)}, u32[]{:S(2)}) collective-permute-start(f32[6,5,2,128]{3,2,1,0:T(2,128)S(1)} %pack.1), channel_id=1, source_target_pairs={{32,0},{48,16},{0,32},{16,48},{33,1},{49,17},{1,33},{17,49},{34,2}... | collective-permute-start | bytes 92168 | tf_op jit(solution)/shard_map/ppermute | solution.py:470
  6.7 3.9 %collective-permute-start = (f32[6,5,2,128]{3,2,1,0:T(2,128)S(1)}, f32[6,5,2,128]{3,2,1,0:T(2,128)S(1)}, u32[]{:S(2)}, u32[]{:S(2)}) collective-permute-start(f32[6,5,2,128]{3,2,1,0:T(2,128)S(1)} %pack.1), channel_id=1, source_target_pairs={{16,0},{32,16},{48,32},{0,48},{17,1},{33,17},{49,33},{1,49},{18,2}... | collective-permute-start | bytes 92168 | tf_op jit(solution)/shard_map/ppermute | solution.py:470
  10.6 1.4 %collective-permute-start.3 = (f32[6,5,8,128]{3,2,1,0:T(8,128)S(1)}, f32[6,5,8,128]{3,2,1,0:T(8,128)S(1)}, u32[]{:S(2)}, u32[]{:S(2)}) collective-permute-start(f32[6,5,8,128]{3,2,1,0:T(8,128)S(1)} %pad_maximum_fusion.1), channel_id=1, source_target_pairs={{0,64},{64,0},{1,65},{65,1},{2,66},{66,2},{3,67},{67,3},{4,68},{68... | collective-permute-start | bytes 368648 | tf_op jit(solution)/shard_map/ppermute | solution.py:475
  12.1 11.4 %collective-permute-start.6 = (f32[12,5,8,128]{3,2,1,0:T(8,128)S(1)}, f32[12,5,8,128]{3,2,1,0:T(8,128)S(1)}, u32[]{:S(2)}, u32[]{:S(2)}) collective-permute-start(f32[12,5,8,128]{3,2,1,0:T(8,128)S(1)} %pad_maximum_fusion.own), channel_id=1, source_target_pairs={{3,0},{4,1},{5,2},{6,3},{7,4},{8,5},{9,6},{10,7},{11,8},{12,9},{13... | collective-permute-start | bytes 737288 | tf_op jit(solution)/shard_map/ppermute | solution.py:482
  17.2 13.8 %collective-permute-start.5 = (f32[12,5,8,128]{3,2,1,0:T(8,128)S(1)}, f32[12,5,8,128]{3,2,1,0:T(8,128)S(1)}, u32[]{:S(2)}, u32[]{:S(2)}) collective-permute-start(f32[12,5,8,128]{3,2,1,0:T(8,128)S(1)} %pad_maximum_fusion.own), channel_id=1, source_target_pairs={{2,0},{3,1},{4,2},{5,3},{6,4},{7,5},{8,6},{9,7},{10,8},{11,9},{12,... | collective-permute-start | bytes 737288 | tf_op jit(solution)/shard_map/ppermute | solution.py:482
  20.0 11.1 %collective-permute-start.4 = (f32[12,5,8,128]{3,2,1,0:T(8,128)S(1)}, f32[12,5,8,128]{3,2,1,0:T(8,128)S(1)}, u32[]{:S(2)}, u32[]{:S(2)}) collective-permute-start(f32[12,5,8,128]{3,2,1,0:T(8,128)S(1)} %pad_maximum_fusion.own), channel_id=1, source_target_pairs={{1,0},{2,1},{3,2},{4,3},{5,4},{6,5},{7,6},{8,7},{9,8},{10,9},{11,1... | collective-permute-start | bytes 737288 | tf_op jit(solution)/shard_map/ppermute | solution.py:482
  23.6 8.0 %collective-permute-start.9 = (f32[12,5,8,128]{3,2,1,0:T(8,128)S(1)}, f32[12,5,8,128]{3,2,1,0:T(8,128)S(1)}, u32[]{:S(2)}, u32[]{:S(2)}) collective-permute-start(f32[12,5,8,128]{3,2,1,0:T(8,128)S(1)} %collective-permute-done.6.a3), channel_id=1, source_target_pairs={{0,64},{64,0},{1,65},{65,1},{2,66},{66,2},{3,67},{67,3},{4,68},{68... | collective-permute-start | bytes 737288 | tf_op jit(solution)/shard_map/ppermute | solution.py:475
  31.1 1.5 %collective-permute-start.8 = (f32[12,5,8,128]{3,2,1,0:T(8,128)S(1)}, f32[12,5,8,128]{3,2,1,0:T(8,128)S(1)}, u32[]{:S(2)}, u32[]{:S(2)}) collective-permute-start(f32[12,5,8,128]{3,2,1,0:T(8,128)S(1)} %collective-permute-done.5.a2), channel_id=1, source_target_pairs={{0,64},{64,0},{1,65},{65,1},{2,66},{66,2},{3,67},{67,3},{4,68},{68... | collective-permute-start | bytes 737288 | tf_op jit(solution)/shard_map/ppermute | solution.py:475
  31.1 1.9 %collective-permute-start.7 = (f32[12,5,8,128]{3,2,1,0:T(8,128)S(1)}, f32[12,5,8,128]{3,2,1,0:T(8,128)S(1)}, u32[]{:S(2)}, u32[]{:S(2)}) collective-permute-start(f32[12,5,8,128]{3,2,1,0:T(8,128)S(1)} %collective-permute-done.4.a1), channel_id=1, source_target_pairs={{0,64},{64,0},{1,65},{65,1},{2,66},{66,2},{3,67},{67,3},{4,68},{68... | collective-permute-start | bytes 737288 | tf_op jit(solution)/shard_map/ppermute | solution.py:475

commit v13 on v12

--- a/solution.py
+++ b/solution.py
@@ -191,7 +191,7 @@
                 chan[x, group * PER + member] = acc
         return carry
 
-    unrolled(NX, 2, gather, 0)
+    unrolled(NX, 3, gather, 0)
 
     def spread(x, carry):
         for c in range(4):
@@ -270,7 +270,7 @@
             past[x * 3 + c] = zero
         return carry
 
-    unrolled(NX, 4, prepare, 0)
+    unrolled(NX, 12, prepare, 0)
 
     def next_vector(x, c, al, be, sc):
         return (raw[x * 3 + c] - al * now[x * 3 + c] - be * past[x * 3 + c]) * sc
@@ -330,7 +330,7 @@
             basis[BASIS, x * 3 + c] = next_vector(x, c, al, be, sc)
         return carry
 
-    unrolled(NX, 4, end, 0)
+    unrolled(NX, 12, end, 0)
 
     number = 0
     for low, high in ((0, 3), (3, BASIS)):

time: 69.6 us -> 69.4 us (level)
  no operation moved by 1% of the time
where the time goes in v13:
time: 69.4 us; the launch traced here: 69.3 us
  Pallas kernels  25.8 us (37%)
  starting transfers between devices  15.7 us (23%)
  waiting for transfers between devices  14.9 us (21%)
  blocking collectives  12.2 us (18%)
    pallas_call x1, Pallas kernels, per_device(): pl.pallas_call(region_kernel, out_shape=(jax.ShapeDtypeStruct((EDGE, 31)...  22.6 us
    all_to_all x1, blocking collectives, per_device(): info = lax.all_to_all(info, GZ, 0, 0, tiled=True)  12.2 us
    ppermute x3, waiting for transfers between devices, fetch(): return lax.ppermute(own, ('gx',) + GZ, pairs)  9.73 us
    ppermute x3, starting transfers between devices, fetch(): return lax.ppermute(own, ('gx',) + GZ, pairs)  9.21 us
    ppermute x3, starting transfers between devices, per_device(): lax.ppermute(packed, 'gy', [((i + k) % 4, i) for i in range(4)])  5.87 us
    ppermute x4, waiting for transfers between devices, swap(): return lax.ppermute(v, 'gx', [(0, 1), (1, 0)])  2.67 us
    ppermute x3, waiting for transfers between devices, per_device(): lax.ppermute(packed, 'gy', [((i + k) % 4, i) for i in range(4)])  2.46 us
    pallas_call x1, Pallas kernels, per_device(): pl.pallas_call(pack_kernel, out_shape=jax.ShapeDtypeStruct((EDGE, GROUPS,...  1.6 us
  transfers between devices with their start and end apart: 10, of which 7 were waited for; matrix products, arithmetic and copies ran while one was open for 0% of the time, Pallas kernels for 0%

profile of v13, /device:TPU:0, one launch (start us, length us, event | category | flops | bytes accessed | tf_op | source)
XLA Modules:
  0.0 69.3 jit_solution(14974118443883601257)
XLA Ops:
  0.6 1.6 %pack.1 = f32[6,5,2,128]{3,2,1,0:T(2,128)S(1)} custom-call(f32[6,6,3,6]{3,2,1,0:T(4,128)} %bitcast.5, f32[6,6,6]{2,1,0:T(8,128)} %polar_in.1, f32[6,6,3,6]{3,2,1,0:T(4,128)} %bitcast.6, s32[6,6,6,56]{3,2,1,0:T(8,128)} %neighbors_in.1), custom_call_target="tpu_custom_call" | custom-call | tf_op jit(solution)/shard_map/pack/pallas_call | solution.py:454
  2.2 1.7 %collective-permute-start.2 = (f32[6,5,2,128]{3,2,1,0:T(2,128)S(1)}, f32[6,5,2,128]{3,2,1,0:T(2,128)S(1)}, u32[]{:S(2)}, u32[]{:S(2)}) collective-permute-start(f32[6,5,2,128]{3,2,1,0:T(2,128)S(1)} %pack.1), channel_id=1, source_target_pairs={{48,0},{0,16},{16,32},{32,48},{49,1},{1,17},{17,33},{33,49},{50,2}... | collective-permute-start | bytes 92168 | tf_op jit(solution)/shard_map/ppermute | solution.py:470
  3.9 2.7 %collective-permute-start.1 = (f32[6,5,2,128]{3,2,1,0:T(2,128)S(1)}, f32[6,5,2,128]{3,2,1,0:T(2,128)S(1)}, u32[]{:S(2)}, u32[]{:S(2)}) collective-permute-start(f32[6,5,2,128]{3,2,1,0:T(2,128)S(1)} %pack.1), channel_id=1, source_target_pairs={{32,0},{48,16},{0,32},{16,48},{33,1},{49,17},{1,33},{17,49},{34,2}... | collective-permute-start | bytes 92168 | tf_op jit(solution)/shard_map/ppermute | solution.py:470
  6.7 1.4 %collective-permute-start = (f32[6,5,2,128]{3,2,1,0:T(2,128)S(1)}, f32[6,5,2,128]{3,2,1,0:T(2,128)S(1)}, u32[]{:S(2)}, u32[]{:S(2)}) collective-permute-start(f32[6,5,2,128]{3,2,1,0:T(2,128)S(1)} %pack.1), channel_id=1, source_target_pairs={{16,0},{32,16},{48,32},{0,48},{17,1},{33,17},{49,33},{1,49},{18,2}... | collective-permute-start | bytes 92168 | tf_op jit(solution)/shard_map/ppermute | solution.py:470
  8.1 0.0 collective-permute-done.2
  8.1 1.2 %collective-permute-done.1 = f32[6,5,2,128]{3,2,1,0:T(2,128)S(1)} collective-permute-done((f32[6,5,2,128]{3,2,1,0:T(2,128)S(1)}, f32[6,5,2,128]{3,2,1,0:T(2,128)S(1)}, u32[]{:S(2)}, u32[]{:S(2)}) %collective-permute-start.1) | collective-permute-done | bytes 30752 | tf_op jit(solution)/shard_map/ppermute | solution.py:470
  9.3 1.2 %collective-permute-done = f32[6,5,2,128]{3,2,1,0:T(2,128)S(1)} collective-permute-done((f32[6,5,2,128]{3,2,1,0:T(2,128)S(1)}, f32[6,5,2,128]{3,2,1,0:T(2,128)S(1)}, u32[]{:S(2)}, u32[]{:S(2)}) %collective-permute-start) | collective-permute-done | bytes 30752 | tf_op jit(solution)/shard_map/ppermute | solution.py:470
  10.6 0.1 pad_maximum_fusion.1
  10.6 0.1 collective-permute-start.3
  10.7 1.3 %collective-permute-done.3 = f32[6,5,8,128]{3,2,1,0:T(8,128)S(1)} collective-permute-done((f32[6,5,8,128]{3,2,1,0:T(8,128)S(1)}, f32[6,5,8,128]{3,2,1,0:T(8,128)S(1)}, u32[]{:S(2)}, u32[]{:S(2)}) %collective-permute-start.3) | collective-permute-done | bytes 122912 | tf_op jit(solution)/shard_map/ppermute | solution.py:475
  12.0 0.1 pad_maximum_fusion.own
  12.1 5.1 %collective-permute-start.6 = (f32[12,5,8,128]{3,2,1,0:T(8,128)S(1)}, f32[12,5,8,128]{3,2,1,0:T(8,128)S(1)}, u32[]{:S(2)}, u32[]{:S(2)}) collective-permute-start(f32[12,5,8,128]{3,2,1,0:T(8,128)S(1)} %pad_maximum_fusion.own), channel_id=1, source_target_pairs={{3,0},{4,1},{5,2},{6,3},{7,4},{8,5},{9,6},{10,7},{11,8},{12,9},{13... | collective-permute-start | bytes 737288 | tf_op jit(solution)/shard_map/ppermute | solution.py:482
  17.2 2.7 %collective-permute-start.5 = (f32[12,5,8,128]{3,2,1,0:T(8,128)S(1)}, f32[12,5,8,128]{3,2,1,0:T(8,128)S(1)}, u32[]{:S(2)}, u32[]{:S(2)}) collective-permute-start(f32[12,5,8,128]{3,2,1,0:T(8,128)S(1)} %pad_maximum_fusion.own), channel_id=1, source_target_pairs={{2,0},{3,1},{4,2},{5,3},{6,4},{7,5},{8,6},{9,7},{10,8},{11,9},{12,... | collective-permute-start | bytes 737288 | tf_op jit(solution)/shard_map/ppermute | solution.py:482
  20.0 1.3 %collective-permute-start.4 = (f32[12,5,8,128]{3,2,1,0:T(8,128)S(1)}, f32[12,5,8,128]{3,2,1,0:T(8,128)S(1)}, u32[]{:S(2)}, u32[]{:S(2)}) collective-permute-start(f32[12,5,8,128]{3,2,1,0:T(8,128)S(1)} %pad_maximum_fusion.own), channel_id=1, source_target_pairs={{1,0},{2,1},{3,2},{4,3},{5,4},{6,5},{7,6},{8,7},{9,8},{10,9},{11,1... | collective-permute-start | bytes 737288 | tf_op jit(solution)/shard_map/ppermute | solution.py:482
  21.3 2.2 %collective-permute-done.6.a3 = f32[12,5,8,128]{3,2,1,0:T(8,128)S(1)} collective-permute-done((f32[12,5,8,128]{3,2,1,0:T(8,128)S(1)}, f32[12,5,8,128]{3,2,1,0:T(8,128)S(1)}, u32[]{:S(2)}, u32[]{:S(2)}) %collective-permute-start.6) | collective-permute-done | bytes 245792 | tf_op jit(solution)/shard_map/ppermute | solution.py:482
  23.6 0.0 collective-permute-start.9
  23.6 7.5 %collective-permute-done.5.a2 = f32[12,5,8,128]{3,2,1,0:T(8,128)S(1)} collective-permute-done((f32[12,5,8,128]{3,2,1,0:T(8,128)S(1)}, f32[12,5,8,128]{3,2,1,0:T(8,128)S(1)}, u32[]{:S(2)}, u32[]{:S(2)}) %collective-permute-start.5) | collective-permute-done | bytes 245792 | tf_op jit(solution)/shard_map/ppermute | solution.py:482
  31.1 0.0 collective-permute-start.8
  31.1 0.0 collective-permute-done.4.a1
  31.1 0.5 collective-permute-start.7
  31.6 0.0 collective-permute-done.9.b3
  31.6 1.0 %collective-permute-done.8.b2 = f32[12,5,8,128]{3,2,1,0:T(8,128)S(1)} collective-permute-done((f32[12,5,8,128]{3,2,1,0:T(8,128)S(1)}, f32[12,5,8,128]{3,2,1,0:T(8,128)S(1)}, u32[]{:S(2)}, u32[]{:S(2)}) %collective-permute-start.8) | collective-permute-done | bytes 245792 | tf_op jit(solution)/shard_map/ppermute | solution.py:475
  32.6 0.4 collective-permute-done.7.b1
  32.9 22.6 %region.1 = (f32[6,31,8,128]{3,2,1,0:T(8,128)S(1)}, f32[16,8,128]{2,1,0:T(8,128)S(1)}) custom-call(f32[12,5,8,128]{3,2,1,0:T(8,128)S(1)} %pad_maximum_fusion.own, f32[12,5,8,128]{3,2,1,0:T(8,128)S(1)} %collective-permute-done.4.a1, f32[12,5,8,128]{3,2,1,0:T(8,128)S(1)} %collective-permute-done.5.a2, f32[12,5,8,128]{3,2,1,0:T(8,128)S(1)} %collective-permute-done.6.a3, ...), custom_call_target="tpu_custom_call" | custom-call | tf_op jit(solution)/shard_map/region/pallas_call | solution.py:488
  55.6 12.2 %all_to_all.5.info = f32[16,8,128]{2,1,0:T(8,128)S(1)} all-to-all(f32[16,8,128]{2,1,0:T(8,128)S(1)} %get-tuple-element.9), channel_id=1, replica_groups=mesh['gx'=2,'gy'=4,'gz_0'=4,'gz_1'=4] {'gz_0','gz_1'}, dimensions={0} | all-to-all | bytes 131072 | tf_op jit(solution)/shard_map/all_to_all | solution.py:509
  67.7 1.5 %finish.1 = (f32[6,6,3,6]{3,2,1,0:T(4,128)}, f32[6,6,3,6]{3,2,1,0:T(4,128)}, f32[1,8]{1,0:T(1,128)}) custom-call(f32[6,31,8,128]{3,2,1,0:T(8,128)S(1)} %get-tuple-element.8.kept, f32[16,8,128]{2,1,0:T(8,128)S(1)} %all_to_all.5.info), custom_call_target="tpu_custom_call" | custom-call | tf_op jit(solution)/shard_map/finish/pallas_call | solution.py:511
Async XLA Ops:
  2.2 5.9 %collective-permute-start.2 = (f32[6,5,2,128]{3,2,1,0:T(2,128)S(1)}, f32[6,5,2,128]{3,2,1,0:T(2,128)S(1)}, u32[]{:S(2)}, u32[]{:S(2)}) collective-permute-start(f32[6,5,2,128]{3,2,1,0:T(2,128)S(1)} %pack.1), channel_id=1, source_target_pairs={{48,0},{0,16},{16,32},{32,48},{49,1},{1,17},{17,33},{33,49},{50,2}... | collective-permute-start | bytes 92168 | tf_op jit(solution)/shard_map/ppermute | solution.py:470
  3.9 5.4 %collective-permute-start.1 = (f32[6,5,2,128]{3,2,1,0:T(2,128)S(1)}, f32[6,5,2,128]{3,2,1,0:T(2,128)S(1)}, u32[]{:S(2)}, u32[]{:S(2)}) collective-permute-start(f32[6,5,2,128]{3,2,1,0:T(2,128)S(1)} %pack.1), channel_id=1, source_target_pairs={{32,0},{48,16},{0,32},{16,48},{33,1},{49,17},{1,33},{17,49},{34,2}... | collective-permute-start | bytes 92168 | tf_op jit(solution)/shard_map/ppermute | solution.py:470
  6.7 3.9 %collective-permute-start = (f32[6,5,2,128]{3,2,1,0:T(2,128)S(1)}, f32[6,5,2,128]{3,2,1,0:T(2,128)S(1)}, u32[]{:S(2)}, u32[]{:S(2)}) collective-permute-start(f32[6,5,2,128]{3,2,1,0:T(2,128)S(1)} %pack.1), channel_id=1, source_target_pairs={{16,0},{32,16},{48,32},{0,48},{17,1},{33,17},{49,33},{1,49},{18,2}... | collective-permute-start | bytes 92168 | tf_op jit(solution)/shard_map/ppermute | solution.py:470
  10.6 1.4 %collective-permute-start.3 = (f32[6,5,8,128]{3,2,1,0:T(8,128)S(1)}, f32[6,5,8,128]{3,2,1,0:T(8,128)S(1)}, u32[]{:S(2)}, u32[]{:S(2)}) collective-permute-start(f32[6,5,8,128]{3,2,1,0:T(8,128)S(1)} %pad_maximum_fusion.1), channel_id=1, source_target_pairs={{0,64},{64,0},{1,65},{65,1},{2,66},{66,2},{3,67},{67,3},{4,68},{68... | collective-permute-start | bytes 368648 | tf_op jit(solution)/shard_map/ppermute | solution.py:475
  12.1 11.4 %collective-permute-start.6 = (f32[12,5,8,128]{3,2,1,0:T(8,128)S(1)}, f32[12,5,8,128]{3,2,1,0:T(8,128)S(1)}, u32[]{:S(2)}, u32[]{:S(2)}) collective-permute-start(f32[12,5,8,128]{3,2,1,0:T(8,128)S(1)} %pad_maximum_fusion.own), channel_id=1, source_target_pairs={{3,0},{4,1},{5,2},{6,3},{7,4},{8,5},{9,6},{10,7},{11,8},{12,9},{13... | collective-permute-start | bytes 737288 | tf_op jit(solution)/shard_map/ppermute | solution.py:482
  17.2 13.8 %collective-permute-start.5 = (f32[12,5,8,128]{3,2,1,0:T(8,128)S(1)}, f32[12,5,8,128]{3,2,1,0:T(8,128)S(1)}, u32[]{:S(2)}, u32[]{:S(2)}) collective-permute-start(f32[12,5,8,128]{3,2,1,0:T(8,128)S(1)} %pad_maximum_fusion.own), channel_id=1, source_target_pairs={{2,0},{3,1},{4,2},{5,3},{6,4},{7,5},{8,6},{9,7},{10,8},{11,9},{12,... | collective-permute-start | bytes 737288 | tf_op jit(solution)/shard_map/ppermute | solution.py:482
  20.0 11.1 %collective-permute-start.4 = (f32[12,5,8,128]{3,2,1,0:T(8,128)S(1)}, f32[12,5,8,128]{3,2,1,0:T(8,128)S(1)}, u32[]{:S(2)}, u32[]{:S(2)}) collective-permute-start(f32[12,5,8,128]{3,2,1,0:T(8,128)S(1)} %pad_maximum_fusion.own), channel_id=1, source_target_pairs={{1,0},{2,1},{3,2},{4,3},{5,4},{6,5},{7,6},{8,7},{9,8},{10,9},{11,1... | collective-permute-start | bytes 737288 | tf_op jit(solution)/shard_map/ppermute | solution.py:482
  23.6 8.0 %collective-permute-start.9 = (f32[12,5,8,128]{3,2,1,0:T(8,128)S(1)}, f32[12,5,8,128]{3,2,1,0:T(8,128)S(1)}, u32[]{:S(2)}, u32[]{:S(2)}) collective-permute-start(f32[12,5,8,128]{3,2,1,0:T(8,128)S(1)} %collective-permute-done.6.a3), channel_id=1, source_target_pairs={{0,64},{64,0},{1,65},{65,1},{2,66},{66,2},{3,67},{67,3},{4,68},{68... | collective-permute-start | bytes 737288 | tf_op jit(solution)/shard_map/ppermute | solution.py:475
  31.1 1.5 %collective-permute-start.8 = (f32[12,5,8,128]{3,2,1,0:T(8,128)S(1)}, f32[12,5,8,128]{3,2,1,0:T(8,128)S(1)}, u32[]{:S(2)}, u32[]{:S(2)}) collective-permute-start(f32[12,5,8,128]{3,2,1,0:T(8,128)S(1)} %collective-permute-done.5.a2), channel_id=1, source_target_pairs={{0,64},{64,0},{1,65},{65,1},{2,66},{66,2},{3,67},{67,3},{4,68},{68... | collective-permute-start | bytes 737288 | tf_op jit(solution)/shard_map/ppermute | solution.py:475
  31.1 1.9 %collective-permute-start.7 = (f32[12,5,8,128]{3,2,1,0:T(8,128)S(1)}, f32[12,5,8,128]{3,2,1,0:T(8,128)S(1)}, u32[]{:S(2)}, u32[]{:S(2)}) collective-permute-start(f32[12,5,8,128]{3,2,1,0:T(8,128)S(1)} %collective-permute-done.4.a1), channel_id=1, source_target_pairs={{0,64},{64,0},{1,65},{65,1},{2,66},{66,2},{3,67},{67,3},{4,68},{68... | collective-permute-start | bytes 737288 | tf_op jit(solution)/shard_map/ppermute | solution.py:475

commit v14 on v13

--- a/solution.py
+++ b/solution.py
@@ -347,7 +347,7 @@
                             sums[n] = sums[n] + weighted * u[q]
             return tuple(sums)
 
-        sums = unrolled(NX, 2, one, (zero,) * len(entries))
+        sums = unrolled(NX, 3, one, (zero,) * len(entries))
         for n in range(len(entries)):
             info = jnp.where(lane == number, total(jnp.where(slab, sums[n], 0.0)), info)
             number += 1
@@ -368,7 +368,7 @@
         kept_out[x, 30] = front(chan[far, 35])
         return carry
 
-    unrolled(EDGE, 2, keep, 0)
+    unrolled(EDGE, 6, keep, 0)
 
 
 def finish_kernel(kept, info, dip_out, res_out, len_out):

time: 69.4 us -> 69.3 us (level)
  no operation moved by 1% of the time
where the time goes in v14:
time: 69.3 us; the launch traced here: 69.2 us
  Pallas kernels  25.7 us (37%)
  starting transfers between devices  15.7 us (23%)
  waiting for transfers between devices  14.9 us (22%)
  blocking collectives  12.2 us (18%)
    pallas_call x1, Pallas kernels, per_device(): pl.pallas_call(region_kernel, out_shape=(jax.ShapeDtypeStruct((EDGE, 31)...  22.5 us
    all_to_all x1, blocking collectives, per_device(): info = lax.all_to_all(info, GZ, 0, 0, tiled=True)  12.2 us
    ppermute x3, waiting for transfers between devices, fetch(): return lax.ppermute(own, ('gx',) + GZ, pairs)  9.73 us
    ppermute x3, starting transfers between devices, fetch(): return lax.ppermute(own, ('gx',) + GZ, pairs)  9.21 us
    ppermute x3, starting transfers between devices, per_device(): lax.ppermute(packed, 'gy', [((i + k) % 4, i) for i in range(4)])  5.87 us
    ppermute x4, waiting for transfers between devices, swap(): return lax.ppermute(v, 'gx', [(0, 1), (1, 0)])  2.67 us
    ppermute x3, waiting for transfers between devices, per_device(): lax.ppermute(packed, 'gy', [((i + k) % 4, i) for i in range(4)])  2.46 us
    pallas_call x1, Pallas kernels, per_device(): pl.pallas_call(pack_kernel, out_shape=jax.ShapeDtypeStruct((EDGE, GROUPS,...  1.6 us
  transfers between devices with their start and end apart: 10, of which 7 were waited for; matrix products, arithmetic and copies ran while one was open for 0% of the time, Pallas kernels for 0%

profile of v14, /device:TPU:0, one launch (start us, length us, event | category | flops | bytes accessed | tf_op | source)
XLA Modules:
  0.0 69.2 jit_solution(12255724887086240315)
XLA Ops:
  0.6 1.6 %pack.1 = f32[6,5,2,128]{3,2,1,0:T(2,128)S(1)} custom-call(f32[6,6,3,6]{3,2,1,0:T(4,128)} %bitcast.5, f32[6,6,6]{2,1,0:T(8,128)} %polar_in.1, f32[6,6,3,6]{3,2,1,0:T(4,128)} %bitcast.6, s32[6,6,6,56]{3,2,1,0:T(8,128)} %neighbors_in.1), custom_call_target="tpu_custom_call" | custom-call | tf_op jit(solution)/shard_map/pack/pallas_call | solution.py:454
  2.2 1.7 %collective-permute-start.2 = (f32[6,5,2,128]{3,2,1,0:T(2,128)S(1)}, f32[6,5,2,128]{3,2,1,0:T(2,128)S(1)}, u32[]{:S(2)}, u32[]{:S(2)}) collective-permute-start(f32[6,5,2,128]{3,2,1,0:T(2,128)S(1)} %pack.1), channel_id=1, source_target_pairs={{48,0},{0,16},{16,32},{32,48},{49,1},{1,17},{17,33},{33,49},{50,2}... | collective-permute-start | bytes 92168 | tf_op jit(solution)/shard_map/ppermute | solution.py:470
  3.9 2.7 %collective-permute-start.1 = (f32[6,5,2,128]{3,2,1,0:T(2,128)S(1)}, f32[6,5,2,128]{3,2,1,0:T(2,128)S(1)}, u32[]{:S(2)}, u32[]{:S(2)}) collective-permute-start(f32[6,5,2,128]{3,2,1,0:T(2,128)S(1)} %pack.1), channel_id=1, source_target_pairs={{32,0},{48,16},{0,32},{16,48},{33,1},{49,17},{1,33},{17,49},{34,2}... | collective-permute-start | bytes 92168 | tf_op jit(solution)/shard_map/ppermute | solution.py:470
  6.7 1.4 %collective-permute-start = (f32[6,5,2,128]{3,2,1,0:T(2,128)S(1)}, f32[6,5,2,128]{3,2,1,0:T(2,128)S(1)}, u32[]{:S(2)}, u32[]{:S(2)}) collective-permute-start(f32[6,5,2,128]{3,2,1,0:T(2,128)S(1)} %pack.1), channel_id=1, source_target_pairs={{16,0},{32,16},{48,32},{0,48},{17,1},{33,17},{49,33},{1,49},{18,2}... | collective-permute-start | bytes 92168 | tf_op jit(solution)/shard_map/ppermute | solution.py:470
  8.1 0.0 collective-permute-done.2
  8.1 1.2 %collective-permute-done.1 = f32[6,5,2,128]{3,2,1,0:T(2,128)S(1)} collective-permute-done((f32[6,5,2,128]{3,2,1,0:T(2,128)S(1)}, f32[6,5,2,128]{3,2,1,0:T(2,128)S(1)}, u32[]{:S(2)}, u32[]{:S(2)}) %collective-permute-start.1) | collective-permute-done | bytes 30752 | tf_op jit(solution)/shard_map/ppermute | solution.py:470
  9.3 1.2 %collective-permute-done = f32[6,5,2,128]{3,2,1,0:T(2,128)S(1)} collective-permute-done((f32[6,5,2,128]{3,2,1,0:T(2,128)S(1)}, f32[6,5,2,128]{3,2,1,0:T(2,128)S(1)}, u32[]{:S(2)}, u32[]{:S(2)}) %collective-permute-start) | collective-permute-done | bytes 30752 | tf_op jit(solution)/shard_map/ppermute | solution.py:470
  10.6 0.1 pad_maximum_fusion.1
  10.6 0.1 collective-permute-start.3
  10.7 1.3 %collective-permute-done.3 = f32[6,5,8,128]{3,2,1,0:T(8,128)S(1)} collective-permute-done((f32[6,5,8,128]{3,2,1,0:T(8,128)S(1)}, f32[6,5,8,128]{3,2,1,0:T(8,128)S(1)}, u32[]{:S(2)}, u32[]{:S(2)}) %collective-permute-start.3) | collective-permute-done | bytes 122912 | tf_op jit(solution)/shard_map/ppermute | solution.py:475
  12.0 0.1 pad_maximum_fusion.own
  12.1 5.1 %collective-permute-start.6 = (f32[12,5,8,128]{3,2,1,0:T(8,128)S(1)}, f32[12,5,8,128]{3,2,1,0:T(8,128)S(1)}, u32[]{:S(2)}, u32[]{:S(2)}) collective-permute-start(f32[12,5,8,128]{3,2,1,0:T(8,128)S(1)} %pad_maximum_fusion.own), channel_id=1, source_target_pairs={{3,0},{4,1},{5,2},{6,3},{7,4},{8,5},{9,6},{10,7},{11,8},{12,9},{13... | collective-permute-start | bytes 737288 | tf_op jit(solution)/shard_map/ppermute | solution.py:482
  17.2 2.7 %collective-permute-start.5 = (f32[12,5,8,128]{3,2,1,0:T(8,128)S(1)}, f32[12,5,8,128]{3,2,1,0:T(8,128)S(1)}, u32[]{:S(2)}, u32[]{:S(2)}) collective-permute-start(f32[12,5,8,128]{3,2,1,0:T(8,128)S(1)} %pad_maximum_fusion.own), channel_id=1, source_target_pairs={{2,0},{3,1},{4,2},{5,3},{6,4},{7,5},{8,6},{9,7},{10,8},{11,9},{12,... | collective-permute-start | bytes 737288 | tf_op jit(solution)/shard_map/ppermute | solution.py:482
  20.0 1.3 %collective-permute-start.4 = (f32[12,5,8,128]{3,2,1,0:T(8,128)S(1)}, f32[12,5,8,128]{3,2,1,0:T(8,128)S(1)}, u32[]{:S(2)}, u32[]{:S(2)}) collective-permute-start(f32[12,5,8,128]{3,2,1,0:T(8,128)S(1)} %pad_maximum_fusion.own), channel_id=1, source_target_pairs={{1,0},{2,1},{3,2},{4,3},{5,4},{6,5},{7,6},{8,7},{9,8},{10,9},{11,1... | collective-permute-start | bytes 737288 | tf_op jit(solution)/shard_map/ppermute | solution.py:482
  21.3 2.2 %collective-permute-done.6.a3 = f32[12,5,8,128]{3,2,1,0:T(8,128)S(1)} collective-permute-done((f32[12,5,8,128]{3,2,1,0:T(8,128)S(1)}, f32[12,5,8,128]{3,2,1,0:T(8,128)S(1)}, u32[]{:S(2)}, u32[]{:S(2)}) %collective-permute-start.6) | collective-permute-done | bytes 245792 | tf_op jit(solution)/shard_map/ppermute | solution.py:482
  23.6 0.0 collective-permute-start.9
  23.6 7.5 %collective-permute-done.5.a2 = f32[12,5,8,128]{3,2,1,0:T(8,128)S(1)} collective-permute-done((f32[12,5,8,128]{3,2,1,0:T(8,128)S(1)}, f32[12,5,8,128]{3,2,1,0:T(8,128)S(1)}, u32[]{:S(2)}, u32[]{:S(2)}) %collective-permute-start.5) | collective-permute-done | bytes 245792 | tf_op jit(solution)/shard_map/ppermute | solution.py:482
  31.1 0.0 collective-permute-start.8
  31.1 0.0 collective-permute-done.4.a1
  31.1 0.5 collective-permute-start.7
  31.6 0.0 collective-permute-done.9.b3
  31.6 1.0 %collective-permute-done.8.b2 = f32[12,5,8,128]{3,2,1,0:T(8,128)S(1)} collective-permute-done((f32[12,5,8,128]{3,2,1,0:T(8,128)S(1)}, f32[12,5,8,128]{3,2,1,0:T(8,128)S(1)}, u32[]{:S(2)}, u32[]{:S(2)}) %collective-permute-start.8) | collective-permute-done | bytes 245792 | tf_op jit(solution)/shard_map/ppermute | solution.py:475
  32.6 0.4 collective-permute-done.7.b1
  32.9 22.5 %region.1 = (f32[6,31,8,128]{3,2,1,0:T(8,128)S(1)}, f32[16,8,128]{2,1,0:T(8,128)S(1)}) custom-call(f32[12,5,8,128]{3,2,1,0:T(8,128)S(1)} %pad_maximum_fusion.own, f32[12,5,8,128]{3,2,1,0:T(8,128)S(1)} %collective-permute-done.4.a1, f32[12,5,8,128]{3,2,1,0:T(8,128)S(1)} %collective-permute-done.5.a2, f32[12,5,8,128]{3,2,1,0:T(8,128)S(1)} %collective-permute-done.6.a3, ...), custom_call_target="tpu_custom_call" | custom-call | tf_op jit(solution)/shard_map/region/pallas_call | solution.py:488
  55.5 12.2 %all_to_all.5.info = f32[16,8,128]{2,1,0:T(8,128)S(1)} all-to-all(f32[16,8,128]{2,1,0:T(8,128)S(1)} %get-tuple-element.9), channel_id=1, replica_groups=mesh['gx'=2,'gy'=4,'gz_0'=4,'gz_1'=4] {'gz_0','gz_1'}, dimensions={0} | all-to-all | bytes 131072 | tf_op jit(solution)/shard_map/all_to_all | solution.py:509
  67.6 1.5 %finish.1 = (f32[6,6,3,6]{3,2,1,0:T(4,128)}, f32[6,6,3,6]{3,2,1,0:T(4,128)}, f32[1,8]{1,0:T(1,128)}) custom-call(f32[6,31,8,128]{3,2,1,0:T(8,128)S(1)} %get-tuple-element.8.kept, f32[16,8,128]{2,1,0:T(8,128)S(1)} %all_to_all.5.info), custom_call_target="tpu_custom_call" | custom-call | tf_op jit(solution)/shard_map/finish/pallas_call | solution.py:511
Async XLA Ops:
  2.2 5.9 %collective-permute-start.2 = (f32[6,5,2,128]{3,2,1,0:T(2,128)S(1)}, f32[6,5,2,128]{3,2,1,0:T(2,128)S(1)}, u32[]{:S(2)}, u32[]{:S(2)}) collective-permute-start(f32[6,5,2,128]{3,2,1,0:T(2,128)S(1)} %pack.1), channel_id=1, source_target_pairs={{48,0},{0,16},{16,32},{32,48},{49,1},{1,17},{17,33},{33,49},{50,2}... | collective-permute-start | bytes 92168 | tf_op jit(solution)/shard_map/ppermute | solution.py:470
  3.9 5.4 %collective-permute-start.1 = (f32[6,5,2,128]{3,2,1,0:T(2,128)S(1)}, f32[6,5,2,128]{3,2,1,0:T(2,128)S(1)}, u32[]{:S(2)}, u32[]{:S(2)}) collective-permute-start(f32[6,5,2,128]{3,2,1,0:T(2,128)S(1)} %pack.1), channel_id=1, source_target_pairs={{32,0},{48,16},{0,32},{16,48},{33,1},{49,17},{1,33},{17,49},{34,2}... | collective-permute-start | bytes 92168 | tf_op jit(solution)/shard_map/ppermute | solution.py:470
  6.7 3.9 %collective-permute-start = (f32[6,5,2,128]{3,2,1,0:T(2,128)S(1)}, f32[6,5,2,128]{3,2,1,0:T(2,128)S(1)}, u32[]{:S(2)}, u32[]{:S(2)}) collective-permute-start(f32[6,5,2,128]{3,2,1,0:T(2,128)S(1)} %pack.1), channel_id=1, source_target_pairs={{16,0},{32,16},{48,32},{0,48},{17,1},{33,17},{49,33},{1,49},{18,2}... | collective-permute-start | bytes 92168 | tf_op jit(solution)/shard_map/ppermute | solution.py:470
  10.6 1.4 %collective-permute-start.3 = (f32[6,5,8,128]{3,2,1,0:T(8,128)S(1)}, f32[6,5,8,128]{3,2,1,0:T(8,128)S(1)}, u32[]{:S(2)}, u32[]{:S(2)}) collective-permute-start(f32[6,5,8,128]{3,2,1,0:T(8,128)S(1)} %pad_maximum_fusion.1), channel_id=1, source_target_pairs={{0,64},{64,0},{1,65},{65,1},{2,66},{66,2},{3,67},{67,3},{4,68},{68... | collective-permute-start | bytes 368648 | tf_op jit(solution)/shard_map/ppermute | solution.py:475
  12.1 11.4 %collective-permute-start.6 = (f32[12,5,8,128]{3,2,1,0:T(8,128)S(1)}, f32[12,5,8,128]{3,2,1,0:T(8,128)S(1)}, u32[]{:S(2)}, u32[]{:S(2)}) collective-permute-start(f32[12,5,8,128]{3,2,1,0:T(8,128)S(1)} %pad_maximum_fusion.own), channel_id=1, source_target_pairs={{3,0},{4,1},{5,2},{6,3},{7,4},{8,5},{9,6},{10,7},{11,8},{12,9},{13... | collective-permute-start | bytes 737288 | tf_op jit(solution)/shard_map/ppermute | solution.py:482
  17.2 13.8 %collective-permute-start.5 = (f32[12,5,8,128]{3,2,1,0:T(8,128)S(1)}, f32[12,5,8,128]{3,2,1,0:T(8,128)S(1)}, u32[]{:S(2)}, u32[]{:S(2)}) collective-permute-start(f32[12,5,8,128]{3,2,1,0:T(8,128)S(1)} %pad_maximum_fusion.own), channel_id=1, source_target_pairs={{2,0},{3,1},{4,2},{5,3},{6,4},{7,5},{8,6},{9,7},{10,8},{11,9},{12,... | collective-permute-start | bytes 737288 | tf_op jit(solution)/shard_map/ppermute | solution.py:482
  20.0 11.1 %collective-permute-start.4 = (f32[12,5,8,128]{3,2,1,0:T(8,128)S(1)}, f32[12,5,8,128]{3,2,1,0:T(8,128)S(1)}, u32[]{:S(2)}, u32[]{:S(2)}) collective-permute-start(f32[12,5,8,128]{3,2,1,0:T(8,128)S(1)} %pad_maximum_fusion.own), channel_id=1, source_target_pairs={{1,0},{2,1},{3,2},{4,3},{5,4},{6,5},{7,6},{8,7},{9,8},{10,9},{11,1... | collective-permute-start | bytes 737288 | tf_op jit(solution)/shard_map/ppermute | solution.py:482
  23.6 8.0 %collective-permute-start.9 = (f32[12,5,8,128]{3,2,1,0:T(8,128)S(1)}, f32[12,5,8,128]{3,2,1,0:T(8,128)S(1)}, u32[]{:S(2)}, u32[]{:S(2)}) collective-permute-start(f32[12,5,8,128]{3,2,1,0:T(8,128)S(1)} %collective-permute-done.6.a3), channel_id=1, source_target_pairs={{0,64},{64,0},{1,65},{65,1},{2,66},{66,2},{3,67},{67,3},{4,68},{68... | collective-permute-start | bytes 737288 | tf_op jit(solution)/shard_map/ppermute | solution.py:475
  31.1 1.5 %collective-permute-start.8 = (f32[12,5,8,128]{3,2,1,0:T(8,128)S(1)}, f32[12,5,8,128]{3,2,1,0:T(8,128)S(1)}, u32[]{:S(2)}, u32[]{:S(2)}) collective-permute-start(f32[12,5,8,128]{3,2,1,0:T(8,128)S(1)} %collective-permute-done.5.a2), channel_id=1, source_target_pairs={{0,64},{64,0},{1,65},{65,1},{2,66},{66,2},{3,67},{67,3},{4,68},{68... | collective-permute-start | bytes 737288 | tf_op jit(solution)/shard_map/ppermute | solution.py:475
  31.1 1.9 %collective-permute-start.7 = (f32[12,5,8,128]{3,2,1,0:T(8,128)S(1)}, f32[12,5,8,128]{3,2,1,0:T(8,128)S(1)}, u32[]{:S(2)}, u32[]{:S(2)}) collective-permute-start(f32[12,5,8,128]{3,2,1,0:T(8,128)S(1)} %collective-permute-done.4.a1), channel_id=1, source_target_pairs={{0,64},{64,0},{1,65},{65,1},{2,66},{66,2},{3,67},{67,3},{4,68},{68... | collective-permute-start | bytes 737288 | tf_op jit(solution)/shard_map/ppermute | solution.py:475
